TPU v7x, 32 devices: a whole 2x2x4 slice. The times are simulated.
32 devices in a mesh: grp: 2 (over y), dp: 16 (over z, x, core).
Axes of the slice: x: 2, y: 2, z: 4, core: 2. Of those that a mesh axis runs over, the one named last changes fastest.
Arguments:
- params: float32 [1900544], P(('grp', 'dp')), parts along dimension 0, may hold values from -0.3 to 0.3
- momentum: float32 [1900544], P(('grp', 'dp')), parts along dimension 0, may hold values from -6 to 6
- noise_draws: float32 [2, 950272], P('grp', 'dp'), parts along dimension 0, may hold values from -6 to 6
- images: float32 [16384, 448], P(('grp', 'dp')), parts along dimension 0, may hold values from -6 to 6
- labels: int32 [16384], P(('grp', 'dp')), parts along dimension 0, may hold values from 0 to 9
- indices: int32 [2, 4096], P('grp', 'dp'), parts along dimension 0, may hold values from 0 to 511
Outputs:
- params_out: float32 [1900544], P(('grp', 'dp')), parts along dimension 0
- momentum_out: float32 [1900544], P(('grp', 'dp')), parts along dimension 0
- losses: float32 [2], P('grp'), parts along dimension 0
There are 2 independent parts, one for each index of `grp`. A program takes and returns all parts, laid end to end along the dimension named above; each array names one. Nothing has to cross between parts.
All inputs are finite; a program needn't handle non-finite values.
Results may differ from a plain program's by a relative error of at most 0.0003.
Values sent between devices are 32-bit elements; how exact they have to be, the bound alone decides.
No kernel may reach another device: no remote copies, remote signals or barrier semaphores. Data moves between devices by JAX's collectives and lax.ppermute only.
A program may use at most 64 MiB of HBM per device.

v0:
```python
import functools
import math

import jax
import jax.numpy as jnp
from jax import lax
from jax.experimental import pallas as pl
from jax.experimental.pallas import tpu as pltpu
from jax.sharding import PartitionSpec as P


H = 2048
OUT = 10
LANES = 128
LIMIT = 16
COPIES = 2

step_size = 0.02
friction = 15.0
F32, BF16 = jnp.float32, jnp.bfloat16


def up8(n):
    return -(-n // 8) * 8


class Plan:
    def __init__(self, devices, din, shard_len, batch):
        self.n = devices
        self.group = devices // COPIES
        self.din = din
        self.cols = H // self.group
        self.nb = self.cols // LANES
        self.rows = shard_len // H
        self.pad = up8(self.rows + 1)
        self.step = H // LANES
        self.flat = shard_len // LANES
        self.batch = batch
        self.half = batch // 2
        self.tail = din + 1 - (devices - 1) * self.rows
        gcd = math.gcd(LANES, OUT)
        self.hp, self.qp = LANES // gcd, OUT // gcd
        self.periods = self.cols // self.hp
        self.classes = up8(OUT)
        self.xrows = -(-(din + 2) // 16) * 16

    @staticmethod
    def fits(devices, din, shard_len, batch):
        if devices & (devices - 1) or devices < 2 * COPIES or shard_len % (8 * LANES) or shard_len % H:
            return False
        group, rows = devices // COPIES, shard_len // H
        if H % (group * LANES) or batch % (2 * LANES) or group not in (4, 8) or din % 8:
            return False
        tail = din + 1 - (devices - 1) * rows
        return 0 < tail and tail + OUT + 1 <= rows


def split(x):
    hi = x.astype(BF16)
    return hi, (x - hi.astype(F32)).astype(BF16)


def split3(x):
    hi = x.astype(BF16)
    rest = x - hi.astype(F32)
    mid = rest.astype(BF16)
    return hi, mid, (rest - mid.astype(F32)).astype(BF16)


def dot(a, b, dims):
    return lax.dot_general(a, b, (dims, ((), ())), preferred_element_type=F32)


NN, NT = ((1,), (0,)), ((1,), (1,))


def iota(shape, axis):
    return lax.broadcasted_iota(jnp.int32, shape, axis)


def pick_kernel(plan, img_ref, lab_ref, idx_ref, *refs):
    parts, (img, lab, idx, sems) = refs[:-4], refs[-4:]
    loads = [pltpu.make_async_copy(s, d, sems.at[i]) for i, (s, d) in enumerate(
        ((idx_ref, idx), (lab_ref, lab), (img_ref, img)))]
    for load in loads:
        load.start()
    for load in loads:
        load.wait()
    pool = img.shape[1]
    hot = (iota((pool, plan.batch), 0) == idx[...]).astype(BF16)
    hi, mid, lo = split3(img[...])
    rows = dot(hi, hot, NN) + dot(mid, hot, NN) + dot(lo, hot, NN)
    spare = plan.xrows - plan.din
    marks = jnp.broadcast_to(lab[...].astype(F32), (spare, pool)).astype(BF16)
    marks = dot(marks, hot, NN)
    at = iota((spare, plan.batch), 0)
    marks = jnp.where(at == 0, 1.0, jnp.where(at == 1, marks, 0.0))
    for i, part in enumerate(parts):
        part[: plan.din, :] = rows[:, i * plan.half : (i + 1) * plan.half]
        part[plan.din :, :] = marks[:, i * plan.half : (i + 1) * plan.half]


def cut_kernel(plan, last_ref, par_ref, out_ref):
    cut_weights(plan, last_ref, par_ref, out_ref)


def cut_weights(plan, last_ref, par_ref, out_ref):
    out_ref[...] = jnp.zeros_like(out_ref)
    for j in range(plan.group):
        for b in range(plan.nb):
            piece = par_ref[pl.ds(j * plan.nb + b, plan.rows, stride=plan.step), :]
            for d in range(j, plan.n, plan.group):
                out_ref[d, : plan.rows, b * LANES : (b + 1) * LANES] = piece

    @pl.when(last_ref[0] == 1)
    def _():
        t = plan.tail
        for j in range(plan.group):
            for d in range(j, plan.n, plan.group):
                out_ref[d, t + OUT, :LANES] = par_ref[(t + OUT) * plan.step, :]
            for b in range(plan.nb):
                start = t * plan.step + j * plan.nb * OUT + b
                piece = par_ref[pl.ds(start, OUT, stride=plan.nb), :]
                for d in range(j, plan.n, plan.group):
                    out_ref[d, t : t + OUT, b * LANES : (b + 1) * LANES] = piece


def class_masks(plan):
    width = plan.qp * LANES
    mask = (iota((plan.classes, width), 1) % OUT == iota((plan.classes, width), 0)).astype(F32)
    place = (iota((width, plan.hp), 0) // OUT == iota((width, plan.hp), 1)).astype(BF16)
    return mask, place


def flat_spot(plan, r):
    row = (plan.n - 1) * plan.pad + plan.tail + r // plan.nb
    col = r % plan.nb * LANES
    return row, col


def blocks_of(plan):
    return [(d, d * plan.rows, min(plan.rows, plan.din + 1 - d * plan.rows)) for d in range(plan.n)]


def forward_kernel(plan, w_ref, *refs):
    x_refs = refs[: 2 * plan.group]
    x_ref, h_ref, a_ref, own_ref, send_ref, lab_ref, c_ref = refs[2 * plan.group :]
    mask, place = class_masks(plan)
    lhs = []
    for p in range(plan.periods):
        parts = []
        for q in range(plan.qp):
            row, col = flat_spot(plan, p * plan.qp + q)
            parts.append(jnp.broadcast_to(w_ref[row : row + 1, col : col + LANES], (plan.classes, LANES)))
        lhs.append(jnp.concatenate(parts, axis=1) * mask)
    hi, mid, lo = split3(jnp.concatenate(lhs, axis=0))
    out_w = dot(hi, place, NN) + dot(mid, place, NN) + dot(lo, place, NN)
    for p in range(plan.periods):
        rows = slice(p * plan.classes, (p + 1) * plan.classes)
        a_ref[:, p * plan.hp : (p + 1) * plan.hp] = out_w[rows]
    a_hi, a_lo = split(a_ref[...])
    a_cat = jnp.concatenate([a_hi, a_lo], axis=0)
    c_ref[...] = jnp.zeros_like(c_ref)
    for d, first, count in blocks_of(plan):
        c_ref[first : first + count, :] = w_ref[d * plan.pad : d * plan.pad + count, :]
    w_hi, w_lo = split(c_ref[...].T)
    w_cat = jnp.concatenate([w_hi, w_lo], axis=0)
    per = plan.batch // LANES
    for m in range(plan.group):
        here = slice(m * plan.batch, (m + 1) * plan.batch)
        got = jnp.concatenate([x_refs[2 * m][...], x_refs[2 * m + 1][...]], axis=1)
        for i in range(per):
            line = got[plan.din + 1 : plan.din + 2, i * LANES : (i + 1) * LANES]
            lab_ref[m * per + i : m * per + i + 1, :] = line
        x_hi, x_lo = split(got)
        x_ref[: plan.xrows, here] = x_hi
        x_ref[plan.xrows :, here] = x_lo
        pre = dot(w_cat, x_hi, NN)
        hidden = jnp.tanh(pre[: plan.cols] + (pre[plan.cols :] + dot(w_hi, x_lo, NN)))
        h_hi, h_lo = split(hidden)
        h_ref[: plan.cols, here] = h_hi
        h_ref[plan.cols :, here] = h_lo
        lg = dot(a_cat, h_hi, NN)
        lg = lg[: plan.classes] + (lg[plan.classes :] + dot(a_hi, h_lo, NN))
        for i in range(per):
            for o in range(OUT):
                row = lg[o : o + 1, i * LANES : (i + 1) * LANES]
                own_ref[o, m * per + i : m * per + i + 1, :] = row
                send_ref[o, (m ^ 1) * per + i : (m ^ 1) * per + i + 1, :] = row


def backward_kernel(plan, own_ref, w_ref, a_ref, x_ref, h_ref, lab_ref, *refs):
    lg_refs, (out_ref, lg_ref, dl_ref, dh_ref, dw_ref) = refs[:-5], refs[-5:]
    per = plan.batch // LANES
    lines = plan.group * per
    diag = iota((plan.classes, LANES), 0) == iota((plan.classes, LANES), 1)
    row = (plan.n - 1) * plan.pad + plan.tail + OUT
    bias = w_ref[row : row + 1, :LANES]
    for m in range(plan.group):
        value = own_ref[:, m * per : (m + 1) * per, :]
        for i, ref in enumerate(lg_refs):
            other = m ^ (2 * (i + 1))
            value = value + ref[:, other * per : (other + 1) * per, :]
        lg_ref[:, m * per : (m + 1) * per, :] = value
    labels = lab_ref[...].astype(jnp.int32)
    logits = [lg_ref[o] + bias[:, o : o + 1] for o in range(OUT)]
    top = functools.reduce(jnp.maximum, logits)
    ex = [jnp.exp(v - top) for v in logits]
    norm = functools.reduce(jnp.add, ex)
    hits = [labels == o for o in range(OUT)]
    picked = functools.reduce(jnp.add, [jnp.where(h, v, 0.0) for h, v in zip(hits, logits)])
    nll = jnp.sum(jnp.sum(jnp.log(norm) + top - picked, axis=1, keepdims=True), axis=0, keepdims=True)
    share = 1.0 / norm
    dl_ref[...] = jnp.zeros_like(dl_ref)
    for o in range(OUT):
        value = ex[o] * share - jnp.where(hits[o], 1.0, 0.0)
        for i in range(lines):
            dl_ref[o : o + 1, i * LANES : (i + 1) * LANES] = value[i : i + 1, :]
    dl = dl_ref[...]
    dbias = jnp.sum(dl, axis=1, keepdims=True)
    dbias = jnp.sum(jnp.where(diag, dbias, 0.0), axis=0, keepdims=True)
    dl_hi, dl_lo = split(dl)
    at_hi, at_lo = split(a_ref[...].T)
    at_cat = jnp.concatenate([at_hi, at_lo], axis=0)
    for m in range(plan.group):
        here = slice(m * plan.batch, (m + 1) * plan.batch)
        hidden = h_ref[: plan.cols, here].astype(F32) + h_ref[plan.cols :, here].astype(F32)
        dh = dot(at_cat, dl_hi[:, here], NN)
        dh = dh[: plan.cols] + (dh[plan.cols :] + dot(at_hi, dl_lo[:, here], NN))
        dh_hi, dh_lo = split(dh * (1.0 - hidden * hidden))
        dh_ref[: plan.cols, here] = dh_hi
        dh_ref[plan.cols :, here] = dh_lo
    da = dot(h_ref[...], dl_hi, NT)
    da = da[: plan.cols] + (da[plan.cols :] + dot(h_ref[: plan.cols, :], dl_lo, NT))
    dw = dot(x_ref[...], dh_ref[: plan.cols, :], NT)
    dw_ref[...] = dw[: plan.xrows] + (dw[plan.xrows :] + dot(x_ref[: plan.xrows, :], dh_ref[plan.cols :, :], NT))
    out_ref[...] = jnp.zeros_like(out_ref)
    for d, first, count in blocks_of(plan):
        out_ref[d * plan.pad : d * plan.pad + count, :] = dw_ref[first : first + count, :]
    mask, place = class_masks(plan)
    hi, mid, lo = split3(da.T)
    parts = []
    for v in (hi, mid, lo):
        parts.append(jnp.concatenate([v[:, p * plan.hp : (p + 1) * plan.hp] for p in range(plan.periods)], axis=0))
    back = dot(parts[0], place, NT) + dot(parts[1], place, NT) + dot(parts[2], place, NT)
    for p in range(plan.periods):
        line = jnp.sum(back[p * plan.classes : (p + 1) * plan.classes] * mask, axis=0, keepdims=True)
        for q in range(plan.qp):
            r, c = flat_spot(plan, p * plan.qp + q)
            out_ref[r : r + 1, c : c + LANES] = line[:, q * LANES : (q + 1) * LANES]
    out_ref[row : row + 1, :LANES] = dbias
    for d in range(plan.n):
        at = d * plan.pad + plan.rows
        out_ref[at : at + 1, :LANES] = jnp.broadcast_to(nll, (1, LANES))


def prepare_kernel(plan, at_ref, par_ref, mom_ref, noise_ref, base_ref, keep_ref, mom, noise, sems):
    loads = [pltpu.make_async_copy(s, d, sems.at[i]) for i, (s, d) in enumerate(
        ((par_ref, keep_ref), (mom_ref, mom), (noise_ref, noise)))]
    for load in loads:
        load.start()
    for load in loads:
        load.wait()
    shape = (plan.flat, LANES)
    index = at_ref[0] + iota(shape, 0) * LANES + iota(shape, 1)
    prior = precision_of(index, plan.din) * keep_ref[...]
    base = (1.0 - step_size * friction) * mom[...] - step_size * prior
    base_ref[...] = base + math.sqrt(2.0 * friction * step_size) * noise[...]


def update_kernel(plan, scale, count, at_ref, got_ref, base_ref, par_ref, par_out, mom_out, loss_ref, grad_ref):
    t = plan.tail
    pieces = []
    for j in range(plan.group):
        piece = got_ref[j * plan.pad : (j + 1) * plan.pad, :]
        for g in range(1, COPIES):
            at = (g * plan.group + j) * plan.pad
            piece = piece + got_ref[at : at + plan.pad, :]
        pieces.append(piece)
        for b in range(plan.nb):
            lanes = slice(b * LANES, (b + 1) * LANES)
            grad_ref[pl.ds(j * plan.nb + b, plan.rows, stride=plan.step), :] = piece[: plan.rows, lanes]
    loss_ref[...] = pieces[0][plan.rows : plan.rows + 1, :LANES] * (1.0 / count)

    @pl.when(at_ref[1] == 1)
    def _():
        row = (t + OUT) * plan.step
        grad_ref[row:, :] = jnp.zeros((plan.flat - row, LANES), F32)
        grad_ref[row : row + 1, :] = pieces[0][t + OUT : t + OUT + 1, :LANES]
        for j in range(plan.group):
            for b in range(plan.nb):
                lanes = slice(b * LANES, (b + 1) * LANES)
                start = t * plan.step + j * plan.nb * OUT + b
                grad_ref[pl.ds(start, OUT, stride=plan.nb), :] = pieces[j][t : t + OUT, lanes]

    mom = base_ref[...] - (step_size * scale) * grad_ref[...]
    mom_out[...] = mom
    par_out[...] = par_ref[...] + step_size * mom


def precision_of(index, din):
    in_end = din * H
    hid_end = in_end + H
    out_end = hid_end + H * OUT
    inner = jnp.where(index < hid_end, 1.0, jnp.where(index < out_end, float(H), 1.0))
    return jnp.where(index < in_end, float(din), inner)


def call(kernel, args, outs, scratch=(), smem=0, limit=16, whole=0, cost=1):
    vm = pl.BlockSpec(memory_space=pltpu.VMEM)
    sm = pl.BlockSpec(memory_space=pltpu.SMEM)
    anywhere = pl.BlockSpec(memory_space=pltpu.HBM)
    specs = [sm] * smem + [anywhere] * whole
    return pl.pallas_call(
        kernel,
        out_shape=[jax.ShapeDtypeStruct(s, t) for s, t in outs],
        in_specs=specs + [vm] * (len(args) - len(specs)),
        out_specs=[vm] * len(outs),
        scratch_shapes=list(scratch),
        compiler_params=pltpu.CompilerParams(vmem_limit_bytes=limit << 20),
        cost_estimate=pl.CostEstimate(flops=cost * 10**9, bytes_accessed=1 << 20, transcendentals=0),
    )(*args)


def fast_body(n, params, momentum, noise_draws, images, labels, indices):
    pool, din = images.shape
    plan = Plan(n, din, params.shape[0], indices.shape[1])
    me = lax.axis_index("dp")
    last = (me == n - 1).astype(jnp.int32)
    flat = (plan.flat, LANES)
    tall = (n * plan.pad, plan.cols)
    total = plan.group * plan.batch
    dense = (OUT, total // LANES, LANES)

    def hop(x, k):
        return lax.ppermute(x, "dp", [(d, d ^ k) for d in range(n)])


    rows = call(
        functools.partial(pick_kernel, plan),
        (images.T, labels.reshape(1, pool), indices),
        [((plan.xrows, plan.half), F32)] * 2,
        [
            pltpu.VMEM((din, pool), F32),
            pltpu.VMEM((1, pool), jnp.int32),
            pltpu.VMEM((1, plan.batch), jnp.int32),
            pltpu.SemaphoreType.DMA((3,)),
        ],
        whole=3,
        limit=LIMIT,
    )
    *rows, mine = lax.optimization_barrier((*rows, params))
    (cut,) = call(
        functools.partial(cut_kernel, plan),
        (last.reshape(1), mine.reshape(flat)),
        [((n, plan.pad, plan.cols), F32)],
        smem=1,
    )
    near = [hop(r, 1) for r in rows]
    xs = {0: rows}
    b2, a4 = hop(rows[1], 2), None
    if plan.group == 8:
        a4 = hop(rows[0], 4)
    a2 = hop(rows[0], 2)
    xs[2] = [a2, b2]
    if plan.group == 8:
        b4 = hop(rows[1], 4)
        xs[4] = [a4, b4]
        xs[6] = [hop(a4, 2), hop(b2, 4)]
    weights = lax.all_to_all(cut.reshape(tall), "dp", 0, 0, tiled=True)
    far = [m for m in xs if m]
    weights, *got = lax.optimization_barrier((weights, *(h for m in far for h in xs[m])))
    slots = [*rows, *near]
    for i in range(0, len(got), 2):
        slots += got[i : i + 2] + [hop(h, 1) for h in got[i : i + 2]]
    x, hidden, outw, own, send, marks = call(
        functools.partial(forward_kernel, plan),
        (weights, *slots),
        [
            ((2 * plan.xrows, total), BF16),
            ((2 * plan.cols, total), BF16),
            ((plan.classes, plan.cols), F32),
            (dense, F32),
            (dense, F32),
            (dense[1:], F32),
        ],
        [pltpu.VMEM((plan.xrows, plan.cols), F32)],
        cost=4,
    )
    own = own + hop(send, 1)
    more = [hop(own, k) for k in range(2, plan.group, 2)]
    (grads,) = call(
        functools.partial(backward_kernel, plan),
        (own, weights, outw, x, hidden, marks, *more),
        [(tall, F32)],
        [
            pltpu.VMEM(dense, F32),
            pltpu.VMEM((plan.classes, total), F32),
            pltpu.VMEM((2 * plan.cols, total), BF16),
            pltpu.VMEM((plan.xrows, plan.cols), F32),
        ],
        cost=4,
    )
    got = lax.all_to_all(grads, "dp", 0, 0, tiled=True)
    scale = pool / plan.batch
    count = n * plan.batch
    spot = jnp.stack([me * params.shape[0], last])
    base, old = call(
        functools.partial(prepare_kernel, plan),
        (spot, params.reshape(flat), momentum.reshape(flat), noise_draws.reshape(flat)),
        [(flat, F32), (flat, F32)],
        [pltpu.VMEM(flat, F32), pltpu.VMEM(flat, F32), pltpu.SemaphoreType.DMA((3,))],
        smem=1,
        whole=3,
    )
    new_params, new_momentum, loss = call(
        functools.partial(update_kernel, plan, scale, count),
        (spot, got, base, old),
        [(flat, F32), (flat, F32), ((1, LANES), F32)],
        [pltpu.VMEM(flat, F32)],
        smem=1,
    )
    return new_params.reshape(-1), new_momentum.reshape(-1), loss[0, :1]


def total_nll(flat_vec, din, chosen_rows, targets):
    in_end = din * H
    hid_end = in_end + H
    w_in = flat_vec[:in_end].reshape(din, H)
    b_in = flat_vec[in_end:hid_end]
    w_out = flat_vec[hid_end : hid_end + H * OUT].reshape(H, OUT)
    b_out = flat_vec[hid_end + H * OUT : hid_end + H * OUT + OUT]
    high = dict(precision=lax.Precision.HIGHEST, preferred_element_type=F32)
    hidden = jnp.tanh(jnp.dot(chosen_rows, w_in, **high) + b_in)
    logits = jnp.dot(hidden, w_out, **high) + b_out
    log_norm = jnp.log(jnp.sum(jnp.exp(logits), axis=1))
    classes = iota(logits.shape, 1)
    picked = jnp.sum(jnp.where(targets[:, None] == classes, logits, 0.0), axis=1)
    return jnp.sum(log_norm - picked)


def plain_body(params, momentum, noise_draws, images, labels, indices):
    shard_len = params.shape[0]
    din = images.shape[1]
    shard_start = lax.axis_index("dp") * shard_len
    precision = precision_of(shard_start + lax.iota(jnp.int32, shard_len), din)
    gathered = lax.all_gather(params, "dp", axis=0, tiled=True)
    chosen_rows = jnp.take(images, indices[0], axis=0)
    targets = jnp.take(labels, indices[0], axis=0)
    nll, pullback = jax.vjp(lambda w: total_nll(w, din, chosen_rows, targets), gathered)
    (local_grad,) = pullback(jnp.ones_like(nll))
    loss = lax.psum(nll, "dp") / (lax.axis_size("dp") * indices.shape[1])
    own_grad = lax.psum_scatter(local_grad, "dp", scatter_dimension=0, tiled=True)
    force = images.shape[0] / indices.shape[1] * own_grad + precision * params
    momentum = (1.0 - step_size * friction) * momentum - step_size * force
    momentum = momentum + math.sqrt(2.0 * friction * step_size) * noise_draws[0]
    return params + step_size * momentum, momentum, loss.reshape(1)


def solution(mesh):
    n = mesh.shape["dp"]

    def body(*args):
        params, images, indices = args[0], args[3], args[5]
        if Plan.fits(n, images.shape[1], params.shape[0], indices.shape[1]):
            return fast_body(n, *args)
        return plain_body(*args)

    placed = (
        P(("grp", "dp")),
        P(("grp", "dp")),
        P("grp", "dp"),
        P(("grp", "dp"), None),
        P(("grp", "dp")),
        P("grp", "dp"),
    )
    return jax.shard_map(
        body,
        mesh=mesh,
        in_specs=placed,
        out_specs=(P(("grp", "dp")), P(("grp", "dp")), P("grp")),
        check_vma=False,
    )
```

profile of v0, /device:TPU:0, one launch (start us, length us, event | category | flops | bytes accessed | tf_op | source)
XLA Modules:
  0.0 82.3 jit_solution(15166885243524674855)
XLA Ops:
  0.6 1.2 %copy-done = f32[512,448]{0,1:T(8,128)S(1)} copy-done((f32[512,448]{0,1:T(8,128)S(1)}, f32[512,448]{0,1:T(8,128)}, u32[]{:S(2)}) %copy-start) | copy-done | bytes 917528
  3.2 0.8 shard_map.85
  4.0 0.9 %copy-done.1 = f32[59392]{0:T(1024)S(1)} copy-done((f32[59392]{0:T(1024)S(1)}, f32[59392]{0:T(1024)}, u32[]{:S(2)}) %copy-start.1) | copy-done | bytes 237592
  5.0 0.9 %shard_map.86 = f32[16,32,256]{2,1,0:T(8,128)} custom-call(s32[1]{0:T(128)} %bitcast.1.last_ref, f32[464,128]{1,0:T(8,128)S(1)} %bitcast.19), custom_call_target="tpu_custom_call" | custom-call | flops 1000000000 | bytes 1048576 | tf_op jit(solution)/shard_map/pallas_call | solution.py:314
  5.9 7.4 %all-to-all-start = ((f32[16,32,256]{2,1,0:T(8,128)}), f32[16,32,256]{2,1,0:T(8,128)S(1)}, u32[]{:S(2)}, u32[]{:S(2)}) async-start(f32[16,32,256]{2,1,0:T(8,128)} %shard_map.86), calls=%async_computation | async-start | bytes 1048576 | tf_op jit(solution)/shard_map/all_to_all | solution.py:370
  13.2 1.9 %collective-permute-start.2 = (f32[464,128]{1,0:T(8,128)S(1)}, f32[464,128]{1,0:T(8,128)S(1)}, u32[]{:S(2)}, u32[]{:S(2)}) collective-permute-start(f32[464,128]{1,0:T(8,128)S(1)} %get-tuple-element.29.refs_0_), channel_id=1, source_target_pairs={{0,4},{1,5},{2,6},{3,7},{4,0},{5,1},{6,2},{7,3},{8,12},{9,13},{10,... | collective-permute-start | bytes 712712 | tf_op jit(solution)/shard_map/ppermute | solution.py:336
  15.2 1.5 %collective-permute-start.1 = (f32[464,128]{1,0:T(8,128)S(1)}, f32[464,128]{1,0:T(8,128)S(1)}, u32[]{:S(2)}, u32[]{:S(2)}) collective-permute-start(f32[464,128]{1,0:T(8,128)S(1)} %get-tuple-element.30.refs_1_), channel_id=1, source_target_pairs={{0,2},{1,3},{2,0},{3,1},{4,6},{5,7},{6,4},{7,5},{8,10},{9,11},{10,... | collective-permute-start | bytes 712712 | tf_op jit(solution)/shard_map/ppermute | solution.py:336
  17.4 13.1 %collective-permute-done.2.refs_8_ = f32[464,128]{1,0:T(8,128)S(1)} collective-permute-done((f32[464,128]{1,0:T(8,128)S(1)}, f32[464,128]{1,0:T(8,128)S(1)}, u32[]{:S(2)}, u32[]{:S(2)}) %collective-permute-start.2) | collective-permute-done | bytes 237600 | tf_op jit(solution)/shard_map/ppermute | solution.py:336
  30.4 1.5 %collective-permute-start.4 = (f32[464,128]{1,0:T(8,128)S(1)}, f32[464,128]{1,0:T(8,128)S(1)}, u32[]{:S(2)}, u32[]{:S(2)}) collective-permute-start(f32[464,128]{1,0:T(8,128)S(1)} %collective-permute-done.2.refs_8_), channel_id=1, source_target_pairs={{0,2},{1,3},{2,0},{3,1},{4,6},{5,7},{6,4},{7,5},{8,10},{9,11},{10,... | collective-permute-start | bytes 712712 | tf_op jit(solution)/shard_map/ppermute | solution.py:336
  33.0 2.5 %collective-permute-done.3.refs_9_ = f32[464,128]{1,0:T(8,128)S(1)} collective-permute-done((f32[464,128]{1,0:T(8,128)S(1)}, f32[464,128]{1,0:T(8,128)S(1)}, u32[]{:S(2)}, u32[]{:S(2)}) %collective-permute-start.3) | collective-permute-done | bytes 237600 | tf_op jit(solution)/shard_map/ppermute | solution.py:336
  35.5 1.7 %collective-permute-done.4.refs_12_ = f32[464,128]{1,0:T(8,128)S(1)} collective-permute-done((f32[464,128]{1,0:T(8,128)S(1)}, f32[464,128]{1,0:T(8,128)S(1)}, u32[]{:S(2)}, u32[]{:S(2)}) %collective-permute-start.4) | collective-permute-done | bytes 237600 | tf_op jit(solution)/shard_map/ppermute | solution.py:336
  37.2 2.8 %collective-permute-done.5.refs_13_ = f32[464,128]{1,0:T(8,128)S(1)} collective-permute-done((f32[464,128]{1,0:T(8,128)S(1)}, f32[464,128]{1,0:T(8,128)S(1)}, u32[]{:S(2)}, u32[]{:S(2)}) %collective-permute-start.5) | collective-permute-done | bytes 237600 | tf_op jit(solution)/shard_map/ppermute | solution.py:336
  43.2 5.1 %shard_map.87 = (bf16[928,2048]{1,0:T(8,128)(2,1)S(1)}, bf16[512,2048]{1,0:T(8,128)(2,1)S(1)}, f32[16,256]{1,0:T(8,128)S(1)}, f32[10,16,128]{2,1,0:T(8,128)S(1)}...) custom-call(f32[512,256]{1,0:T(8,128)S(1)} %bitcast.15, f32[464,128]{1,0:T(8,128)S(1)} %get-tuple-element.29.refs_0_, ...), custom_call_target="tpu_custom_call" | custom-call | flops 4000000000 | bytes 1048576 | tf_op jit(solution)/shard_map/pallas_call | solution.py:314
  48.6 1.1 %collective-permute-done.14 = f32[10,16,128]{2,1,0:T(8,128)S(1)} collective-permute-done((f32[10,16,128]{2,1,0:T(8,128)S(1)}, f32[10,16,128]{2,1,0:T(8,128)S(1)}, u32[]{:S(2)}, u32[]{:S(2)}) %collective-permute-start.14) | collective-permute-done | bytes 81952 | tf_op jit(solution)/shard_map/ppermute | solution.py:336
  49.7 1.5 %collective-permute-start.15 = (f32[10,16,128]{2,1,0:T(8,128)S(1)}, f32[10,16,128]{2,1,0:T(8,128)S(1)}, u32[]{:S(2)}, u32[]{:S(2)}) collective-permute-start(f32[10,16,128]{2,1,0:T(8,128)S(1)} %add.3.own_ref), channel_id=1, source_target_pairs={{0,2},{1,3},{2,0},{3,1},{4,6},{5,7},{6,4},{7,5},{8,10},{9,11},{10,... | collective-permute-start | bytes 245768 | tf_op jit(solution)/shard_map/ppermute | solution.py:336
  51.8 1.5 %collective-permute-start.17 = (f32[10,16,128]{2,1,0:T(8,128)S(1)}, f32[10,16,128]{2,1,0:T(8,128)S(1)}, u32[]{:S(2)}, u32[]{:S(2)}) collective-permute-start(f32[10,16,128]{2,1,0:T(8,128)S(1)} %add.3.own_ref), channel_id=1, source_target_pairs={{0,6},{1,7},{2,4},{3,5},{4,2},{5,3},{6,0},{7,1},{8,14},{9,15},{10,... | collective-permute-start | bytes 245768 | tf_op jit(solution)/shard_map/ppermute | solution.py:336
  53.3 1.0 %collective-permute-done.15.refs_0_ = f32[10,16,128]{2,1,0:T(8,128)S(1)} collective-permute-done((f32[10,16,128]{2,1,0:T(8,128)S(1)}, f32[10,16,128]{2,1,0:T(8,128)S(1)}, u32[]{:S(2)}, u32[]{:S(2)}) %collective-permute-start.15) | collective-permute-done | bytes 81952 | tf_op jit(solution)/shard_map/ppermute | solution.py:336
  54.3 2.1 %collective-permute-done.16.refs_1_ = f32[10,16,128]{2,1,0:T(8,128)S(1)} collective-permute-done((f32[10,16,128]{2,1,0:T(8,128)S(1)}, f32[10,16,128]{2,1,0:T(8,128)S(1)}, u32[]{:S(2)}, u32[]{:S(2)}) %collective-permute-start.16) | collective-permute-done | bytes 81952 | tf_op jit(solution)/shard_map/ppermute | solution.py:336
  56.4 1.1 %collective-permute-done.17.refs_2_ = f32[10,16,128]{2,1,0:T(8,128)S(1)} collective-permute-done((f32[10,16,128]{2,1,0:T(8,128)S(1)}, f32[10,16,128]{2,1,0:T(8,128)S(1)}, u32[]{:S(2)}, u32[]{:S(2)}) %collective-permute-start.17) | collective-permute-done | bytes 81952 | tf_op jit(solution)/shard_map/ppermute | solution.py:336
  57.5 4.4 %shard_map.88 = f32[512,256]{1,0:T(8,128)} custom-call(f32[10,16,128]{2,1,0:T(8,128)S(1)} %add.3.own_ref, f32[512,256]{1,0:T(8,128)S(1)} %bitcast.16, f32[16,256]{1,0:T(8,128)S(1)} %get-tuple-element.40.a_ref, bf16[928,2048]{1,0:T(8,128)(2,1)S(1)} %get-tuple-element.41.x_ref, bf16[512,2048]{1,0:T(8,128)(2,1)S(1)} %get-tuple-element.42.h_ref, ...), custom_call_target="tpu_custom_call" | custom-call | flops 4000000000 | bytes 1048576 | tf_op jit(solution)/shard_map/pallas_call | solution.py:314
  61.9 4.6 %all-to-all-start.1 = ((f32[16,32,256]{2,1,0:T(8,128)}), f32[16,32,256]{2,1,0:T(8,128)S(1)}, u32[]{:S(2)}, u32[]{:S(2)}) async-start(f32[16,32,256]{2,1,0:T(8,128)} %bitcast.6), calls=%async_computation.1 | async-start | bytes 1048576 | tf_op jit(solution)/shard_map/all_to_all | solution.py:404
  66.6 1.6 %shard_map.89 = (f32[464,128]{1,0:T(8,128)S(1)}, f32[464,128]{1,0:T(8,128)S(1)}) custom-call(s32[2]{0:T(128)S(1)} %pad_add_fusion.at_ref, f32[464,128]{1,0:T(8,128)S(1)} %bitcast.20, f32[464,128]{1,0:T(8,128)S(1)} %bitcast.21, f32[464,128]{1,0:T(8,128)S(1)} %bitcast.22), custom_call_target="tpu_custom_call" | custom-call | flops 1000000000 | bytes 1048576 | tf_op jit(solution)/shard_map/pallas_call | solution.py:314
  68.3 12.6 %all-to-all-done.1 = f32[16,32,256]{2,1,0:T(8,128)S(1)} async-done(((f32[16,32,256]{2,1,0:T(8,128)}), f32[16,32,256]{2,1,0:T(8,128)S(1)}, u32[]{:S(2)}, u32[]{:S(2)}) %all-to-all-start.1) | async-done | bytes 524320 | tf_op jit(solution)/shard_map/all_to_all | solution.py:404
  80.8 1.5 %shard_map.90 = (f32[464,128]{1,0:T(8,128)}, f32[464,128]{1,0:T(8,128)}, f32[1,128]{1,0:T(1,128)}) custom-call(s32[2]{0:T(128)S(1)} %pad_add_fusion.at_ref, f32[512,256]{1,0:T(8,128)S(1)} %bitcast.17, f32[464,128]{1,0:T(8,128)S(1)} %get-tuple-element.44.base_ref, f32[464,128]{1,0:T(8,128)S(1)} %get-tuple-element.45.par_ref), custom_call_target="tpu_custom_call" | custom-call | flops 1000000000 | bytes 1048576 | tf_op jit(solution)/shard_map/pallas_call | solution.py:314
  (38 shorter events, 7.3 us)
Async XLA Ops:
  0.6 1.2 %copy-start = (f32[512,448]{0,1:T(8,128)S(1)}, f32[512,448]{0,1:T(8,128)}, u32[]{:S(2)}) copy-start(f32[512,448]{0,1:T(8,128)} %param.9) | copy-start | bytes 2752516
  5.9 34.2 %all-to-all-start = ((f32[16,32,256]{2,1,0:T(8,128)}), f32[16,32,256]{2,1,0:T(8,128)S(1)}, u32[]{:S(2)}, u32[]{:S(2)}) async-start(f32[16,32,256]{2,1,0:T(8,128)} %shard_map.86), calls=%async_computation | async-start | bytes 1048576 | tf_op jit(solution)/shard_map/all_to_all | solution.py:370
  13.2 17.2 %collective-permute-start.2 = (f32[464,128]{1,0:T(8,128)S(1)}, f32[464,128]{1,0:T(8,128)S(1)}, u32[]{:S(2)}, u32[]{:S(2)}) collective-permute-start(f32[464,128]{1,0:T(8,128)S(1)} %get-tuple-element.29.refs_0_), channel_id=1, source_target_pairs={{0,4},{1,5},{2,6},{3,7},{4,0},{5,1},{6,2},{7,3},{8,12},{9,13},{10,... | collective-permute-start | bytes 712712 | tf_op jit(solution)/shard_map/ppermute | solution.py:336
  15.2 16.7 %collective-permute-start.1 = (f32[464,128]{1,0:T(8,128)S(1)}, f32[464,128]{1,0:T(8,128)S(1)}, u32[]{:S(2)}, u32[]{:S(2)}) collective-permute-start(f32[464,128]{1,0:T(8,128)S(1)} %get-tuple-element.30.refs_1_), channel_id=1, source_target_pairs={{0,2},{1,3},{2,0},{3,1},{4,6},{5,7},{6,4},{7,5},{8,10},{9,11},{10,... | collective-permute-start | bytes 712712 | tf_op jit(solution)/shard_map/ppermute | solution.py:336
  16.6 15.8 %collective-permute-start = (f32[464,128]{1,0:T(8,128)S(1)}, f32[464,128]{1,0:T(8,128)S(1)}, u32[]{:S(2)}, u32[]{:S(2)}) collective-permute-start(f32[464,128]{1,0:T(8,128)S(1)} %get-tuple-element.29.refs_0_), channel_id=1, source_target_pairs={{0,2},{1,3},{2,0},{3,1},{4,6},{5,7},{6,4},{7,5},{8,10},{9,11},{10,... | collective-permute-start | bytes 712712 | tf_op jit(solution)/shard_map/ppermute | solution.py:336
  17.2 18.3 %collective-permute-start.3 = (f32[464,128]{1,0:T(8,128)S(1)}, f32[464,128]{1,0:T(8,128)S(1)}, u32[]{:S(2)}, u32[]{:S(2)}) collective-permute-start(f32[464,128]{1,0:T(8,128)S(1)} %get-tuple-element.30.refs_1_), channel_id=1, source_target_pairs={{0,4},{1,5},{2,6},{3,7},{4,0},{5,1},{6,2},{7,3},{8,12},{9,13},{10,... | collective-permute-start | bytes 712712 | tf_op jit(solution)/shard_map/ppermute | solution.py:336
  30.4 6.8 %collective-permute-start.4 = (f32[464,128]{1,0:T(8,128)S(1)}, f32[464,128]{1,0:T(8,128)S(1)}, u32[]{:S(2)}, u32[]{:S(2)}) collective-permute-start(f32[464,128]{1,0:T(8,128)S(1)} %collective-permute-done.2.refs_8_), channel_id=1, source_target_pairs={{0,2},{1,3},{2,0},{3,1},{4,6},{5,7},{6,4},{7,5},{8,10},{9,11},{10,... | collective-permute-start | bytes 712712 | tf_op jit(solution)/shard_map/ppermute | solution.py:336
  31.9 8.1 %collective-permute-start.5 = (f32[464,128]{1,0:T(8,128)S(1)}, f32[464,128]{1,0:T(8,128)S(1)}, u32[]{:S(2)}, u32[]{:S(2)}) collective-permute-start(f32[464,128]{1,0:T(8,128)S(1)} %collective-permute-done.1.refs_5_), channel_id=1, source_target_pairs={{0,4},{1,5},{2,6},{3,7},{4,0},{5,1},{6,2},{7,3},{8,12},{9,13},{10,... | collective-permute-start | bytes 712712 | tf_op jit(solution)/shard_map/ppermute | solution.py:336
  32.5 8.1 %collective-permute-start.6 = (f32[464,128]{1,0:T(8,128)S(1)}, f32[464,128]{1,0:T(8,128)S(1)}, u32[]{:S(2)}, u32[]{:S(2)}) collective-permute-start(f32[464,128]{1,0:T(8,128)S(1)} %get-tuple-element.29.refs_0_), channel_id=1, source_target_pairs={{0,1},{1,0},{2,3},{3,2},{4,5},{5,4},{6,7},{7,6},{8,9},{9,8},{10,11... | collective-permute-start | bytes 712712 | tf_op jit(solution)/shard_map/ppermute | solution.py:336
  32.5 8.6 %collective-permute-start.7 = (f32[464,128]{1,0:T(8,128)S(1)}, f32[464,128]{1,0:T(8,128)S(1)}, u32[]{:S(2)}, u32[]{:S(2)}) collective-permute-start(f32[464,128]{1,0:T(8,128)S(1)} %get-tuple-element.30.refs_1_), channel_id=1, source_target_pairs={{0,1},{1,0},{2,3},{3,2},{4,5},{5,4},{6,7},{7,6},{8,9},{9,8},{10,11... | collective-permute-start | bytes 712712 | tf_op jit(solution)/shard_map/ppermute | solution.py:336
  40.0 1.5 %collective-permute-start.8 = (f32[464,128]{1,0:T(8,128)S(1)}, f32[464,128]{1,0:T(8,128)S(1)}, u32[]{:S(2)}, u32[]{:S(2)}) collective-permute-start(f32[464,128]{1,0:T(8,128)S(1)} %collective-permute-done.refs_4_), channel_id=1, source_target_pairs={{0,1},{1,0},{2,3},{3,2},{4,5},{5,4},{6,7},{7,6},{8,9},{9,8},{10,11... | collective-permute-start | bytes 712712 | tf_op jit(solution)/shard_map/ppermute | solution.py:336
  40.0 1.8 %collective-permute-start.9 = (f32[464,128]{1,0:T(8,128)S(1)}, f32[464,128]{1,0:T(8,128)S(1)}, u32[]{:S(2)}, u32[]{:S(2)}) collective-permute-start(f32[464,128]{1,0:T(8,128)S(1)} %collective-permute-done.1.refs_5_), channel_id=1, source_target_pairs={{0,1},{1,0},{2,3},{3,2},{4,5},{5,4},{6,7},{7,6},{8,9},{9,8},{10,11... | collective-permute-start | bytes 712712 | tf_op jit(solution)/shard_map/ppermute | solution.py:336
  40.6 1.7 %collective-permute-start.10 = (f32[464,128]{1,0:T(8,128)S(1)}, f32[464,128]{1,0:T(8,128)S(1)}, u32[]{:S(2)}, u32[]{:S(2)}) collective-permute-start(f32[464,128]{1,0:T(8,128)S(1)} %collective-permute-done.2.refs_8_), channel_id=1, source_target_pairs={{0,1},{1,0},{2,3},{3,2},{4,5},{5,4},{6,7},{7,6},{8,9},{9,8},{10,11... | collective-permute-start | bytes 712712 | tf_op jit(solution)/shard_map/ppermute | solution.py:336
  40.6 2.0 %collective-permute-start.11 = (f32[464,128]{1,0:T(8,128)S(1)}, f32[464,128]{1,0:T(8,128)S(1)}, u32[]{:S(2)}, u32[]{:S(2)}) collective-permute-start(f32[464,128]{1,0:T(8,128)S(1)} %collective-permute-done.3.refs_9_), channel_id=1, source_target_pairs={{0,1},{1,0},{2,3},{3,2},{4,5},{5,4},{6,7},{7,6},{8,9},{9,8},{10,11... | collective-permute-start | bytes 712712 | tf_op jit(solution)/shard_map/ppermute | solution.py:336
  41.1 1.8 %collective-permute-start.12 = (f32[464,128]{1,0:T(8,128)S(1)}, f32[464,128]{1,0:T(8,128)S(1)}, u32[]{:S(2)}, u32[]{:S(2)}) collective-permute-start(f32[464,128]{1,0:T(8,128)S(1)} %collective-permute-done.4.refs_12_), channel_id=1, source_target_pairs={{0,1},{1,0},{2,3},{3,2},{4,5},{5,4},{6,7},{7,6},{8,9},{9,8},{10,11... | collective-permute-start | bytes 712712 | tf_op jit(solution)/shard_map/ppermute | solution.py:336
  41.5 1.7 %collective-permute-start.13 = (f32[464,128]{1,0:T(8,128)S(1)}, f32[464,128]{1,0:T(8,128)S(1)}, u32[]{:S(2)}, u32[]{:S(2)}) collective-permute-start(f32[464,128]{1,0:T(8,128)S(1)} %collective-permute-done.5.refs_13_), channel_id=1, source_target_pairs={{0,1},{1,0},{2,3},{3,2},{4,5},{5,4},{6,7},{7,6},{8,9},{9,8},{10,11... | collective-permute-start | bytes 712712 | tf_op jit(solution)/shard_map/ppermute | solution.py:336
  48.4 1.3 %collective-permute-start.14 = (f32[10,16,128]{2,1,0:T(8,128)S(1)}, f32[10,16,128]{2,1,0:T(8,128)S(1)}, u32[]{:S(2)}, u32[]{:S(2)}) collective-permute-start(f32[10,16,128]{2,1,0:T(8,128)S(1)} %get-tuple-element.39), channel_id=1, source_target_pairs={{0,1},{1,0},{2,3},{3,2},{4,5},{5,4},{6,7},{7,6},{8,9},{9,8},{10,11... | collective-permute-start | bytes 245768 | tf_op jit(solution)/shard_map/ppermute | solution.py:336
  49.7 4.6 %collective-permute-start.15 = (f32[10,16,128]{2,1,0:T(8,128)S(1)}, f32[10,16,128]{2,1,0:T(8,128)S(1)}, u32[]{:S(2)}, u32[]{:S(2)}) collective-permute-start(f32[10,16,128]{2,1,0:T(8,128)S(1)} %add.3.own_ref), channel_id=1, source_target_pairs={{0,2},{1,3},{2,0},{3,1},{4,6},{5,7},{6,4},{7,5},{8,10},{9,11},{10,... | collective-permute-start | bytes 245768 | tf_op jit(solution)/shard_map/ppermute | solution.py:336
  51.3 5.1 %collective-permute-start.16 = (f32[10,16,128]{2,1,0:T(8,128)S(1)}, f32[10,16,128]{2,1,0:T(8,128)S(1)}, u32[]{:S(2)}, u32[]{:S(2)}) collective-permute-start(f32[10,16,128]{2,1,0:T(8,128)S(1)} %add.3.own_ref), channel_id=1, source_target_pairs={{0,4},{1,5},{2,6},{3,7},{4,0},{5,1},{6,2},{7,3},{8,12},{9,13},{10,... | collective-permute-start | bytes 245768 | tf_op jit(solution)/shard_map/ppermute | solution.py:336
  51.8 5.6 %collective-permute-start.17 = (f32[10,16,128]{2,1,0:T(8,128)S(1)}, f32[10,16,128]{2,1,0:T(8,128)S(1)}, u32[]{:S(2)}, u32[]{:S(2)}) collective-permute-start(f32[10,16,128]{2,1,0:T(8,128)S(1)} %add.3.own_ref), channel_id=1, source_target_pairs={{0,6},{1,7},{2,4},{3,5},{4,2},{5,3},{6,0},{7,1},{8,14},{9,15},{10,... | collective-permute-start | bytes 245768 | tf_op jit(solution)/shard_map/ppermute | solution.py:336
  57.5 9.2 %copy-start.2 = (f32[59392]{0:T(1024)S(1)}, f32[59392]{0:T(1024)}, u32[]{:S(2)}) copy-start(f32[59392]{0:T(1024)} %param.6) | copy-start | bytes 712708
  57.5 9.2 %copy-start.3 = (f32[59392]{0:T(1024)S(1)}, f32[59392]{0:T(1024)}, u32[]{:S(2)}) copy-start(f32[59392]{0:T(1024)} %param.7) | copy-start | bytes 712708
  57.5 9.2 %copy-start.4 = (f32[1,59392]{1,0:T(1,128)S(1)}, f32[1,59392]{1,0:T(1,128)}, u32[]{:S(2)}) copy-start(f32[1,59392]{1,0:T(1,128)} %param.8) | copy-start | bytes 712708
  61.9 18.9 %all-to-all-start.1 = ((f32[16,32,256]{2,1,0:T(8,128)}), f32[16,32,256]{2,1,0:T(8,128)S(1)}, u32[]{:S(2)}, u32[]{:S(2)}) async-start(f32[16,32,256]{2,1,0:T(8,128)} %bitcast.6), calls=%async_computation.1 | async-start | bytes 1048576 | tf_op jit(solution)/shard_map/all_to_all | solution.py:404
  (3 other events, 2.3 us)
where the time goes:
time: 82.7 us; the launch traced here: 82.3 us
  waiting for transfers between devices  39.9 us (48%)
  starting transfers between devices  23.7 us (29%)
  Pallas kernels  14.4 us (17%)
  local copies, waits for them, and re-layouts  3.48 us (4%)
    ppermute x18, waiting for transfers between devices, hop(): return lax.ppermute(x, 'dp', [(d, d ^ k) for d in range(n)])  27.4 us
    pallas_call x6, Pallas kernels, call(): pl.pallas_call(kernel, out_shape=[jax.ShapeDtypeStruct(s, t) for s, t in...  14.4 us
    all_to_all x1, waiting for transfers between devices, fast_body(): got = lax.all_to_all(grads, 'dp', 0, 0, tiled=True)  12.6 us
    ppermute x18, starting transfers between devices, hop(): return lax.ppermute(x, 'dp', [(d, d ^ k) for d in range(n)])  11.7 us
    all_to_all x1, starting transfers between devices, fast_body(): weights = lax.all_to_all(cut.reshape(tall), 'dp', 0, 0, tiled=True)  7.38 us
    all_to_all x1, starting transfers between devices, fast_body(): got = lax.all_to_all(grads, 'dp', 0, 0, tiled=True)  4.65 us
    unnamed x14, local copies, waits for them, and re-layouts  3.48 us
  transfers between devices with their start and end apart: 20, of which 15 were waited for; matrix products, arithmetic and copies ran while one was open for 0% of the time, Pallas kernels for 2%

commit v1 on v0

--- a/solution.py
+++ b/solution.py
@@ -12,7 +12,7 @@
 H = 2048
 OUT = 10
 LANES = 128
-LIMIT = 16
+SHARE = 0.62
 COPIES = 2
 
 step_size = 0.02
@@ -34,22 +34,24 @@
         self.rows = shard_len // H
         self.pad = up8(self.rows + 1)
         self.step = H // LANES
+        self.early, self.rest = (0, 2, 4), (1, 3, 5, 6, 7)
         self.flat = shard_len // LANES
         self.batch = batch
-        self.half = batch // 2
         self.tail = din + 1 - (devices - 1) * self.rows
         gcd = math.gcd(LANES, OUT)
         self.hp, self.qp = LANES // gcd, OUT // gcd
         self.periods = self.cols // self.hp
         self.classes = up8(OUT)
         self.xrows = -(-(din + 2) // 16) * 16
+        first = round(SHARE * self.xrows / 16) * 16
+        self.parts = (slice(0, first), slice(first, self.xrows))
 
     @staticmethod
     def fits(devices, din, shard_len, batch):
         if devices & (devices - 1) or devices < 2 * COPIES or shard_len % (8 * LANES) or shard_len % H:
             return False
         group, rows = devices // COPIES, shard_len // H
-        if H % (group * LANES) or batch % (2 * LANES) or group not in (4, 8) or din % 8:
+        if H % (group * LANES) or batch % LANES or group != 8 or din % 8:
             return False
         tail = din + 1 - (devices - 1) * rows
         return 0 < tail and tail + OUT + 1 <= rows
@@ -78,26 +80,19 @@
     return lax.broadcasted_iota(jnp.int32, shape, axis)
 
 
-def pick_kernel(plan, img_ref, lab_ref, idx_ref, *refs):
-    parts, (img, lab, idx, sems) = refs[:-4], refs[-4:]
-    loads = [pltpu.make_async_copy(s, d, sems.at[i]) for i, (s, d) in enumerate(
-        ((idx_ref, idx), (lab_ref, lab), (img_ref, img)))]
-    for load in loads:
-        load.start()
-    for load in loads:
-        load.wait()
-    pool = img.shape[1]
-    hot = (iota((pool, plan.batch), 0) == idx[...]).astype(BF16)
-    hi, mid, lo = split3(img[...])
+def pick_kernel(plan, img_ref, meta_ref, *parts):
+    pool = img_ref.shape[1]
+    picks = meta_ref[:, pool:].astype(jnp.int32)
+    hot = (iota((pool, plan.batch), 0) == picks).astype(BF16)
+    hi, mid, lo = split3(img_ref[...])
     rows = dot(hi, hot, NN) + dot(mid, hot, NN) + dot(lo, hot, NN)
     spare = plan.xrows - plan.din
-    marks = jnp.broadcast_to(lab[...].astype(F32), (spare, pool)).astype(BF16)
+    marks = jnp.broadcast_to(meta_ref[:, :pool], (spare, pool)).astype(BF16)
     marks = dot(marks, hot, NN)
     at = iota((spare, plan.batch), 0)
-    marks = jnp.where(at == 0, 1.0, jnp.where(at == 1, marks, 0.0))
-    for i, part in enumerate(parts):
-        part[: plan.din, :] = rows[:, i * plan.half : (i + 1) * plan.half]
-        part[plan.din :, :] = marks[:, i * plan.half : (i + 1) * plan.half]
+    rows = jnp.concatenate([rows, jnp.where(at == 0, 1.0, jnp.where(at == 1, marks, 0.0))], axis=0)
+    for part, ref in zip(plan.parts, parts):
+        ref[...] = rows[part]
 
 
 def cut_kernel(plan, last_ref, par_ref, out_ref):
@@ -142,9 +137,7 @@
     return [(d, d * plan.rows, min(plan.rows, plan.din + 1 - d * plan.rows)) for d in range(plan.n)]
 
 
-def forward_kernel(plan, w_ref, *refs):
-    x_refs = refs[: 2 * plan.group]
-    x_ref, h_ref, a_ref, own_ref, send_ref, lab_ref, c_ref = refs[2 * plan.group :]
+def out_weights(plan, w_ref, a_ref):
     mask, place = class_masks(plan)
     lhs = []
     for p in range(plan.periods):
@@ -158,41 +151,97 @@
     for p in range(plan.periods):
         rows = slice(p * plan.classes, (p + 1) * plan.classes)
         a_ref[:, p * plan.hp : (p + 1) * plan.hp] = out_w[rows]
-    a_hi, a_lo = split(a_ref[...])
-    a_cat = jnp.concatenate([a_hi, a_lo], axis=0)
+
+
+def split_rows(plan, parts, x_ref, here):
+    for part, ref in zip(plan.parts, parts):
+        hi, lo = split(ref[...])
+        x_ref[part, here] = hi
+        x_ref[plan.xrows + part.start : plan.xrows + part.stop, here] = lo
+
+
+def keep_labels(plan, m, ref, lab_ref):
+    per = plan.batch // LANES
+    mark = plan.din + 1 - plan.parts[1].start
+    for i in range(per):
+        row = ref[mark : mark + 1, i * LANES : (i + 1) * LANES]
+        lab_ref[m * per + i : m * per + i + 1, :] = row
+
+
+def forward_slot(plan, m, x, w_cat, a_cat, h_ref, here, own_ref, send_ref):
+    per = plan.batch // LANES
+    x_hi, x_lo = x
+    pre = dot(w_cat, x_hi, NN)
+    hidden = jnp.tanh(pre[: plan.cols] + (pre[plan.cols :] + dot(w_cat[: plan.cols], x_lo, NN)))
+    h_hi, h_lo = split(hidden)
+    h_ref[: plan.cols, here] = h_hi
+    h_ref[plan.cols :, here] = h_lo
+    lg = dot(a_cat, h_hi, NN)
+    lg = lg[: plan.classes] + (lg[plan.classes :] + dot(a_cat[: plan.classes], h_lo, NN))
+    for i in range(per):
+        own, other = m * per + i, (m ^ 1) * per + i
+        for o in range(OUT):
+            row = lg[o : o + 1, i * LANES : (i + 1) * LANES]
+            own_ref[o, own : own + 1, :] = row
+            send_ref[o, other : other + 1, :] = row
+
+
+def ready_kernel(plan, *refs):
+    join_ref, lab_ref = refs[-2:]
+    lab_ref[...] = jnp.zeros_like(lab_ref)
+    for s, m in enumerate(plan.early):
+        pair = refs[2 * s : 2 * s + 2]
+        keep_labels(plan, m, pair[1], lab_ref)
+        for part, ref in zip(plan.parts, pair):
+            join_ref[s, part, :] = ref[...]
+
+
+def front_kernel(plan, w_ref, join_ref, x_ref, h_ref, a_ref, cat_ref, own_ref, send_ref, c_ref):
+    out_weights(plan, w_ref, a_ref)
+    a_cat = jnp.concatenate(split(a_ref[...]), axis=0)
     c_ref[...] = jnp.zeros_like(c_ref)
-    for d, first, count in blocks_of(plan):
-        c_ref[first : first + count, :] = w_ref[d * plan.pad : d * plan.pad + count, :]
-    w_hi, w_lo = split(c_ref[...].T)
-    w_cat = jnp.concatenate([w_hi, w_lo], axis=0)
-    per = plan.batch // LANES
-    for m in range(plan.group):
-        here = slice(m * plan.batch, (m + 1) * plan.batch)
-        got = jnp.concatenate([x_refs[2 * m][...], x_refs[2 * m + 1][...]], axis=1)
-        for i in range(per):
-            line = got[plan.din + 1 : plan.din + 2, i * LANES : (i + 1) * LANES]
-            lab_ref[m * per + i : m * per + i + 1, :] = line
-        x_hi, x_lo = split(got)
-        x_ref[: plan.xrows, here] = x_hi
-        x_ref[plan.xrows :, here] = x_lo
-        pre = dot(w_cat, x_hi, NN)
-        hidden = jnp.tanh(pre[: plan.cols] + (pre[plan.cols :] + dot(w_hi, x_lo, NN)))
-        h_hi, h_lo = split(hidden)
-        h_ref[: plan.cols, here] = h_hi
-        h_ref[plan.cols :, here] = h_lo
-        lg = dot(a_cat, h_hi, NN)
-        lg = lg[: plan.classes] + (lg[plan.classes :] + dot(a_hi, h_lo, NN))
-        for i in range(per):
-            for o in range(OUT):
-                row = lg[o : o + 1, i * LANES : (i + 1) * LANES]
-                own_ref[o, m * per + i : m * per + i + 1, :] = row
-                send_ref[o, (m ^ 1) * per + i : (m ^ 1) * per + i + 1, :] = row
-
-
-def backward_kernel(plan, own_ref, w_ref, a_ref, x_ref, h_ref, lab_ref, *refs):
+    for d, first, rows in blocks_of(plan):
+        c_ref[first : first + rows, :] = w_ref[d * plan.pad : d * plan.pad + rows, :]
+    w_cat = jnp.concatenate(split(c_ref[...].T), axis=0)
+    cat_ref[...] = w_cat
+    own_ref[...] = jnp.zeros_like(own_ref)
+    send_ref[...] = jnp.zeros_like(send_ref)
+    for s, m in enumerate(plan.early):
+        here = slice(s * plan.batch, (s + 1) * plan.batch)
+        x = split(join_ref[s])
+        x_ref[: plan.xrows, here] = x[0]
+        x_ref[plan.xrows :, here] = x[1]
+        forward_slot(plan, m, x, w_cat, a_cat, h_ref, here, own_ref, send_ref)
+
+
+def rest_kernel(plan, cat_ref, a_ref, own1_ref, send1_ref, lab1_ref, join_ref, *refs):
+    x_ref, h_ref, own_ref, send_ref, lab_ref = refs[-5:]
+    own_ref[...] = own1_ref[...]
+    send_ref[...] = send1_ref[...]
+    lab_ref[...] = lab1_ref[...]
+    w_cat = cat_ref[...]
+    a_cat = jnp.concatenate(split(a_ref[...]), axis=0)
+    mark, joined = plan.parts[1].start, len(plan.early)
+    for s, m in enumerate(plan.rest):
+        here = slice(s * plan.batch, (s + 1) * plan.batch)
+        if s < joined:
+            keep_labels(plan, m, join_ref.at[s, mark:, :], lab_ref)
+            x = split(join_ref[s])
+            x_ref[: plan.xrows, here] = x[0]
+            x_ref[plan.xrows :, here] = x[1]
+        else:
+            pair = refs[2 * (s - joined) :][:2]
+            keep_labels(plan, m, pair[1], lab_ref)
+            split_rows(plan, pair, x_ref, here)
+            x = x_ref[: plan.xrows, here], x_ref[plan.xrows :, here]
+        forward_slot(plan, m, x, w_cat, a_cat, h_ref, here, own_ref, send_ref)
+
+
+def backward_kernel(plan, own_ref, w_ref, a_ref, x1_ref, x2_ref, h1_ref, h2_ref, lab_ref, *refs):
     lg_refs, (out_ref, lg_ref, dl_ref, dh_ref, dw_ref) = refs[:-5], refs[-5:]
     per = plan.batch // LANES
     lines = plan.group * per
+    order = (*plan.early, *plan.rest)
     diag = iota((plan.classes, LANES), 0) == iota((plan.classes, LANES), 1)
     row = (plan.n - 1) * plan.pad + plan.tail + OUT
     bias = w_ref[row : row + 1, :LANES]
@@ -215,30 +264,44 @@
     for o in range(OUT):
         value = ex[o] * share - jnp.where(hits[o], 1.0, 0.0)
         for i in range(lines):
-            dl_ref[o : o + 1, i * LANES : (i + 1) * LANES] = value[i : i + 1, :]
+            at = (order.index(i // per) * per + i % per) * LANES
+            dl_ref[o : o + 1, at : at + LANES] = value[i : i + 1, :]
     dl = dl_ref[...]
     dbias = jnp.sum(dl, axis=1, keepdims=True)
     dbias = jnp.sum(jnp.where(diag, dbias, 0.0), axis=0, keepdims=True)
     dl_hi, dl_lo = split(dl)
-    at_hi, at_lo = split(a_ref[...].T)
-    at_cat = jnp.concatenate([at_hi, at_lo], axis=0)
-    for m in range(plan.group):
-        here = slice(m * plan.batch, (m + 1) * plan.batch)
-        hidden = h_ref[: plan.cols, here].astype(F32) + h_ref[plan.cols :, here].astype(F32)
-        dh = dot(at_cat, dl_hi[:, here], NN)
-        dh = dh[: plan.cols] + (dh[plan.cols :] + dot(at_hi, dl_lo[:, here], NN))
-        dh_hi, dh_lo = split(dh * (1.0 - hidden * hidden))
-        dh_ref[: plan.cols, here] = dh_hi
-        dh_ref[plan.cols :, here] = dh_lo
-    da = dot(h_ref[...], dl_hi, NT)
-    da = da[: plan.cols] + (da[plan.cols :] + dot(h_ref[: plan.cols, :], dl_lo, NT))
-    dw = dot(x_ref[...], dh_ref[: plan.cols, :], NT)
-    dw_ref[...] = dw[: plan.xrows] + (dw[plan.xrows :] + dot(x_ref[: plan.xrows, :], dh_ref[plan.cols :, :], NT))
+    dl_cat = jnp.concatenate([dl_hi, dl_lo], axis=0)
+    dl_three = jnp.concatenate([dl_hi, dl_hi, dl_lo], axis=0)
+    a_hi, a_lo = split(a_ref[...])
+    a_three = jnp.concatenate([v.astype(F32) for v in (a_hi, a_lo, a_hi)], axis=0).T.astype(BF16)
+    cols, xrows, classes = plan.cols, plan.xrows, plan.classes
+    da, start = 0.0, 0
+    for h_ref in (h1_ref, h2_ref):
+        width = h_ref.shape[1]
+        for at in range(0, width, plan.batch):
+            here = slice(start + at, start + at + plan.batch)
+            local = slice(at, at + plan.batch)
+            hidden = h_ref[:cols, local].astype(F32) + h_ref[cols:, local].astype(F32)
+            dh = dot(a_three, dl_three[:, here], NN)
+            dh_hi, dh_lo = split(dh * (1.0 - hidden * hidden))
+            dh_ref[:cols, here] = dh_hi
+            dh_ref[cols:, here] = dh_lo
+        da = da + dot(h_ref[...], dl_cat[:, start : start + width], NT)
+        start += width
+    da = da.T
+    da = da[:classes, :cols] + (da[classes:, :cols] + da[:classes, cols:])
+    dw, start = 0.0, 0
+    for x_ref in (x1_ref, x2_ref):
+        here = slice(start, start + x_ref.shape[1])
+        part = dot(x_ref[...], dh_ref[:cols, here], NT)
+        dw = dw + (part[:xrows] + (part[xrows:] + dot(x_ref[:xrows, :], dh_ref[cols:, here], NT)))
+        start = here.stop
+    dw_ref[...] = dw
     out_ref[...] = jnp.zeros_like(out_ref)
     for d, first, count in blocks_of(plan):
         out_ref[d * plan.pad : d * plan.pad + count, :] = dw_ref[first : first + count, :]
     mask, place = class_masks(plan)
-    hi, mid, lo = split3(da.T)
+    hi, mid, lo = split3(da)
     parts = []
     for v in (hi, mid, lo):
         parts.append(jnp.concatenate([v[:, p * plan.hp : (p + 1) * plan.hp] for p in range(plan.periods)], axis=0))
@@ -336,62 +399,65 @@
         return lax.ppermute(x, "dp", [(d, d ^ k) for d in range(n)])
 
 
-    rows = call(
+    meta = jnp.concatenate([labels, indices[0]]).astype(F32).reshape(1, -1)
+    a, b = call(
         functools.partial(pick_kernel, plan),
-        (images.T, labels.reshape(1, pool), indices),
-        [((plan.xrows, plan.half), F32)] * 2,
-        [
-            pltpu.VMEM((din, pool), F32),
-            pltpu.VMEM((1, pool), jnp.int32),
-            pltpu.VMEM((1, plan.batch), jnp.int32),
-            pltpu.SemaphoreType.DMA((3,)),
-        ],
-        whole=3,
-        limit=LIMIT,
-    )
-    *rows, mine = lax.optimization_barrier((*rows, params))
+        (images.T, meta),
+        [((part.stop - part.start, plan.batch), F32) for part in plan.parts],
+    )
+    b2 = hop(b, 2)
+    a4 = hop(a, 4)
+    a2 = hop(a, 2)
+    b4 = hop(b, 4)
+    a6 = hop(a4, 2)
+    b6 = hop(b2, 4)
     (cut,) = call(
         functools.partial(cut_kernel, plan),
-        (last.reshape(1), mine.reshape(flat)),
+        (last.reshape(1), params.reshape(flat)),
         [((n, plan.pad, plan.cols), F32)],
         smem=1,
     )
-    near = [hop(r, 1) for r in rows]
-    xs = {0: rows}
-    b2, a4 = hop(rows[1], 2), None
-    if plan.group == 8:
-        a4 = hop(rows[0], 4)
-    a2 = hop(rows[0], 2)
-    xs[2] = [a2, b2]
-    if plan.group == 8:
-        b4 = hop(rows[1], 4)
-        xs[4] = [a4, b4]
-        xs[6] = [hop(a4, 2), hop(b2, 4)]
     weights = lax.all_to_all(cut.reshape(tall), "dp", 0, 0, tiled=True)
-    far = [m for m in xs if m]
-    weights, *got = lax.optimization_barrier((weights, *(h for m in far for h in xs[m])))
-    slots = [*rows, *near]
-    for i in range(0, len(got), 2):
-        slots += got[i : i + 2] + [hop(h, 1) for h in got[i : i + 2]]
-    x, hidden, outw, own, send, marks = call(
-        functools.partial(forward_kernel, plan),
-        (weights, *slots),
+    half = len(plan.early) * plan.batch
+    join, marks = call(
+        functools.partial(ready_kernel, plan),
+        (a, b, a2, b2, a4, b4),
+        [((len(plan.early), plan.xrows, plan.batch), F32), (dense[1:], F32)],
+    )
+    weights, join = lax.optimization_barrier((weights, join))
+    other = hop(join, 1)
+    x1, h1, outw, cat, own, send = call(
+        functools.partial(front_kernel, plan),
+        (weights, join),
         [
-            ((2 * plan.xrows, total), BF16),
-            ((2 * plan.cols, total), BF16),
+            ((2 * plan.xrows, half), BF16),
+            ((2 * plan.cols, half), BF16),
             ((plan.classes, plan.cols), F32),
+            ((2 * plan.cols, plan.xrows), BF16),
+            (dense, F32),
+            (dense, F32),
+        ],
+        [pltpu.VMEM((plan.xrows, plan.cols), F32)],
+        cost=3,
+    )
+    outw, a6, b6 = lax.optimization_barrier((outw, a6, b6))
+    x2, h2, own, send, marks = call(
+        functools.partial(rest_kernel, plan),
+        (cat, outw, own, send, marks, other, a6, b6, hop(a6, 1), hop(b6, 1)),
+        [
+            ((2 * plan.xrows, total - half), BF16),
+            ((2 * plan.cols, total - half), BF16),
             (dense, F32),
             (dense, F32),
             (dense[1:], F32),
         ],
-        [pltpu.VMEM((plan.xrows, plan.cols), F32)],
-        cost=4,
+        cost=3,
     )
     own = own + hop(send, 1)
     more = [hop(own, k) for k in range(2, plan.group, 2)]
     (grads,) = call(
         functools.partial(backward_kernel, plan),
-        (own, weights, outw, x, hidden, marks, *more),
+        (own, weights, outw, x1, x2, h1, h2, marks, *more),
         [(tall, F32)],
         [
             pltpu.VMEM(dense, F32),

time: 82.7 us -> 79.5 us (0.961)
  local copies, waits for them, and re-layouts: 3.48 us -> 0.96 us
  waiting for transfers between devices: 39.9 us -> 41.6 us
  Pallas kernels: 14.4 us -> 13.2 us
  starting transfers between devices: 23.7 us -> 22.6 us
    unnamed x14, local copies, waits for them, and re-layouts: 3.48 us -> 0.96 us
    ppermute x18 -> x13, waiting for transfers between devices: 27.4 us -> 29 us  [hop(): return lax.ppermute(x, 'dp', [(d, d ^ k) for d in range(n)])]
    pallas_call x6 -> x8, Pallas kernels: 14.4 us -> 13.2 us  [call(): pl.pallas_call(kernel, out_shape=[jax.ShapeDtypeStruct(s, t) for s, t in...]
    ppermute x18 -> x13, starting transfers between devices: 11.7 us -> 10.5 us  [hop(): return lax.ppermute(x, 'dp', [(d, d ^ k) for d in range(n)])]
  transfers between devices with their start and end apart: 20 -> 15, of which waited for: 15 -> 10; matrix products, arithmetic and copies ran while one was open for 0% -> 0% of each run, Pallas kernels for 2% -> 5%
where the time goes in v1:
time: 79.5 us; the launch traced here: 79.2 us
  waiting for transfers between devices  41.6 us (52%)
  starting transfers between devices  22.6 us (28%)
  Pallas kernels  13.2 us (17%)
  local copies, waits for them, and re-layouts  0.96 us (1%)
    ppermute x13, waiting for transfers between devices, hop(): return lax.ppermute(x, 'dp', [(d, d ^ k) for d in range(n)])  29 us
    pallas_call x8, Pallas kernels, call(): pl.pallas_call(kernel, out_shape=[jax.ShapeDtypeStruct(s, t) for s, t in...  13.2 us
    all_to_all x1, waiting for transfers between devices, fast_body(): got = lax.all_to_all(grads, 'dp', 0, 0, tiled=True)  12.6 us
    ppermute x13, starting transfers between devices, hop(): return lax.ppermute(x, 'dp', [(d, d ^ k) for d in range(n)])  10.5 us
    all_to_all x1, starting transfers between devices, fast_body(): weights = lax.all_to_all(cut.reshape(tall), 'dp', 0, 0, tiled=True)  7.39 us
    all_to_all x1, starting transfers between devices, fast_body(): got = lax.all_to_all(grads, 'dp', 0, 0, tiled=True)  4.64 us
  transfers between devices with their start and end apart: 15, of which 10 were waited for; matrix products, arithmetic and copies ran while one was open for 0% of the time, Pallas kernels for 5%

profile of v1, /device:TPU:0, one launch (start us, length us, event | category | flops | bytes accessed | tf_op | source)
XLA Modules:
  0.0 79.2 jit_solution(10984394062055797838)
XLA Ops:
  0.6 0.9 %copy-done.1 = f32[59392]{0:T(1024)S(1)} copy-done((f32[59392]{0:T(1024)S(1)}, f32[59392]{0:T(1024)}, u32[]{:S(2)}) %copy-start.1) | copy-done | bytes 237592
  1.6 0.9 %shard_map.85 = f32[16,32,256]{2,1,0:T(8,128)} custom-call(s32[1]{0:T(128)} %bitcast.1.last_ref, f32[464,128]{1,0:T(8,128)S(1)} %bitcast.18), custom_call_target="tpu_custom_call" | custom-call | flops 1000000000 | bytes 1048576 | tf_op jit(solution)/shard_map/pallas_call | solution.py:377
  2.5 7.4 %all-to-all-start = ((f32[16,32,256]{2,1,0:T(8,128)}), f32[16,32,256]{2,1,0:T(8,128)S(1)}, u32[]{:S(2)}, u32[]{:S(2)}) async-start(f32[16,32,256]{2,1,0:T(8,128)} %shard_map.85), calls=%async_computation | async-start | bytes 1048576 | tf_op jit(solution)/shard_map/all_to_all | solution.py:420
  10.5 2.0 %collective-permute-start = (f32[288,256]{1,0:T(8,128)S(1)}, f32[288,256]{1,0:T(8,128)S(1)}, u32[]{:S(2)}, u32[]{:S(2)}) collective-permute-start(f32[288,256]{1,0:T(8,128)S(1)} %get-tuple-element.28.refs_0_), channel_id=1, source_target_pairs={{0,2},{1,3},{2,0},{3,1},{4,6},{5,7},{6,4},{7,5},{8,10},{9,11},{10,... | collective-permute-start | bytes 884744 | tf_op jit(solution)/shard_map/ppermute | solution.py:399
  12.5 1.5 %collective-permute-start.2 = (f32[288,256]{1,0:T(8,128)S(1)}, f32[288,256]{1,0:T(8,128)S(1)}, u32[]{:S(2)}, u32[]{:S(2)}) collective-permute-start(f32[288,256]{1,0:T(8,128)S(1)} %get-tuple-element.28.refs_0_), channel_id=1, source_target_pairs={{0,4},{1,5},{2,6},{3,7},{4,0},{5,1},{6,2},{7,3},{8,12},{9,13},{10,... | collective-permute-start | bytes 884744 | tf_op jit(solution)/shard_map/ppermute | solution.py:399
  14.6 14.2 %collective-permute-done.1.refs_3_ = f32[176,256]{1,0:T(8,128)S(1)} collective-permute-done((f32[176,256]{1,0:T(8,128)S(1)}, f32[176,256]{1,0:T(8,128)S(1)}, u32[]{:S(2)}, u32[]{:S(2)}) %collective-permute-start.1) | collective-permute-done | bytes 180256 | tf_op jit(solution)/shard_map/ppermute | solution.py:399
  28.8 2.8 %collective-permute-done.3.refs_5_ = f32[176,256]{1,0:T(8,128)S(1)} collective-permute-done((f32[176,256]{1,0:T(8,128)S(1)}, f32[176,256]{1,0:T(8,128)S(1)}, u32[]{:S(2)}, u32[]{:S(2)}) %collective-permute-start.3) | collective-permute-done | bytes 180256 | tf_op jit(solution)/shard_map/ppermute | solution.py:399
  31.8 1.5 %collective-permute-start.4 = (f32[288,256]{1,0:T(8,128)S(1)}, f32[288,256]{1,0:T(8,128)S(1)}, u32[]{:S(2)}, u32[]{:S(2)}) collective-permute-start(f32[288,256]{1,0:T(8,128)S(1)} %collective-permute-done.2.refs_4_), channel_id=1, source_target_pairs={{0,2},{1,3},{2,0},{3,1},{4,6},{5,7},{6,4},{7,5},{8,10},{9,11},{10,... | collective-permute-start | bytes 884744 | tf_op jit(solution)/shard_map/ppermute | solution.py:399
  33.9 1.9 %shard_map.88 = (bf16[928,768]{1,0:T(8,128)(2,1)S(1)}, bf16[512,768]{1,0:T(8,128)(2,1)S(1)}, f32[16,256]{1,0:T(8,128)S(1)}, bf16[512,464]{1,0:T(8,128)(2,1)S(1)}...) custom-call(f32[512,256]{1,0:T(8,128)S(1)} %bitcast.14, f32[3,464,256]{2,1,0:T(8,128)S(1)} %get-tuple-element.32.join_ref), custom_call_target="tpu_custom_call" | custom-call | flops 3000000000 | bytes 1048576 | tf_op jit(solution)/shard_map/pallas_call | solution.py:377
  35.8 4.1 %collective-permute-done.5.refs_1_ = f32[176,256]{1,0:T(8,128)S(1)} collective-permute-done((f32[176,256]{1,0:T(8,128)S(1)}, f32[176,256]{1,0:T(8,128)S(1)}, u32[]{:S(2)}, u32[]{:S(2)}) %collective-permute-start.5) | collective-permute-done | bytes 180256 | tf_op jit(solution)/shard_map/ppermute | solution.py:399
  39.9 1.3 %collective-permute-done.4.refs_0_ = f32[288,256]{1,0:T(8,128)S(1)} collective-permute-done((f32[288,256]{1,0:T(8,128)S(1)}, f32[288,256]{1,0:T(8,128)S(1)}, u32[]{:S(2)}, u32[]{:S(2)}) %collective-permute-start.4) | collective-permute-done | bytes 294944 | tf_op jit(solution)/shard_map/ppermute | solution.py:399
  41.7 1.3 %collective-permute-done.8.refs_3_ = f32[176,256]{1,0:T(8,128)S(1)} collective-permute-done((f32[176,256]{1,0:T(8,128)S(1)}, f32[176,256]{1,0:T(8,128)S(1)}, u32[]{:S(2)}, u32[]{:S(2)}) %collective-permute-start.8) | collective-permute-done | bytes 180256 | tf_op jit(solution)/shard_map/ppermute | solution.py:399
  43.0 3.0 %shard_map.89 = (bf16[928,1280]{1,0:T(8,128)(2,1)S(1)}, bf16[512,1280]{1,0:T(8,128)(2,1)S(1)}, f32[10,16,128]{2,1,0:T(8,128)S(1)}, f32[10,16,128]{2,1,0:T(8,128)S(1)}, f32[16,128]{1,0:T(8,128)S(1)}) custom-call(bf16[512,464]{1,0:T(8,128)(2,1)S(1)} %get-tuple-element.33.cat_ref, f32[16,256]{1,0:T(8,128)S(1)} %get-tuple-element.35.a_ref, ...), custom_call_target="tpu_custom_call" | custom-call | flops 3000000000 | bytes 1048576 | tf_op jit(solution)/shard_map/pallas_call | solution.py:377
  46.2 1.1 %collective-permute-done.9 = f32[10,16,128]{2,1,0:T(8,128)S(1)} collective-permute-done((f32[10,16,128]{2,1,0:T(8,128)S(1)}, f32[10,16,128]{2,1,0:T(8,128)S(1)}, u32[]{:S(2)}, u32[]{:S(2)}) %collective-permute-start.9) | collective-permute-done | bytes 81952 | tf_op jit(solution)/shard_map/ppermute | solution.py:399
  47.4 1.5 %collective-permute-start.10 = (f32[10,16,128]{2,1,0:T(8,128)S(1)}, f32[10,16,128]{2,1,0:T(8,128)S(1)}, u32[]{:S(2)}, u32[]{:S(2)}) collective-permute-start(f32[10,16,128]{2,1,0:T(8,128)S(1)} %add.3.own_ref), channel_id=1, source_target_pairs={{0,2},{1,3},{2,0},{3,1},{4,6},{5,7},{6,4},{7,5},{8,10},{9,11},{10,... | collective-permute-start | bytes 245768 | tf_op jit(solution)/shard_map/ppermute | solution.py:399
  49.5 1.5 %collective-permute-start.12 = (f32[10,16,128]{2,1,0:T(8,128)S(1)}, f32[10,16,128]{2,1,0:T(8,128)S(1)}, u32[]{:S(2)}, u32[]{:S(2)}) collective-permute-start(f32[10,16,128]{2,1,0:T(8,128)S(1)} %add.3.own_ref), channel_id=1, source_target_pairs={{0,6},{1,7},{2,4},{3,5},{4,2},{5,3},{6,0},{7,1},{8,14},{9,15},{10,... | collective-permute-start | bytes 245768 | tf_op jit(solution)/shard_map/ppermute | solution.py:399
  50.9 1.0 %collective-permute-done.10.refs_0_ = f32[10,16,128]{2,1,0:T(8,128)S(1)} collective-permute-done((f32[10,16,128]{2,1,0:T(8,128)S(1)}, f32[10,16,128]{2,1,0:T(8,128)S(1)}, u32[]{:S(2)}, u32[]{:S(2)}) %collective-permute-start.10) | collective-permute-done | bytes 81952 | tf_op jit(solution)/shard_map/ppermute | solution.py:399
  51.9 2.1 %collective-permute-done.11.refs_1_ = f32[10,16,128]{2,1,0:T(8,128)S(1)} collective-permute-done((f32[10,16,128]{2,1,0:T(8,128)S(1)}, f32[10,16,128]{2,1,0:T(8,128)S(1)}, u32[]{:S(2)}, u32[]{:S(2)}) %collective-permute-start.11) | collective-permute-done | bytes 81952 | tf_op jit(solution)/shard_map/ppermute | solution.py:399
  54.0 1.1 %collective-permute-done.12.refs_2_ = f32[10,16,128]{2,1,0:T(8,128)S(1)} collective-permute-done((f32[10,16,128]{2,1,0:T(8,128)S(1)}, f32[10,16,128]{2,1,0:T(8,128)S(1)}, u32[]{:S(2)}, u32[]{:S(2)}) %collective-permute-start.12) | collective-permute-done | bytes 81952 | tf_op jit(solution)/shard_map/ppermute | solution.py:399
  55.1 3.7 %shard_map.90 = f32[512,256]{1,0:T(8,128)} custom-call(f32[10,16,128]{2,1,0:T(8,128)S(1)} %add.3.own_ref, f32[512,256]{1,0:T(8,128)S(1)} %bitcast.15, f32[16,256]{1,0:T(8,128)S(1)} %get-tuple-element.35.a_ref, bf16[928,768]{1,0:T(8,128)(2,1)S(1)} %get-tuple-element.43.x1_ref, bf16[928,1280]{1,0:T(8,128)(2,1)S(1)} %get-tuple-element.44.x2_ref, ...), custom_call_target="tpu_custom_call" | custom-call | flops 4000000000 | bytes 1048576 | tf_op jit(solution)/shard_map/pallas_call | solution.py:377
  58.8 4.6 %all-to-all-start.1 = ((f32[16,32,256]{2,1,0:T(8,128)}), f32[16,32,256]{2,1,0:T(8,128)S(1)}, u32[]{:S(2)}, u32[]{:S(2)}) async-start(f32[16,32,256]{2,1,0:T(8,128)} %bitcast.6), calls=%async_computation.1 | async-start | bytes 1048576 | tf_op jit(solution)/shard_map/all_to_all | solution.py:470
  63.5 1.6 %shard_map.91 = (f32[464,128]{1,0:T(8,128)S(1)}, f32[464,128]{1,0:T(8,128)S(1)}) custom-call(s32[2]{0:T(128)S(1)} %pad_add_fusion.at_ref, f32[464,128]{1,0:T(8,128)S(1)} %bitcast.19, f32[464,128]{1,0:T(8,128)S(1)} %bitcast.20, f32[464,128]{1,0:T(8,128)S(1)} %bitcast.21), custom_call_target="tpu_custom_call" | custom-call | flops 1000000000 | bytes 1048576 | tf_op jit(solution)/shard_map/pallas_call | solution.py:377
  65.1 12.6 %all-to-all-done.1 = f32[16,32,256]{2,1,0:T(8,128)S(1)} async-done(((f32[16,32,256]{2,1,0:T(8,128)}), f32[16,32,256]{2,1,0:T(8,128)S(1)}, u32[]{:S(2)}, u32[]{:S(2)}) %all-to-all-start.1) | async-done | bytes 524320 | tf_op jit(solution)/shard_map/all_to_all | solution.py:470
  77.7 1.5 %shard_map.92 = (f32[464,128]{1,0:T(8,128)}, f32[464,128]{1,0:T(8,128)}, f32[1,128]{1,0:T(1,128)}) custom-call(s32[2]{0:T(128)S(1)} %pad_add_fusion.at_ref, f32[512,256]{1,0:T(8,128)S(1)} %bitcast.16, f32[464,128]{1,0:T(8,128)S(1)} %get-tuple-element.48.base_ref, f32[464,128]{1,0:T(8,128)S(1)} %get-tuple-element.49.par_ref), custom_call_target="tpu_custom_call" | custom-call | flops 1000000000 | bytes 1048576 | tf_op jit(solution)/shard_map/pallas_call | solution.py:377
  (31 shorter events, 3.4 us)
Async XLA Ops:
  0.6 0.9 %copy-start.1 = (f32[59392]{0:T(1024)S(1)}, f32[59392]{0:T(1024)}, u32[]{:S(2)}) copy-start(f32[59392]{0:T(1024)} %param.6) | copy-start | bytes 712708
  1.6 8.3 %copy-start.5 = (s32[512]{0:T(512)S(1)}, s32[512]{0:T(512)}, u32[]{:S(2)}) copy-start(s32[512]{0:T(512)} %param.10) | copy-start | bytes 6148
  1.6 8.3 %copy-start.6 = (s32[1,256]{1,0:T(1,128)S(1)}, s32[1,256]{1,0:T(1,128)}, u32[]{:S(2)}) copy-start(s32[1,256]{1,0:T(1,128)} %param.11) | copy-start | bytes 3076
  1.6 8.3 %copy-start = (f32[512,448]{0,1:T(8,128)S(1)}, f32[512,448]{0,1:T(8,128)}, u32[]{:S(2)}) copy-start(f32[512,448]{0,1:T(8,128)} %param.9) | copy-start | bytes 2752516
  2.5 29.2 %all-to-all-start = ((f32[16,32,256]{2,1,0:T(8,128)}), f32[16,32,256]{2,1,0:T(8,128)S(1)}, u32[]{:S(2)}, u32[]{:S(2)}) async-start(f32[16,32,256]{2,1,0:T(8,128)} %shard_map.85), calls=%async_computation | async-start | bytes 1048576 | tf_op jit(solution)/shard_map/all_to_all | solution.py:420
  10.5 21.1 %collective-permute-start = (f32[288,256]{1,0:T(8,128)S(1)}, f32[288,256]{1,0:T(8,128)S(1)}, u32[]{:S(2)}, u32[]{:S(2)}) collective-permute-start(f32[288,256]{1,0:T(8,128)S(1)} %get-tuple-element.28.refs_0_), channel_id=1, source_target_pairs={{0,2},{1,3},{2,0},{3,1},{4,6},{5,7},{6,4},{7,5},{8,10},{9,11},{10,... | collective-permute-start | bytes 884744 | tf_op jit(solution)/shard_map/ppermute | solution.py:399
  12.5 19.1 %collective-permute-start.2 = (f32[288,256]{1,0:T(8,128)S(1)}, f32[288,256]{1,0:T(8,128)S(1)}, u32[]{:S(2)}, u32[]{:S(2)}) collective-permute-start(f32[288,256]{1,0:T(8,128)S(1)} %get-tuple-element.28.refs_0_), channel_id=1, source_target_pairs={{0,4},{1,5},{2,6},{3,7},{4,0},{5,1},{6,2},{7,3},{8,12},{9,13},{10,... | collective-permute-start | bytes 884744 | tf_op jit(solution)/shard_map/ppermute | solution.py:399
  13.9 14.8 %collective-permute-start.1 = (f32[176,256]{1,0:T(8,128)S(1)}, f32[176,256]{1,0:T(8,128)S(1)}, u32[]{:S(2)}, u32[]{:S(2)}) collective-permute-start(f32[176,256]{1,0:T(8,128)S(1)} %get-tuple-element.29.refs_1_), channel_id=1, source_target_pairs={{0,2},{1,3},{2,0},{3,1},{4,6},{5,7},{6,4},{7,5},{8,10},{9,11},{10,... | collective-permute-start | bytes 540680 | tf_op jit(solution)/shard_map/ppermute | solution.py:399
  14.5 17.1 %collective-permute-start.3 = (f32[176,256]{1,0:T(8,128)S(1)}, f32[176,256]{1,0:T(8,128)S(1)}, u32[]{:S(2)}, u32[]{:S(2)}) collective-permute-start(f32[176,256]{1,0:T(8,128)S(1)} %get-tuple-element.29.refs_1_), channel_id=1, source_target_pairs={{0,4},{1,5},{2,6},{3,7},{4,0},{5,1},{6,2},{7,3},{8,12},{9,13},{10,... | collective-permute-start | bytes 540680 | tf_op jit(solution)/shard_map/ppermute | solution.py:399
  31.7 11.3 %collective-permute-start.6 = (f32[3,464,256]{2,1,0:T(8,128)S(1)}, f32[3,464,256]{2,1,0:T(8,128)S(1)}, u32[]{:S(2)}, u32[]{:S(2)}) collective-permute-start(f32[3,464,256]{2,1,0:T(8,128)S(1)} %get-tuple-element.32.join_ref), channel_id=1, source_target_pairs={{0,1},{1,0},{2,3},{3,2},{4,5},{5,4},{6,7},{7,6},{8,9},{9,8},{10,11... | collective-permute-start | bytes 4276232 | tf_op jit(solution)/shard_map/ppermute | solution.py:399
  31.8 9.4 %collective-permute-start.4 = (f32[288,256]{1,0:T(8,128)S(1)}, f32[288,256]{1,0:T(8,128)S(1)}, u32[]{:S(2)}, u32[]{:S(2)}) collective-permute-start(f32[288,256]{1,0:T(8,128)S(1)} %collective-permute-done.2.refs_4_), channel_id=1, source_target_pairs={{0,2},{1,3},{2,0},{3,1},{4,6},{5,7},{6,4},{7,5},{8,10},{9,11},{10,... | collective-permute-start | bytes 884744 | tf_op jit(solution)/shard_map/ppermute | solution.py:399
  33.3 6.6 %collective-permute-start.5 = (f32[176,256]{1,0:T(8,128)S(1)}, f32[176,256]{1,0:T(8,128)S(1)}, u32[]{:S(2)}, u32[]{:S(2)}) collective-permute-start(f32[176,256]{1,0:T(8,128)S(1)} %collective-permute-done.1.refs_3_), channel_id=1, source_target_pairs={{0,4},{1,5},{2,6},{3,7},{4,0},{5,1},{6,2},{7,3},{8,12},{9,13},{10,... | collective-permute-start | bytes 540680 | tf_op jit(solution)/shard_map/ppermute | solution.py:399
  41.2 1.8 %collective-permute-start.7 = (f32[288,256]{1,0:T(8,128)S(1)}, f32[288,256]{1,0:T(8,128)S(1)}, u32[]{:S(2)}, u32[]{:S(2)}) collective-permute-start(f32[288,256]{1,0:T(8,128)S(1)} %collective-permute-done.4.refs_0_), channel_id=1, source_target_pairs={{0,1},{1,0},{2,3},{3,2},{4,5},{5,4},{6,7},{7,6},{8,9},{9,8},{10,11... | collective-permute-start | bytes 884744 | tf_op jit(solution)/shard_map/ppermute | solution.py:399
  41.2 1.8 %collective-permute-start.8 = (f32[176,256]{1,0:T(8,128)S(1)}, f32[176,256]{1,0:T(8,128)S(1)}, u32[]{:S(2)}, u32[]{:S(2)}) collective-permute-start(f32[176,256]{1,0:T(8,128)S(1)} %collective-permute-done.5.refs_1_), channel_id=1, source_target_pairs={{0,1},{1,0},{2,3},{3,2},{4,5},{5,4},{6,7},{7,6},{8,9},{9,8},{10,11... | collective-permute-start | bytes 540680 | tf_op jit(solution)/shard_map/ppermute | solution.py:399
  46.0 1.3 %collective-permute-start.9 = (f32[10,16,128]{2,1,0:T(8,128)S(1)}, f32[10,16,128]{2,1,0:T(8,128)S(1)}, u32[]{:S(2)}, u32[]{:S(2)}) collective-permute-start(f32[10,16,128]{2,1,0:T(8,128)S(1)} %get-tuple-element.42), channel_id=1, source_target_pairs={{0,1},{1,0},{2,3},{3,2},{4,5},{5,4},{6,7},{7,6},{8,9},{9,8},{10,11... | collective-permute-start | bytes 245768 | tf_op jit(solution)/shard_map/ppermute | solution.py:399
  47.4 4.6 %collective-permute-start.10 = (f32[10,16,128]{2,1,0:T(8,128)S(1)}, f32[10,16,128]{2,1,0:T(8,128)S(1)}, u32[]{:S(2)}, u32[]{:S(2)}) collective-permute-start(f32[10,16,128]{2,1,0:T(8,128)S(1)} %add.3.own_ref), channel_id=1, source_target_pairs={{0,2},{1,3},{2,0},{3,1},{4,6},{5,7},{6,4},{7,5},{8,10},{9,11},{10,... | collective-permute-start | bytes 245768 | tf_op jit(solution)/shard_map/ppermute | solution.py:399
  48.9 5.1 %collective-permute-start.11 = (f32[10,16,128]{2,1,0:T(8,128)S(1)}, f32[10,16,128]{2,1,0:T(8,128)S(1)}, u32[]{:S(2)}, u32[]{:S(2)}) collective-permute-start(f32[10,16,128]{2,1,0:T(8,128)S(1)} %add.3.own_ref), channel_id=1, source_target_pairs={{0,4},{1,5},{2,6},{3,7},{4,0},{5,1},{6,2},{7,3},{8,12},{9,13},{10,... | collective-permute-start | bytes 245768 | tf_op jit(solution)/shard_map/ppermute | solution.py:399
  49.5 5.6 %collective-permute-start.12 = (f32[10,16,128]{2,1,0:T(8,128)S(1)}, f32[10,16,128]{2,1,0:T(8,128)S(1)}, u32[]{:S(2)}, u32[]{:S(2)}) collective-permute-start(f32[10,16,128]{2,1,0:T(8,128)S(1)} %add.3.own_ref), channel_id=1, source_target_pairs={{0,6},{1,7},{2,4},{3,5},{4,2},{5,3},{6,0},{7,1},{8,14},{9,15},{10,... | collective-permute-start | bytes 245768 | tf_op jit(solution)/shard_map/ppermute | solution.py:399
  55.1 8.4 %copy-start.2 = (f32[59392]{0:T(1024)S(1)}, f32[59392]{0:T(1024)}, u32[]{:S(2)}) copy-start(f32[59392]{0:T(1024)} %param.6) | copy-start | bytes 712708
  55.1 8.4 %copy-start.3 = (f32[59392]{0:T(1024)S(1)}, f32[59392]{0:T(1024)}, u32[]{:S(2)}) copy-start(f32[59392]{0:T(1024)} %param.7) | copy-start | bytes 712708
  55.1 8.4 %copy-start.4 = (f32[1,59392]{1,0:T(1,128)S(1)}, f32[1,59392]{1,0:T(1,128)}, u32[]{:S(2)}) copy-start(f32[1,59392]{1,0:T(1,128)} %param.8) | copy-start | bytes 712708
  58.8 18.9 %all-to-all-start.1 = ((f32[16,32,256]{2,1,0:T(8,128)}), f32[16,32,256]{2,1,0:T(8,128)S(1)}, u32[]{:S(2)}, u32[]{:S(2)}) async-start(f32[16,32,256]{2,1,0:T(8,128)} %bitcast.6), calls=%async_computation.1 | async-start | bytes 1048576 | tf_op jit(solution)/shard_map/all_to_all | solution.py:470

commit v2 on v1

--- a/solution.py
+++ b/solution.py
@@ -12,7 +12,7 @@
 H = 2048
 OUT = 10
 LANES = 128
-SHARE = 0.62
+SHARE = 0.72
 COPIES = 2
 
 step_size = 0.02
@@ -32,9 +32,10 @@
         self.cols = H // self.group
         self.nb = self.cols // LANES
         self.rows = shard_len // H
-        self.pad = up8(self.rows + 1)
+        self.unit = self.rows * self.nb
+        self.back = self.unit + self.nb
         self.step = H // LANES
-        self.early, self.rest = (0, 2, 4), (1, 3, 5, 6, 7)
+        self.early, self.middle, self.rest = (0, 2), (1, 3, 4), (5, 6, 7)
         self.flat = shard_len // LANES
         self.batch = batch
         self.tail = din + 1 - (devices - 1) * self.rows
@@ -100,24 +101,23 @@
 
 
 def cut_weights(plan, last_ref, par_ref, out_ref):
-    out_ref[...] = jnp.zeros_like(out_ref)
     for j in range(plan.group):
         for b in range(plan.nb):
             piece = par_ref[pl.ds(j * plan.nb + b, plan.rows, stride=plan.step), :]
             for d in range(j, plan.n, plan.group):
-                out_ref[d, : plan.rows, b * LANES : (b + 1) * LANES] = piece
+                out_ref[pl.ds(d * plan.unit + b, plan.rows, stride=plan.nb), :] = piece
 
     @pl.when(last_ref[0] == 1)
     def _():
-        t = plan.tail
+        t, count = plan.tail, OUT * plan.nb
+        bias = par_ref[(t + OUT) * plan.step : (t + OUT) * plan.step + 1, :]
         for j in range(plan.group):
+            start = t * plan.step + j * count
+            piece = par_ref[start : start + count, :]
             for d in range(j, plan.n, plan.group):
-                out_ref[d, t + OUT, :LANES] = par_ref[(t + OUT) * plan.step, :]
-            for b in range(plan.nb):
-                start = t * plan.step + j * plan.nb * OUT + b
-                piece = par_ref[pl.ds(start, OUT, stride=plan.nb), :]
-                for d in range(j, plan.n, plan.group):
-                    out_ref[d, t : t + OUT, b * LANES : (b + 1) * LANES] = piece
+                at = d * plan.unit + t * plan.nb
+                out_ref[at : at + count, :] = piece
+                out_ref[at + count : at + count + 1, :] = bias
 
 
 def class_masks(plan):
@@ -125,12 +125,6 @@
     mask = (iota((plan.classes, width), 1) % OUT == iota((plan.classes, width), 0)).astype(F32)
     place = (iota((width, plan.hp), 0) // OUT == iota((width, plan.hp), 1)).astype(BF16)
     return mask, place
-
-
-def flat_spot(plan, r):
-    row = (plan.n - 1) * plan.pad + plan.tail + r // plan.nb
-    col = r % plan.nb * LANES
-    return row, col
 
 
 def blocks_of(plan):
@@ -143,8 +137,8 @@
     for p in range(plan.periods):
         parts = []
         for q in range(plan.qp):
-            row, col = flat_spot(plan, p * plan.qp + q)
-            parts.append(jnp.broadcast_to(w_ref[row : row + 1, col : col + LANES], (plan.classes, LANES)))
+            row = (plan.n - 1) * plan.unit + plan.tail * plan.nb + p * plan.qp + q
+            parts.append(jnp.broadcast_to(w_ref[row : row + 1, :], (plan.classes, LANES)))
         lhs.append(jnp.concatenate(parts, axis=1) * mask)
     hi, mid, lo = split3(jnp.concatenate(lhs, axis=0))
     out_w = dot(hi, place, NN) + dot(mid, place, NN) + dot(lo, place, NN)
@@ -201,7 +195,9 @@
     a_cat = jnp.concatenate(split(a_ref[...]), axis=0)
     c_ref[...] = jnp.zeros_like(c_ref)
     for d, first, rows in blocks_of(plan):
-        c_ref[first : first + rows, :] = w_ref[d * plan.pad : d * plan.pad + rows, :]
+        for b in range(plan.nb):
+            piece = w_ref[pl.ds(d * plan.unit + b, rows, stride=plan.nb), :]
+            c_ref[first : first + rows, b * LANES : (b + 1) * LANES] = piece
     w_cat = jnp.concatenate(split(c_ref[...].T), axis=0)
     cat_ref[...] = w_cat
     own_ref[...] = jnp.zeros_like(own_ref)
@@ -214,37 +210,37 @@
         forward_slot(plan, m, x, w_cat, a_cat, h_ref, here, own_ref, send_ref)
 
 
-def rest_kernel(plan, cat_ref, a_ref, own1_ref, send1_ref, lab1_ref, join_ref, *refs):
+def later_kernel(plan, slots, joined, cat_ref, a_ref, own1_ref, send1_ref, lab1_ref, *refs):
     x_ref, h_ref, own_ref, send_ref, lab_ref = refs[-5:]
     own_ref[...] = own1_ref[...]
     send_ref[...] = send1_ref[...]
     lab_ref[...] = lab1_ref[...]
     w_cat = cat_ref[...]
     a_cat = jnp.concatenate(split(a_ref[...]), axis=0)
-    mark, joined = plan.parts[1].start, len(plan.early)
-    for s, m in enumerate(plan.rest):
+    pairs = refs[min(joined, 1) : -5]
+    for s, m in enumerate(slots):
         here = slice(s * plan.batch, (s + 1) * plan.batch)
         if s < joined:
-            keep_labels(plan, m, join_ref.at[s, mark:, :], lab_ref)
-            x = split(join_ref[s])
+            keep_labels(plan, m, refs[0].at[s, plan.parts[1].start :, :], lab_ref)
+            x = split(refs[0][s])
             x_ref[: plan.xrows, here] = x[0]
             x_ref[plan.xrows :, here] = x[1]
         else:
-            pair = refs[2 * (s - joined) :][:2]
+            pair = pairs[2 * (s - joined) :][:2]
             keep_labels(plan, m, pair[1], lab_ref)
             split_rows(plan, pair, x_ref, here)
             x = x_ref[: plan.xrows, here], x_ref[plan.xrows :, here]
         forward_slot(plan, m, x, w_cat, a_cat, h_ref, here, own_ref, send_ref)
 
 
-def backward_kernel(plan, own_ref, w_ref, a_ref, x1_ref, x2_ref, h1_ref, h2_ref, lab_ref, *refs):
+def backward_kernel(plan, own_ref, w_ref, a_ref, x1_ref, x2_ref, x3_ref, h1_ref, h2_ref, h3_ref, lab_ref, *refs):
     lg_refs, (out_ref, lg_ref, dl_ref, dh_ref, dw_ref) = refs[:-5], refs[-5:]
     per = plan.batch // LANES
     lines = plan.group * per
-    order = (*plan.early, *plan.rest)
+    order = (*plan.early, *plan.middle, *plan.rest)
     diag = iota((plan.classes, LANES), 0) == iota((plan.classes, LANES), 1)
-    row = (plan.n - 1) * plan.pad + plan.tail + OUT
-    bias = w_ref[row : row + 1, :LANES]
+    row = (plan.n - 1) * plan.unit + (plan.tail + OUT) * plan.nb
+    bias = w_ref[row : row + 1, :]
     for m in range(plan.group):
         value = own_ref[:, m * per : (m + 1) * per, :]
         for i, ref in enumerate(lg_refs):
@@ -276,7 +272,7 @@
     a_three = jnp.concatenate([v.astype(F32) for v in (a_hi, a_lo, a_hi)], axis=0).T.astype(BF16)
     cols, xrows, classes = plan.cols, plan.xrows, plan.classes
     da, start = 0.0, 0
-    for h_ref in (h1_ref, h2_ref):
+    for h_ref in (h1_ref, h2_ref, h3_ref):
         width = h_ref.shape[1]
         for at in range(0, width, plan.batch):
             here = slice(start + at, start + at + plan.batch)
@@ -291,7 +287,7 @@
     da = da.T
     da = da[:classes, :cols] + (da[classes:, :cols] + da[:classes, cols:])
     dw, start = 0.0, 0
-    for x_ref in (x1_ref, x2_ref):
+    for x_ref in (x1_ref, x2_ref, x3_ref):
         here = slice(start, start + x_ref.shape[1])
         part = dot(x_ref[...], dh_ref[:cols, here], NT)
         dw = dw + (part[:xrows] + (part[xrows:] + dot(x_ref[:xrows, :], dh_ref[cols:, here], NT)))
@@ -299,7 +295,9 @@
     dw_ref[...] = dw
     out_ref[...] = jnp.zeros_like(out_ref)
     for d, first, count in blocks_of(plan):
-        out_ref[d * plan.pad : d * plan.pad + count, :] = dw_ref[first : first + count, :]
+        for b in range(plan.nb):
+            piece = dw_ref[first : first + count, b * LANES : (b + 1) * LANES]
+            out_ref[pl.ds(d * plan.back + b, count, stride=plan.nb), :] = piece
     mask, place = class_masks(plan)
     hi, mid, lo = split3(da)
     parts = []
@@ -309,12 +307,13 @@
     for p in range(plan.periods):
         line = jnp.sum(back[p * plan.classes : (p + 1) * plan.classes] * mask, axis=0, keepdims=True)
         for q in range(plan.qp):
-            r, c = flat_spot(plan, p * plan.qp + q)
-            out_ref[r : r + 1, c : c + LANES] = line[:, q * LANES : (q + 1) * LANES]
-    out_ref[row : row + 1, :LANES] = dbias
+            r = (plan.n - 1) * plan.back + plan.tail * plan.nb + p * plan.qp + q
+            out_ref[r : r + 1, :] = line[:, q * LANES : (q + 1) * LANES]
+    row = (plan.n - 1) * plan.back + (plan.tail + OUT) * plan.nb
+    out_ref[row : row + 1, :] = dbias
     for d in range(plan.n):
-        at = d * plan.pad + plan.rows
-        out_ref[at : at + 1, :LANES] = jnp.broadcast_to(nll, (1, LANES))
+        at = d * plan.back + plan.unit
+        out_ref[at : at + 1, :] = jnp.broadcast_to(nll, (1, LANES))
 
 
 def prepare_kernel(plan, at_ref, par_ref, mom_ref, noise_ref, base_ref, keep_ref, mom, noise, sems):
@@ -332,29 +331,28 @@
 
 
 def update_kernel(plan, scale, count, at_ref, got_ref, base_ref, par_ref, par_out, mom_out, loss_ref, grad_ref):
-    t = plan.tail
-    pieces = []
+    def summed(j, start, size, stride=1):
+        total = 0.0
+        for g in range(COPIES):
+            at = (g * plan.group + j) * plan.back + start
+            total = total + got_ref[pl.ds(at, size, stride=stride), :]
+        return total
+
     for j in range(plan.group):
-        piece = got_ref[j * plan.pad : (j + 1) * plan.pad, :]
-        for g in range(1, COPIES):
-            at = (g * plan.group + j) * plan.pad
-            piece = piece + got_ref[at : at + plan.pad, :]
-        pieces.append(piece)
         for b in range(plan.nb):
-            lanes = slice(b * LANES, (b + 1) * LANES)
-            grad_ref[pl.ds(j * plan.nb + b, plan.rows, stride=plan.step), :] = piece[: plan.rows, lanes]
-    loss_ref[...] = pieces[0][plan.rows : plan.rows + 1, :LANES] * (1.0 / count)
+            spot = pl.ds(j * plan.nb + b, plan.rows, stride=plan.step)
+            grad_ref[spot, :] = summed(j, b, plan.rows, plan.nb)
+    loss_ref[...] = summed(0, plan.unit, 1) * (1.0 / count)
 
     @pl.when(at_ref[1] == 1)
     def _():
+        t, size = plan.tail, OUT * plan.nb
         row = (t + OUT) * plan.step
         grad_ref[row:, :] = jnp.zeros((plan.flat - row, LANES), F32)
-        grad_ref[row : row + 1, :] = pieces[0][t + OUT : t + OUT + 1, :LANES]
+        grad_ref[row : row + 1, :] = summed(0, (t + OUT) * plan.nb, 1)
         for j in range(plan.group):
-            for b in range(plan.nb):
-                lanes = slice(b * LANES, (b + 1) * LANES)
-                start = t * plan.step + j * plan.nb * OUT + b
-                grad_ref[pl.ds(start, OUT, stride=plan.nb), :] = pieces[j][t : t + OUT, lanes]
+            at = t * plan.step + j * size
+            grad_ref[at : at + size, :] = summed(j, t * plan.nb, size)
 
     mom = base_ref[...] - (step_size * scale) * grad_ref[...]
     mom_out[...] = mom
@@ -391,7 +389,11 @@
     me = lax.axis_index("dp")
     last = (me == n - 1).astype(jnp.int32)
     flat = (plan.flat, LANES)
-    tall = (n * plan.pad, plan.cols)
+
+    def exchange(x):
+        x = x.reshape(n, -1, plan.nb, LANES)
+        return lax.all_to_all(x, "dp", 0, 0, tiled=True).reshape(-1, LANES)
+
     total = plan.group * plan.batch
     dense = (OUT, total // LANES, LANES)
 
@@ -414,14 +416,14 @@
     (cut,) = call(
         functools.partial(cut_kernel, plan),
         (last.reshape(1), params.reshape(flat)),
-        [((n, plan.pad, plan.cols), F32)],
+        [((n * plan.unit, LANES), F32)],
         smem=1,
     )
-    weights = lax.all_to_all(cut.reshape(tall), "dp", 0, 0, tiled=True)
+    weights = exchange(cut)
     half = len(plan.early) * plan.batch
     join, marks = call(
         functools.partial(ready_kernel, plan),
-        (a, b, a2, b2, a4, b4),
+        (a, b, a2, b2),
         [((len(plan.early), plan.xrows, plan.batch), F32), (dense[1:], F32)],
     )
     weights, join = lax.optimization_barrier((weights, join))
@@ -440,25 +442,33 @@
         [pltpu.VMEM((plan.xrows, plan.cols), F32)],
         cost=3,
     )
+
+    def later(slots, joined, *args):
+        width = len(slots) * plan.batch
+        return call(
+            functools.partial(later_kernel, plan, slots, joined),
+            (cat, outw, own, send, marks, *args),
+            [
+                ((2 * plan.xrows, width), BF16),
+                ((2 * plan.cols, width), BF16),
+                (dense, F32),
+                (dense, F32),
+                (dense[1:], F32),
+            ],
+            cost=2,
+        )
+
+    a5, b5 = hop(a4, 1), hop(b4, 1)
     outw, a6, b6 = lax.optimization_barrier((outw, a6, b6))
-    x2, h2, own, send, marks = call(
-        functools.partial(rest_kernel, plan),
-        (cat, outw, own, send, marks, other, a6, b6, hop(a6, 1), hop(b6, 1)),
-        [
-            ((2 * plan.xrows, total - half), BF16),
-            ((2 * plan.cols, total - half), BF16),
-            (dense, F32),
-            (dense, F32),
-            (dense[1:], F32),
-        ],
-        cost=3,
-    )
+    a7, b7 = hop(a6, 1), hop(b6, 1)
+    x2, h2, own, send, marks = later(plan.middle, len(plan.early), other, a4, b4)
+    x3, h3, own, send, marks = later(plan.rest, 0, a5, b5, a6, b6, a7, b7)
     own = own + hop(send, 1)
     more = [hop(own, k) for k in range(2, plan.group, 2)]
     (grads,) = call(
         functools.partial(backward_kernel, plan),
-        (own, weights, outw, x1, x2, h1, h2, marks, *more),
-        [(tall, F32)],
+        (own, weights, outw, x1, x2, x3, h1, h2, h3, marks, *more),
+        [((n * plan.back, LANES), F32)],
         [
             pltpu.VMEM(dense, F32),
             pltpu.VMEM((plan.classes, total), F32),
@@ -467,7 +477,7 @@
         ],
         cost=4,
     )
-    got = lax.all_to_all(grads, "dp", 0, 0, tiled=True)
+    got = exchange(grads)
     scale = pool / plan.batch
     count = n * plan.batch
     spot = jnp.stack([me * params.shape[0], last])

time: 79.5 us -> 91.5 us (1.15)
  waiting for transfers between devices: 41.6 us -> 52.5 us
    ppermute x13 -> x15, waiting for transfers between devices: 29 us -> 40.5 us  [hop(): return lax.ppermute(x, 'dp', [(d, d ^ k) for d in range(n)])]
    ppermute x13 -> x15, starting transfers between devices: 10.5 us -> 11.3 us  [hop(): return lax.ppermute(x, 'dp', [(d, d ^ k) for d in range(n)])]
    pallas_call x8 -> x9, Pallas kernels: 13.2 us -> 13.4 us  [call(): pl.pallas_call(kernel, out_shape=[jax.ShapeDtypeStruct(s, t) for s, t in...]
  transfers between devices with their start and end apart: 15 -> 17, of which waited for: 10 -> 10; matrix products, arithmetic and copies ran while one was open for 0% -> 0% of each run, Pallas kernels for 5% -> 6%
where the time goes in v2:
time: 91.5 us; the launch traced here: 91.1 us
  waiting for transfers between devices  52.5 us (57%)
  starting transfers between devices  23.4 us (26%)
  Pallas kernels  13.4 us (15%)
  local copies, waits for them, and re-layouts  0.96 us (1%)
    ppermute x15, waiting for transfers between devices, hop(): return lax.ppermute(x, 'dp', [(d, d ^ k) for d in range(n)])  40.5 us
    pallas_call x9, Pallas kernels, call(): pl.pallas_call(kernel, out_shape=[jax.ShapeDtypeStruct(s, t) for s, t in...  13.4 us
    all_to_all x2, starting transfers between devices, exchange(): return lax.all_to_all(x, 'dp', 0, 0, tiled=True).reshape(-1, LANES)  12 us
    all_to_all x2, waiting for transfers between devices, exchange(): return lax.all_to_all(x, 'dp', 0, 0, tiled=True).reshape(-1, LANES)  12 us
    ppermute x15, starting transfers between devices, hop(): return lax.ppermute(x, 'dp', [(d, d ^ k) for d in range(n)])  11.3 us
  transfers between devices with their start and end apart: 17, of which 10 were waited for; matrix products, arithmetic and copies ran while one was open for 0% of the time, Pallas kernels for 6%

profile of v2, /device:TPU:0, one launch (start us, length us, event | category | flops | bytes accessed | tf_op | source)
XLA Modules:
  0.0 91.1 jit_solution(7893994611469020817)
XLA Ops:
  0.6 0.9 %copy-done.1 = f32[59392]{0:T(1024)S(1)} copy-done((f32[59392]{0:T(1024)S(1)}, f32[59392]{0:T(1024)}, u32[]{:S(2)}) %copy-start.1) | copy-done | bytes 237592
  2.5 7.4 %all-to-all-start = ((f32[16,29,2,128]{3,2,1,0:T(2,128)}), f32[16,29,2,128]{3,2,1,0:T(2,128)S(1)}, u32[]{:S(2)}, u32[]{:S(2)}) async-start(f32[16,29,2,128]{3,2,1,0:T(2,128)} %bitcast.3), calls=%async_computation | async-start | bytes 950272 | tf_op jit(solution)/shard_map/all_to_all | solution.py:395
  10.5 2.0 %collective-permute-start = (f32[336,256]{1,0:T(8,128)S(1)}, f32[336,256]{1,0:T(8,128)S(1)}, u32[]{:S(2)}, u32[]{:S(2)}) collective-permute-start(f32[336,256]{1,0:T(8,128)S(1)} %get-tuple-element.33.refs_0_), channel_id=1, source_target_pairs={{0,2},{1,3},{2,0},{3,1},{4,6},{5,7},{6,4},{7,5},{8,10},{9,11},{10,... | collective-permute-start | bytes 1032200 | tf_op jit(solution)/shard_map/ppermute | solution.py:401
  12.6 15.7 %collective-permute-done.1.refs_3_ = f32[128,256]{1,0:T(8,128)S(1)} collective-permute-done((f32[128,256]{1,0:T(8,128)S(1)}, f32[128,256]{1,0:T(8,128)S(1)}, u32[]{:S(2)}, u32[]{:S(2)}) %collective-permute-start.1) | collective-permute-done | bytes 131104 | tf_op jit(solution)/shard_map/ppermute | solution.py:401
  28.4 1.5 %collective-permute-start.2 = (f32[336,256]{1,0:T(8,128)S(1)}, f32[336,256]{1,0:T(8,128)S(1)}, u32[]{:S(2)}, u32[]{:S(2)}) collective-permute-start(f32[336,256]{1,0:T(8,128)S(1)} %get-tuple-element.33.refs_0_), channel_id=1, source_target_pairs={{0,4},{1,5},{2,6},{3,7},{4,0},{5,1},{6,2},{7,3},{8,12},{9,13},{10,... | collective-permute-start | bytes 1032200 | tf_op jit(solution)/shard_map/ppermute | solution.py:401
  29.9 8.9 %collective-permute-done.2.refs_1_ = f32[336,256]{1,0:T(8,128)S(1)} collective-permute-done((f32[336,256]{1,0:T(8,128)S(1)}, f32[336,256]{1,0:T(8,128)S(1)}, u32[]{:S(2)}, u32[]{:S(2)}) %collective-permute-start.2) | collective-permute-done | bytes 344096 | tf_op jit(solution)/shard_map/ppermute | solution.py:401
  39.5 1.4 %collective-permute-start.4 = (f32[128,256]{1,0:T(8,128)S(1)}, f32[128,256]{1,0:T(8,128)S(1)}, u32[]{:S(2)}, u32[]{:S(2)}) collective-permute-start(f32[128,256]{1,0:T(8,128)S(1)} %collective-permute-done.1.refs_3_), channel_id=1, source_target_pairs={{0,4},{1,5},{2,6},{3,7},{4,0},{5,1},{6,2},{7,3},{8,12},{9,13},{10,... | collective-permute-start | bytes 393224 | tf_op jit(solution)/shard_map/ppermute | solution.py:401
  40.9 1.5 %shard_map.88 = (bf16[928,512]{1,0:T(8,128)(2,1)S(1)}, bf16[512,512]{1,0:T(8,128)(2,1)S(1)}, f32[16,256]{1,0:T(8,128)S(1)}, bf16[512,464]{1,0:T(8,128)(2,1)S(1)}...) custom-call(f32[928,128]{1,0:T(8,128)S(1)} %bitcast.16, f32[2,464,256]{2,1,0:T(8,128)S(1)} %get-tuple-element.37.join_ref), custom_call_target="tpu_custom_call" | custom-call | flops 3000000000 | bytes 1048576 | tf_op jit(solution)/shard_map/pallas_call | solution.py:375
  42.4 2.0 %collective-permute-done.4.refs_3_ = f32[128,256]{1,0:T(8,128)S(1)} collective-permute-done((f32[128,256]{1,0:T(8,128)S(1)}, f32[128,256]{1,0:T(8,128)S(1)}, u32[]{:S(2)}, u32[]{:S(2)}) %collective-permute-start.4) | collective-permute-done | bytes 131104 | tf_op jit(solution)/shard_map/ppermute | solution.py:401
  44.5 3.9 %collective-permute-done.3.refs_2_ = f32[336,256]{1,0:T(8,128)S(1)} collective-permute-done((f32[336,256]{1,0:T(8,128)S(1)}, f32[336,256]{1,0:T(8,128)S(1)}, u32[]{:S(2)}, u32[]{:S(2)}) %collective-permute-start.3) | collective-permute-done | bytes 344096 | tf_op jit(solution)/shard_map/ppermute | solution.py:401
  48.4 1.5 %collective-permute-start.6 = (f32[128,256]{1,0:T(8,128)S(1)}, f32[128,256]{1,0:T(8,128)S(1)}, u32[]{:S(2)}, u32[]{:S(2)}) collective-permute-start(f32[128,256]{1,0:T(8,128)S(1)} %get-tuple-element.34.refs_1_), channel_id=1, source_target_pairs={{0,4},{1,5},{2,6},{3,7},{4,0},{5,1},{6,2},{7,3},{8,12},{9,13},{10,... | collective-permute-start | bytes 393224 | tf_op jit(solution)/shard_map/ppermute | solution.py:401
  49.9 4.4 %collective-permute-done.6.refs_2_ = f32[128,256]{1,0:T(8,128)S(1)} collective-permute-done((f32[128,256]{1,0:T(8,128)S(1)}, f32[128,256]{1,0:T(8,128)S(1)}, u32[]{:S(2)}, u32[]{:S(2)}) %collective-permute-start.6) | collective-permute-done | bytes 131104 | tf_op jit(solution)/shard_map/ppermute | solution.py:401
  54.8 1.8 %shard_map.89 = (bf16[928,768]{1,0:T(8,128)(2,1)S(1)}, bf16[512,768]{1,0:T(8,128)(2,1)S(1)}, f32[10,16,128]{2,1,0:T(8,128)S(1)}, f32[10,16,128]{2,1,0:T(8,128)S(1)}, f32[16,128]{1,0:T(8,128)S(1)}) custom-call(bf16[512,464]{1,0:T(8,128)(2,1)S(1)} %get-tuple-element.38.cat_ref, f32[16,256]{1,0:T(8,128)S(1)} %get-tuple-element.40.a_ref, ...), custom_call_target="tpu_custom_call" | custom-call | flops 2000000000 | bytes 1048576 | tf_op jit(solution)/shard_map/pallas_call | solution.py:375
  56.6 1.8 %shard_map.90 = (bf16[928,768]{1,0:T(8,128)(2,1)S(1)}, bf16[512,768]{1,0:T(8,128)(2,1)S(1)}, f32[10,16,128]{2,1,0:T(8,128)S(1)}, f32[10,16,128]{2,1,0:T(8,128)S(1)}, f32[16,128]{1,0:T(8,128)S(1)}) custom-call(bf16[512,464]{1,0:T(8,128)(2,1)S(1)} %get-tuple-element.38.cat_ref, f32[16,256]{1,0:T(8,128)S(1)} %get-tuple-element.40.a_ref, ...), custom_call_target="tpu_custom_call" | custom-call | flops 2000000000 | bytes 1048576 | tf_op jit(solution)/shard_map/pallas_call | solution.py:375
  58.5 1.3 %collective-permute-done.11 = f32[10,16,128]{2,1,0:T(8,128)S(1)} collective-permute-done((f32[10,16,128]{2,1,0:T(8,128)S(1)}, f32[10,16,128]{2,1,0:T(8,128)S(1)}, u32[]{:S(2)}, u32[]{:S(2)}) %collective-permute-start.11) | collective-permute-done | bytes 81952 | tf_op jit(solution)/shard_map/ppermute | solution.py:401
  60.5 1.4 %collective-permute-start.13 = (f32[10,16,128]{2,1,0:T(8,128)S(1)}, f32[10,16,128]{2,1,0:T(8,128)S(1)}, u32[]{:S(2)}, u32[]{:S(2)}) collective-permute-start(f32[10,16,128]{2,1,0:T(8,128)S(1)} %add.3.own_ref), channel_id=1, source_target_pairs={{0,4},{1,5},{2,6},{3,7},{4,0},{5,1},{6,2},{7,3},{8,12},{9,13},{10,... | collective-permute-start | bytes 245768 | tf_op jit(solution)/shard_map/ppermute | solution.py:401
  61.9 1.5 %collective-permute-start.14 = (f32[10,16,128]{2,1,0:T(8,128)S(1)}, f32[10,16,128]{2,1,0:T(8,128)S(1)}, u32[]{:S(2)}, u32[]{:S(2)}) collective-permute-start(f32[10,16,128]{2,1,0:T(8,128)S(1)} %add.3.own_ref), channel_id=1, source_target_pairs={{0,6},{1,7},{2,4},{3,5},{4,2},{5,3},{6,0},{7,1},{8,14},{9,15},{10,... | collective-permute-start | bytes 245768 | tf_op jit(solution)/shard_map/ppermute | solution.py:401
  63.3 1.0 %collective-permute-done.12.refs_0_ = f32[10,16,128]{2,1,0:T(8,128)S(1)} collective-permute-done((f32[10,16,128]{2,1,0:T(8,128)S(1)}, f32[10,16,128]{2,1,0:T(8,128)S(1)}, u32[]{:S(2)}, u32[]{:S(2)}) %collective-permute-start.12) | collective-permute-done | bytes 81952 | tf_op jit(solution)/shard_map/ppermute | solution.py:401
  64.9 2.6 %collective-permute-done.14.refs_2_ = f32[10,16,128]{2,1,0:T(8,128)S(1)} collective-permute-done((f32[10,16,128]{2,1,0:T(8,128)S(1)}, f32[10,16,128]{2,1,0:T(8,128)S(1)}, u32[]{:S(2)}, u32[]{:S(2)}) %collective-permute-start.14) | collective-permute-done | bytes 81952 | tf_op jit(solution)/shard_map/ppermute | solution.py:401
  67.5 3.7 %shard_map.91 = f32[960,128]{1,0:T(8,128)} custom-call(f32[10,16,128]{2,1,0:T(8,128)S(1)} %add.3.own_ref, f32[928,128]{1,0:T(8,128)S(1)} %bitcast.17, f32[16,256]{1,0:T(8,128)S(1)} %get-tuple-element.40.a_ref, bf16[928,512]{1,0:T(8,128)(2,1)S(1)} %get-tuple-element.51.x1_ref, bf16[928,768]{1,0:T(8,128)(2,1)S(1)} %get-tuple-element.52.x2_ref, ...), custom_call_target="tpu_custom_call" | custom-call | flops 4000000000 | bytes 1048576 | tf_op jit(solution)/shard_map/pallas_call | solution.py:375
  71.2 4.6 %all-to-all-start.1 = ((f32[16,30,2,128]{3,2,1,0:T(2,128)}), f32[16,30,2,128]{3,2,1,0:T(2,128)S(1)}, u32[]{:S(2)}, u32[]{:S(2)}) async-start(f32[16,30,2,128]{3,2,1,0:T(2,128)} %bitcast.7), calls=%async_computation.1 | async-start | bytes 983040 | tf_op jit(solution)/shard_map/all_to_all | solution.py:395
  76.0 1.6 %shard_map.92 = (f32[464,128]{1,0:T(8,128)S(1)}, f32[464,128]{1,0:T(8,128)S(1)}) custom-call(s32[2]{0:T(128)S(1)} %pad_add_fusion.at_ref, f32[464,128]{1,0:T(8,128)S(1)} %bitcast.20, f32[464,128]{1,0:T(8,128)S(1)} %bitcast.21, f32[464,128]{1,0:T(8,128)S(1)} %bitcast.22), custom_call_target="tpu_custom_call" | custom-call | flops 1000000000 | bytes 1048576 | tf_op jit(solution)/shard_map/pallas_call | solution.py:375
  77.6 12.0 %all-to-all-done.1 = f32[16,30,2,128]{3,2,1,0:T(2,128)S(1)} async-done(((f32[16,30,2,128]{3,2,1,0:T(2,128)}), f32[16,30,2,128]{3,2,1,0:T(2,128)S(1)}, u32[]{:S(2)}, u32[]{:S(2)}) %all-to-all-start.1) | async-done | bytes 491552 | tf_op jit(solution)/shard_map/all_to_all | solution.py:395
  89.6 1.5 %shard_map.93 = (f32[464,128]{1,0:T(8,128)}, f32[464,128]{1,0:T(8,128)}, f32[1,128]{1,0:T(1,128)}) custom-call(s32[2]{0:T(128)S(1)} %pad_add_fusion.at_ref, f32[960,128]{1,0:T(8,128)S(1)} %bitcast.15, f32[464,128]{1,0:T(8,128)S(1)} %get-tuple-element.58.base_ref, f32[464,128]{1,0:T(8,128)S(1)} %get-tuple-element.59.par_ref), custom_call_target="tpu_custom_call" | custom-call | flops 1000000000 | bytes 1048576 | tf_op jit(solution)/shard_map/pallas_call | solution.py:375
  (36 shorter events, 4.3 us)
Async XLA Ops:
  0.6 0.9 %copy-start.1 = (f32[59392]{0:T(1024)S(1)}, f32[59392]{0:T(1024)}, u32[]{:S(2)}) copy-start(f32[59392]{0:T(1024)} %param.6) | copy-start | bytes 712708
  1.6 8.3 %copy-start.5 = (s32[512]{0:T(512)S(1)}, s32[512]{0:T(512)}, u32[]{:S(2)}) copy-start(s32[512]{0:T(512)} %param.10) | copy-start | bytes 6148
  1.6 8.3 %copy-start.6 = (s32[1,256]{1,0:T(1,128)S(1)}, s32[1,256]{1,0:T(1,128)}, u32[]{:S(2)}) copy-start(s32[1,256]{1,0:T(1,128)} %param.11) | copy-start | bytes 3076
  1.6 8.3 %copy-start = (f32[512,448]{0,1:T(8,128)S(1)}, f32[512,448]{0,1:T(8,128)}, u32[]{:S(2)}) copy-start(f32[512,448]{0,1:T(8,128)} %param.9) | copy-start | bytes 2752516
  2.5 25.8 %all-to-all-start = ((f32[16,29,2,128]{3,2,1,0:T(2,128)}), f32[16,29,2,128]{3,2,1,0:T(2,128)S(1)}, u32[]{:S(2)}, u32[]{:S(2)}) async-start(f32[16,29,2,128]{3,2,1,0:T(2,128)} %bitcast.3), calls=%async_computation | async-start | bytes 950272 | tf_op jit(solution)/shard_map/all_to_all | solution.py:395
  10.5 17.8 %collective-permute-start = (f32[336,256]{1,0:T(8,128)S(1)}, f32[336,256]{1,0:T(8,128)S(1)}, u32[]{:S(2)}, u32[]{:S(2)}) collective-permute-start(f32[336,256]{1,0:T(8,128)S(1)} %get-tuple-element.33.refs_0_), channel_id=1, source_target_pairs={{0,2},{1,3},{2,0},{3,1},{4,6},{5,7},{6,4},{7,5},{8,10},{9,11},{10,... | collective-permute-start | bytes 1032200 | tf_op jit(solution)/shard_map/ppermute | solution.py:401
  12.5 15.8 %collective-permute-start.1 = (f32[128,256]{1,0:T(8,128)S(1)}, f32[128,256]{1,0:T(8,128)S(1)}, u32[]{:S(2)}, u32[]{:S(2)}) collective-permute-start(f32[128,256]{1,0:T(8,128)S(1)} %get-tuple-element.34.refs_1_), channel_id=1, source_target_pairs={{0,2},{1,3},{2,0},{3,1},{4,6},{5,7},{6,4},{7,5},{8,10},{9,11},{10,... | collective-permute-start | bytes 393224 | tf_op jit(solution)/shard_map/ppermute | solution.py:401
  28.3 26.5 %collective-permute-start.5 = (f32[2,464,256]{2,1,0:T(8,128)S(1)}, f32[2,464,256]{2,1,0:T(8,128)S(1)}, u32[]{:S(2)}, u32[]{:S(2)}) collective-permute-start(f32[2,464,256]{2,1,0:T(8,128)S(1)} %get-tuple-element.37.join_ref), channel_id=1, source_target_pairs={{0,1},{1,0},{2,3},{3,2},{4,5},{5,4},{6,7},{7,6},{8,9},{9,8},{10,11... | collective-permute-start | bytes 2850824 | tf_op jit(solution)/shard_map/ppermute | solution.py:401
  28.4 10.5 %collective-permute-start.2 = (f32[336,256]{1,0:T(8,128)S(1)}, f32[336,256]{1,0:T(8,128)S(1)}, u32[]{:S(2)}, u32[]{:S(2)}) collective-permute-start(f32[336,256]{1,0:T(8,128)S(1)} %get-tuple-element.33.refs_0_), channel_id=1, source_target_pairs={{0,4},{1,5},{2,6},{3,7},{4,0},{5,1},{6,2},{7,3},{8,12},{9,13},{10,... | collective-permute-start | bytes 1032200 | tf_op jit(solution)/shard_map/ppermute | solution.py:401
  38.9 9.5 %collective-permute-start.3 = (f32[336,256]{1,0:T(8,128)S(1)}, f32[336,256]{1,0:T(8,128)S(1)}, u32[]{:S(2)}, u32[]{:S(2)}) collective-permute-start(f32[336,256]{1,0:T(8,128)S(1)} %collective-permute-done.2.refs_1_), channel_id=1, source_target_pairs={{0,2},{1,3},{2,0},{3,1},{4,6},{5,7},{6,4},{7,5},{8,10},{9,11},{10,... | collective-permute-start | bytes 1032200 | tf_op jit(solution)/shard_map/ppermute | solution.py:401
  39.5 5.0 %collective-permute-start.4 = (f32[128,256]{1,0:T(8,128)S(1)}, f32[128,256]{1,0:T(8,128)S(1)}, u32[]{:S(2)}, u32[]{:S(2)}) collective-permute-start(f32[128,256]{1,0:T(8,128)S(1)} %collective-permute-done.1.refs_3_), channel_id=1, source_target_pairs={{0,4},{1,5},{2,6},{3,7},{4,0},{5,1},{6,2},{7,3},{8,12},{9,13},{10,... | collective-permute-start | bytes 393224 | tf_op jit(solution)/shard_map/ppermute | solution.py:401
  40.9 15.7 %collective-permute-start.7 = (f32[336,256]{1,0:T(8,128)S(1)}, f32[336,256]{1,0:T(8,128)S(1)}, u32[]{:S(2)}, u32[]{:S(2)}) collective-permute-start(f32[336,256]{1,0:T(8,128)S(1)} %collective-permute-done.2.refs_1_), channel_id=1, source_target_pairs={{0,1},{1,0},{2,3},{3,2},{4,5},{5,4},{6,7},{7,6},{8,9},{9,8},{10,11... | collective-permute-start | bytes 1032200 | tf_op jit(solution)/shard_map/ppermute | solution.py:401
  48.4 8.2 %collective-permute-start.9 = (f32[336,256]{1,0:T(8,128)S(1)}, f32[336,256]{1,0:T(8,128)S(1)}, u32[]{:S(2)}, u32[]{:S(2)}) collective-permute-start(f32[336,256]{1,0:T(8,128)S(1)} %collective-permute-done.3.refs_2_), channel_id=1, source_target_pairs={{0,1},{1,0},{2,3},{3,2},{4,5},{5,4},{6,7},{7,6},{8,9},{9,8},{10,11... | collective-permute-start | bytes 1032200 | tf_op jit(solution)/shard_map/ppermute | solution.py:401
  48.4 5.9 %collective-permute-start.6 = (f32[128,256]{1,0:T(8,128)S(1)}, f32[128,256]{1,0:T(8,128)S(1)}, u32[]{:S(2)}, u32[]{:S(2)}) collective-permute-start(f32[128,256]{1,0:T(8,128)S(1)} %get-tuple-element.34.refs_1_), channel_id=1, source_target_pairs={{0,4},{1,5},{2,6},{3,7},{4,0},{5,1},{6,2},{7,3},{8,12},{9,13},{10,... | collective-permute-start | bytes 393224 | tf_op jit(solution)/shard_map/ppermute | solution.py:401
  54.3 2.3 %collective-permute-start.8 = (f32[128,256]{1,0:T(8,128)S(1)}, f32[128,256]{1,0:T(8,128)S(1)}, u32[]{:S(2)}, u32[]{:S(2)}) collective-permute-start(f32[128,256]{1,0:T(8,128)S(1)} %collective-permute-done.6.refs_2_), channel_id=1, source_target_pairs={{0,1},{1,0},{2,3},{3,2},{4,5},{5,4},{6,7},{7,6},{8,9},{9,8},{10,11... | collective-permute-start | bytes 393224 | tf_op jit(solution)/shard_map/ppermute | solution.py:401
  54.3 2.3 %collective-permute-start.10 = (f32[128,256]{1,0:T(8,128)S(1)}, f32[128,256]{1,0:T(8,128)S(1)}, u32[]{:S(2)}, u32[]{:S(2)}) collective-permute-start(f32[128,256]{1,0:T(8,128)S(1)} %collective-permute-done.4.refs_3_), channel_id=1, source_target_pairs={{0,1},{1,0},{2,3},{3,2},{4,5},{5,4},{6,7},{7,6},{8,9},{9,8},{10,11... | collective-permute-start | bytes 393224 | tf_op jit(solution)/shard_map/ppermute | solution.py:401
  58.4 1.3 %collective-permute-start.11 = (f32[10,16,128]{2,1,0:T(8,128)S(1)}, f32[10,16,128]{2,1,0:T(8,128)S(1)}, u32[]{:S(2)}, u32[]{:S(2)}) collective-permute-start(f32[10,16,128]{2,1,0:T(8,128)S(1)} %get-tuple-element.50), channel_id=1, source_target_pairs={{0,1},{1,0},{2,3},{3,2},{4,5},{5,4},{6,7},{7,6},{8,9},{9,8},{10,11... | collective-permute-start | bytes 245768 | tf_op jit(solution)/shard_map/ppermute | solution.py:401
  59.8 4.6 %collective-permute-start.12 = (f32[10,16,128]{2,1,0:T(8,128)S(1)}, f32[10,16,128]{2,1,0:T(8,128)S(1)}, u32[]{:S(2)}, u32[]{:S(2)}) collective-permute-start(f32[10,16,128]{2,1,0:T(8,128)S(1)} %add.3.own_ref), channel_id=1, source_target_pairs={{0,2},{1,3},{2,0},{3,1},{4,6},{5,7},{6,4},{7,5},{8,10},{9,11},{10,... | collective-permute-start | bytes 245768 | tf_op jit(solution)/shard_map/ppermute | solution.py:401
  60.5 4.4 %collective-permute-start.13 = (f32[10,16,128]{2,1,0:T(8,128)S(1)}, f32[10,16,128]{2,1,0:T(8,128)S(1)}, u32[]{:S(2)}, u32[]{:S(2)}) collective-permute-start(f32[10,16,128]{2,1,0:T(8,128)S(1)} %add.3.own_ref), channel_id=1, source_target_pairs={{0,4},{1,5},{2,6},{3,7},{4,0},{5,1},{6,2},{7,3},{8,12},{9,13},{10,... | collective-permute-start | bytes 245768 | tf_op jit(solution)/shard_map/ppermute | solution.py:401
  61.9 5.6 %collective-permute-start.14 = (f32[10,16,128]{2,1,0:T(8,128)S(1)}, f32[10,16,128]{2,1,0:T(8,128)S(1)}, u32[]{:S(2)}, u32[]{:S(2)}) collective-permute-start(f32[10,16,128]{2,1,0:T(8,128)S(1)} %add.3.own_ref), channel_id=1, source_target_pairs={{0,6},{1,7},{2,4},{3,5},{4,2},{5,3},{6,0},{7,1},{8,14},{9,15},{10,... | collective-permute-start | bytes 245768 | tf_op jit(solution)/shard_map/ppermute | solution.py:401
  67.5 8.4 %copy-start.2 = (f32[59392]{0:T(1024)S(1)}, f32[59392]{0:T(1024)}, u32[]{:S(2)}) copy-start(f32[59392]{0:T(1024)} %param.6) | copy-start | bytes 712708
  67.5 8.4 %copy-start.3 = (f32[59392]{0:T(1024)S(1)}, f32[59392]{0:T(1024)}, u32[]{:S(2)}) copy-start(f32[59392]{0:T(1024)} %param.7) | copy-start | bytes 712708
  67.5 8.4 %copy-start.4 = (f32[1,59392]{1,0:T(1,128)S(1)}, f32[1,59392]{1,0:T(1,128)}, u32[]{:S(2)}) copy-start(f32[1,59392]{1,0:T(1,128)} %param.8) | copy-start | bytes 712708
  71.2 18.4 %all-to-all-start.1 = ((f32[16,30,2,128]{3,2,1,0:T(2,128)}), f32[16,30,2,128]{3,2,1,0:T(2,128)S(1)}, u32[]{:S(2)}, u32[]{:S(2)}) async-start(f32[16,30,2,128]{3,2,1,0:T(2,128)} %bitcast.7), calls=%async_computation.1 | async-start | bytes 983040 | tf_op jit(solution)/shard_map/all_to_all | solution.py:395

commit v3 on v2

--- a/solution.py
+++ b/solution.py
@@ -162,22 +162,22 @@
         lab_ref[m * per + i : m * per + i + 1, :] = row
 
 
-def forward_slot(plan, m, x, w_cat, a_cat, h_ref, here, own_ref, send_ref):
+def forward_slots(plan, slots, x_ref, w_cat, a_cat, h_ref, own_ref, send_ref):
     per = plan.batch // LANES
-    x_hi, x_lo = x
-    pre = dot(w_cat, x_hi, NN)
-    hidden = jnp.tanh(pre[: plan.cols] + (pre[plan.cols :] + dot(w_cat[: plan.cols], x_lo, NN)))
-    h_hi, h_lo = split(hidden)
-    h_ref[: plan.cols, here] = h_hi
-    h_ref[plan.cols :, here] = h_lo
+    pre = dot(w_cat, x_ref[: plan.xrows, :], NN)
+    pre = pre[: plan.cols] + (pre[plan.cols :] + dot(w_cat[: plan.cols], x_ref[plan.xrows :, :], NN))
+    h_hi, h_lo = split(jnp.tanh(pre))
+    h_ref[: plan.cols, :] = h_hi
+    h_ref[plan.cols :, :] = h_lo
     lg = dot(a_cat, h_hi, NN)
     lg = lg[: plan.classes] + (lg[plan.classes :] + dot(a_cat[: plan.classes], h_lo, NN))
-    for i in range(per):
-        own, other = m * per + i, (m ^ 1) * per + i
-        for o in range(OUT):
-            row = lg[o : o + 1, i * LANES : (i + 1) * LANES]
-            own_ref[o, own : own + 1, :] = row
-            send_ref[o, other : other + 1, :] = row
+    for s, m in enumerate(slots):
+        for i in range(per):
+            own, other, at = m * per + i, (m ^ 1) * per + i, (s * per + i) * LANES
+            for o in range(OUT):
+                row = lg[o : o + 1, at : at + LANES]
+                own_ref[o, own : own + 1, :] = row
+                send_ref[o, other : other + 1, :] = row
 
 
 def ready_kernel(plan, *refs):
@@ -207,7 +207,7 @@
         x = split(join_ref[s])
         x_ref[: plan.xrows, here] = x[0]
         x_ref[plan.xrows :, here] = x[1]
-        forward_slot(plan, m, x, w_cat, a_cat, h_ref, here, own_ref, send_ref)
+    forward_slots(plan, plan.early, x_ref, w_cat, a_cat, h_ref, own_ref, send_ref)
 
 
 def later_kernel(plan, slots, joined, cat_ref, a_ref, own1_ref, send1_ref, lab1_ref, *refs):
@@ -229,8 +229,7 @@
             pair = pairs[2 * (s - joined) :][:2]
             keep_labels(plan, m, pair[1], lab_ref)
             split_rows(plan, pair, x_ref, here)
-            x = x_ref[: plan.xrows, here], x_ref[plan.xrows :, here]
-        forward_slot(plan, m, x, w_cat, a_cat, h_ref, here, own_ref, send_ref)
+    forward_slots(plan, slots, x_ref, w_cat, a_cat, h_ref, own_ref, send_ref)
 
 
 def backward_kernel(plan, own_ref, w_ref, a_ref, x1_ref, x2_ref, x3_ref, h1_ref, h2_ref, h3_ref, lab_ref, *refs):

time: 91.5 us -> 90.2 us (0.986)
  Pallas kernels: 13.4 us -> 11.5 us
    pallas_call x9, Pallas kernels: 13.4 us -> 11.5 us  [call(): pl.pallas_call(kernel, out_shape=[jax.ShapeDtypeStruct(s, t) for s, t in...]
  transfers between devices with their start and end apart: 17 -> 17, of which waited for: 10 -> 10; matrix products, arithmetic and copies ran while one was open for 0% -> 0% of each run, Pallas kernels for 6% -> 5%
where the time goes in v3:
time: 90.2 us; the launch traced here: 89.8 us
  waiting for transfers between devices  52.9 us (59%)
  starting transfers between devices  23.5 us (26%)
  Pallas kernels  11.5 us (13%)
  local copies, waits for them, and re-layouts  0.96 us (1%)
    ppermute x15, waiting for transfers between devices, hop(): return lax.ppermute(x, 'dp', [(d, d ^ k) for d in range(n)])  40.9 us
    all_to_all x2, starting transfers between devices, exchange(): return lax.all_to_all(x, 'dp', 0, 0, tiled=True).reshape(-1, LANES)  12 us
    all_to_all x2, waiting for transfers between devices, exchange(): return lax.all_to_all(x, 'dp', 0, 0, tiled=True).reshape(-1, LANES)  12 us
    pallas_call x9, Pallas kernels, call(): pl.pallas_call(kernel, out_shape=[jax.ShapeDtypeStruct(s, t) for s, t in...  11.5 us
    ppermute x15, starting transfers between devices, hop(): return lax.ppermute(x, 'dp', [(d, d ^ k) for d in range(n)])  11.5 us
  transfers between devices with their start and end apart: 17, of which 10 were waited for; matrix products, arithmetic and copies ran while one was open for 0% of the time, Pallas kernels for 5%

profile of v3, /device:TPU:0, one launch (start us, length us, event | category | flops | bytes accessed | tf_op | source)
XLA Modules:
  0.0 89.8 jit_solution(16591036795520977885)
XLA Ops:
  0.6 0.9 %copy-done.1 = f32[59392]{0:T(1024)S(1)} copy-done((f32[59392]{0:T(1024)S(1)}, f32[59392]{0:T(1024)}, u32[]{:S(2)}) %copy-start.1) | copy-done | bytes 237592
  2.5 7.4 %all-to-all-start = ((f32[16,29,2,128]{3,2,1,0:T(2,128)}), f32[16,29,2,128]{3,2,1,0:T(2,128)S(1)}, u32[]{:S(2)}, u32[]{:S(2)}) async-start(f32[16,29,2,128]{3,2,1,0:T(2,128)} %bitcast.3), calls=%async_computation | async-start | bytes 950272 | tf_op jit(solution)/shard_map/all_to_all | solution.py:394
  10.5 2.0 %collective-permute-start = (f32[336,256]{1,0:T(8,128)S(1)}, f32[336,256]{1,0:T(8,128)S(1)}, u32[]{:S(2)}, u32[]{:S(2)}) collective-permute-start(f32[336,256]{1,0:T(8,128)S(1)} %get-tuple-element.33.refs_0_), channel_id=1, source_target_pairs={{0,2},{1,3},{2,0},{3,1},{4,6},{5,7},{6,4},{7,5},{8,10},{9,11},{10,... | collective-permute-start | bytes 1032200 | tf_op jit(solution)/shard_map/ppermute | solution.py:400
  12.6 15.7 %collective-permute-done.1.refs_3_ = f32[128,256]{1,0:T(8,128)S(1)} collective-permute-done((f32[128,256]{1,0:T(8,128)S(1)}, f32[128,256]{1,0:T(8,128)S(1)}, u32[]{:S(2)}, u32[]{:S(2)}) %collective-permute-start.1) | collective-permute-done | bytes 131104 | tf_op jit(solution)/shard_map/ppermute | solution.py:400
  28.4 1.5 %collective-permute-start.2 = (f32[336,256]{1,0:T(8,128)S(1)}, f32[336,256]{1,0:T(8,128)S(1)}, u32[]{:S(2)}, u32[]{:S(2)}) collective-permute-start(f32[336,256]{1,0:T(8,128)S(1)} %get-tuple-element.33.refs_0_), channel_id=1, source_target_pairs={{0,4},{1,5},{2,6},{3,7},{4,0},{5,1},{6,2},{7,3},{8,12},{9,13},{10,... | collective-permute-start | bytes 1032200 | tf_op jit(solution)/shard_map/ppermute | solution.py:400
  29.9 8.9 %collective-permute-done.2.refs_1_ = f32[336,256]{1,0:T(8,128)S(1)} collective-permute-done((f32[336,256]{1,0:T(8,128)S(1)}, f32[336,256]{1,0:T(8,128)S(1)}, u32[]{:S(2)}, u32[]{:S(2)}) %collective-permute-start.2) | collective-permute-done | bytes 344096 | tf_op jit(solution)/shard_map/ppermute | solution.py:400
  39.5 1.4 %collective-permute-start.4 = (f32[128,256]{1,0:T(8,128)S(1)}, f32[128,256]{1,0:T(8,128)S(1)}, u32[]{:S(2)}, u32[]{:S(2)}) collective-permute-start(f32[128,256]{1,0:T(8,128)S(1)} %collective-permute-done.1.refs_3_), channel_id=1, source_target_pairs={{0,4},{1,5},{2,6},{3,7},{4,0},{5,1},{6,2},{7,3},{8,12},{9,13},{10,... | collective-permute-start | bytes 393224 | tf_op jit(solution)/shard_map/ppermute | solution.py:400
  40.9 0.9 %shard_map.88 = (bf16[928,512]{1,0:T(8,128)(2,1)S(1)}, bf16[512,512]{1,0:T(8,128)(2,1)S(1)}, f32[16,256]{1,0:T(8,128)S(1)}, bf16[512,464]{1,0:T(8,128)(2,1)S(1)}...) custom-call(f32[928,128]{1,0:T(8,128)S(1)} %bitcast.16, f32[2,464,256]{2,1,0:T(8,128)S(1)} %get-tuple-element.37.join_ref), custom_call_target="tpu_custom_call" | custom-call | flops 3000000000 | bytes 1048576 | tf_op jit(solution)/shard_map/pallas_call | solution.py:374
  41.8 2.6 %collective-permute-done.4.refs_3_ = f32[128,256]{1,0:T(8,128)S(1)} collective-permute-done((f32[128,256]{1,0:T(8,128)S(1)}, f32[128,256]{1,0:T(8,128)S(1)}, u32[]{:S(2)}, u32[]{:S(2)}) %collective-permute-start.4) | collective-permute-done | bytes 131104 | tf_op jit(solution)/shard_map/ppermute | solution.py:400
  44.5 3.9 %collective-permute-done.3.refs_2_ = f32[336,256]{1,0:T(8,128)S(1)} collective-permute-done((f32[336,256]{1,0:T(8,128)S(1)}, f32[336,256]{1,0:T(8,128)S(1)}, u32[]{:S(2)}, u32[]{:S(2)}) %collective-permute-start.3) | collective-permute-done | bytes 344096 | tf_op jit(solution)/shard_map/ppermute | solution.py:400
  48.4 1.5 %collective-permute-start.6 = (f32[128,256]{1,0:T(8,128)S(1)}, f32[128,256]{1,0:T(8,128)S(1)}, u32[]{:S(2)}, u32[]{:S(2)}) collective-permute-start(f32[128,256]{1,0:T(8,128)S(1)} %get-tuple-element.34.refs_1_), channel_id=1, source_target_pairs={{0,4},{1,5},{2,6},{3,7},{4,0},{5,1},{6,2},{7,3},{8,12},{9,13},{10,... | collective-permute-start | bytes 393224 | tf_op jit(solution)/shard_map/ppermute | solution.py:400
  49.9 4.4 %collective-permute-done.6.refs_2_ = f32[128,256]{1,0:T(8,128)S(1)} collective-permute-done((f32[128,256]{1,0:T(8,128)S(1)}, f32[128,256]{1,0:T(8,128)S(1)}, u32[]{:S(2)}, u32[]{:S(2)}) %collective-permute-start.6) | collective-permute-done | bytes 131104 | tf_op jit(solution)/shard_map/ppermute | solution.py:400
  54.8 1.1 %shard_map.89 = (bf16[928,768]{1,0:T(8,128)(2,1)S(1)}, bf16[512,768]{1,0:T(8,128)(2,1)S(1)}, f32[10,16,128]{2,1,0:T(8,128)S(1)}, f32[10,16,128]{2,1,0:T(8,128)S(1)}, f32[16,128]{1,0:T(8,128)S(1)}) custom-call(bf16[512,464]{1,0:T(8,128)(2,1)S(1)} %get-tuple-element.38.cat_ref, f32[16,256]{1,0:T(8,128)S(1)} %get-tuple-element.40.a_ref, ...), custom_call_target="tpu_custom_call" | custom-call | flops 2000000000 | bytes 1048576 | tf_op jit(solution)/shard_map/pallas_call | solution.py:374
  56.0 1.1 %shard_map.90 = (bf16[928,768]{1,0:T(8,128)(2,1)S(1)}, bf16[512,768]{1,0:T(8,128)(2,1)S(1)}, f32[10,16,128]{2,1,0:T(8,128)S(1)}, f32[10,16,128]{2,1,0:T(8,128)S(1)}, f32[16,128]{1,0:T(8,128)S(1)}) custom-call(bf16[512,464]{1,0:T(8,128)(2,1)S(1)} %get-tuple-element.38.cat_ref, f32[16,256]{1,0:T(8,128)S(1)} %get-tuple-element.40.a_ref, ...), custom_call_target="tpu_custom_call" | custom-call | flops 2000000000 | bytes 1048576 | tf_op jit(solution)/shard_map/pallas_call | solution.py:374
  57.4 1.1 %collective-permute-done.11 = f32[10,16,128]{2,1,0:T(8,128)S(1)} collective-permute-done((f32[10,16,128]{2,1,0:T(8,128)S(1)}, f32[10,16,128]{2,1,0:T(8,128)S(1)}, u32[]{:S(2)}, u32[]{:S(2)}) %collective-permute-start.11) | collective-permute-done | bytes 81952 | tf_op jit(solution)/shard_map/ppermute | solution.py:400
  59.2 1.4 %collective-permute-start.13 = (f32[10,16,128]{2,1,0:T(8,128)S(1)}, f32[10,16,128]{2,1,0:T(8,128)S(1)}, u32[]{:S(2)}, u32[]{:S(2)}) collective-permute-start(f32[10,16,128]{2,1,0:T(8,128)S(1)} %add.3.own_ref), channel_id=1, source_target_pairs={{0,4},{1,5},{2,6},{3,7},{4,0},{5,1},{6,2},{7,3},{8,12},{9,13},{10,... | collective-permute-start | bytes 245768 | tf_op jit(solution)/shard_map/ppermute | solution.py:400
  60.6 1.5 %collective-permute-start.14 = (f32[10,16,128]{2,1,0:T(8,128)S(1)}, f32[10,16,128]{2,1,0:T(8,128)S(1)}, u32[]{:S(2)}, u32[]{:S(2)}) collective-permute-start(f32[10,16,128]{2,1,0:T(8,128)S(1)} %add.3.own_ref), channel_id=1, source_target_pairs={{0,6},{1,7},{2,4},{3,5},{4,2},{5,3},{6,0},{7,1},{8,14},{9,15},{10,... | collective-permute-start | bytes 245768 | tf_op jit(solution)/shard_map/ppermute | solution.py:400
  62.0 1.0 %collective-permute-done.12.refs_0_ = f32[10,16,128]{2,1,0:T(8,128)S(1)} collective-permute-done((f32[10,16,128]{2,1,0:T(8,128)S(1)}, f32[10,16,128]{2,1,0:T(8,128)S(1)}, u32[]{:S(2)}, u32[]{:S(2)}) %collective-permute-start.12) | collective-permute-done | bytes 81952 | tf_op jit(solution)/shard_map/ppermute | solution.py:400
  63.6 2.6 %collective-permute-done.14.refs_2_ = f32[10,16,128]{2,1,0:T(8,128)S(1)} collective-permute-done((f32[10,16,128]{2,1,0:T(8,128)S(1)}, f32[10,16,128]{2,1,0:T(8,128)S(1)}, u32[]{:S(2)}, u32[]{:S(2)}) %collective-permute-start.14) | collective-permute-done | bytes 81952 | tf_op jit(solution)/shard_map/ppermute | solution.py:400
  66.2 3.7 %shard_map.91 = f32[960,128]{1,0:T(8,128)} custom-call(f32[10,16,128]{2,1,0:T(8,128)S(1)} %add.3.own_ref, f32[928,128]{1,0:T(8,128)S(1)} %bitcast.17, f32[16,256]{1,0:T(8,128)S(1)} %get-tuple-element.40.a_ref, bf16[928,512]{1,0:T(8,128)(2,1)S(1)} %get-tuple-element.51.x1_ref, bf16[928,768]{1,0:T(8,128)(2,1)S(1)} %get-tuple-element.52.x2_ref, ...), custom_call_target="tpu_custom_call" | custom-call | flops 4000000000 | bytes 1048576 | tf_op jit(solution)/shard_map/pallas_call | solution.py:374
  69.9 4.6 %all-to-all-start.1 = ((f32[16,30,2,128]{3,2,1,0:T(2,128)}), f32[16,30,2,128]{3,2,1,0:T(2,128)S(1)}, u32[]{:S(2)}, u32[]{:S(2)}) async-start(f32[16,30,2,128]{3,2,1,0:T(2,128)} %bitcast.7), calls=%async_computation.1 | async-start | bytes 983040 | tf_op jit(solution)/shard_map/all_to_all | solution.py:394
  74.7 1.6 %shard_map.92 = (f32[464,128]{1,0:T(8,128)S(1)}, f32[464,128]{1,0:T(8,128)S(1)}) custom-call(s32[2]{0:T(128)S(1)} %pad_add_fusion.at_ref, f32[464,128]{1,0:T(8,128)S(1)} %bitcast.20, f32[464,128]{1,0:T(8,128)S(1)} %bitcast.21, f32[464,128]{1,0:T(8,128)S(1)} %bitcast.22), custom_call_target="tpu_custom_call" | custom-call | flops 1000000000 | bytes 1048576 | tf_op jit(solution)/shard_map/pallas_call | solution.py:374
  76.3 12.0 %all-to-all-done.1 = f32[16,30,2,128]{3,2,1,0:T(2,128)S(1)} async-done(((f32[16,30,2,128]{3,2,1,0:T(2,128)}), f32[16,30,2,128]{3,2,1,0:T(2,128)S(1)}, u32[]{:S(2)}, u32[]{:S(2)}) %all-to-all-start.1) | async-done | bytes 491552 | tf_op jit(solution)/shard_map/all_to_all | solution.py:394
  88.3 1.5 %shard_map.93 = (f32[464,128]{1,0:T(8,128)}, f32[464,128]{1,0:T(8,128)}, f32[1,128]{1,0:T(1,128)}) custom-call(s32[2]{0:T(128)S(1)} %pad_add_fusion.at_ref, f32[960,128]{1,0:T(8,128)S(1)} %bitcast.15, f32[464,128]{1,0:T(8,128)S(1)} %get-tuple-element.58.base_ref, f32[464,128]{1,0:T(8,128)S(1)} %get-tuple-element.59.par_ref), custom_call_target="tpu_custom_call" | custom-call | flops 1000000000 | bytes 1048576 | tf_op jit(solution)/shard_map/pallas_call | solution.py:374
  (36 shorter events, 4.5 us)
Async XLA Ops:
  0.6 0.9 %copy-start.1 = (f32[59392]{0:T(1024)S(1)}, f32[59392]{0:T(1024)}, u32[]{:S(2)}) copy-start(f32[59392]{0:T(1024)} %param.6) | copy-start | bytes 712708
  1.6 8.3 %copy-start.5 = (s32[512]{0:T(512)S(1)}, s32[512]{0:T(512)}, u32[]{:S(2)}) copy-start(s32[512]{0:T(512)} %param.10) | copy-start | bytes 6148
  1.6 8.3 %copy-start.6 = (s32[1,256]{1,0:T(1,128)S(1)}, s32[1,256]{1,0:T(1,128)}, u32[]{:S(2)}) copy-start(s32[1,256]{1,0:T(1,128)} %param.11) | copy-start | bytes 3076
  1.6 8.3 %copy-start = (f32[512,448]{0,1:T(8,128)S(1)}, f32[512,448]{0,1:T(8,128)}, u32[]{:S(2)}) copy-start(f32[512,448]{0,1:T(8,128)} %param.9) | copy-start | bytes 2752516
  2.5 25.8 %all-to-all-start = ((f32[16,29,2,128]{3,2,1,0:T(2,128)}), f32[16,29,2,128]{3,2,1,0:T(2,128)S(1)}, u32[]{:S(2)}, u32[]{:S(2)}) async-start(f32[16,29,2,128]{3,2,1,0:T(2,128)} %bitcast.3), calls=%async_computation | async-start | bytes 950272 | tf_op jit(solution)/shard_map/all_to_all | solution.py:394
  10.5 17.8 %collective-permute-start = (f32[336,256]{1,0:T(8,128)S(1)}, f32[336,256]{1,0:T(8,128)S(1)}, u32[]{:S(2)}, u32[]{:S(2)}) collective-permute-start(f32[336,256]{1,0:T(8,128)S(1)} %get-tuple-element.33.refs_0_), channel_id=1, source_target_pairs={{0,2},{1,3},{2,0},{3,1},{4,6},{5,7},{6,4},{7,5},{8,10},{9,11},{10,... | collective-permute-start | bytes 1032200 | tf_op jit(solution)/shard_map/ppermute | solution.py:400
  12.5 15.8 %collective-permute-start.1 = (f32[128,256]{1,0:T(8,128)S(1)}, f32[128,256]{1,0:T(8,128)S(1)}, u32[]{:S(2)}, u32[]{:S(2)}) collective-permute-start(f32[128,256]{1,0:T(8,128)S(1)} %get-tuple-element.34.refs_1_), channel_id=1, source_target_pairs={{0,2},{1,3},{2,0},{3,1},{4,6},{5,7},{6,4},{7,5},{8,10},{9,11},{10,... | collective-permute-start | bytes 393224 | tf_op jit(solution)/shard_map/ppermute | solution.py:400
  28.3 26.5 %collective-permute-start.5 = (f32[2,464,256]{2,1,0:T(8,128)S(1)}, f32[2,464,256]{2,1,0:T(8,128)S(1)}, u32[]{:S(2)}, u32[]{:S(2)}) collective-permute-start(f32[2,464,256]{2,1,0:T(8,128)S(1)} %get-tuple-element.37.join_ref), channel_id=1, source_target_pairs={{0,1},{1,0},{2,3},{3,2},{4,5},{5,4},{6,7},{7,6},{8,9},{9,8},{10,11... | collective-permute-start | bytes 2850824 | tf_op jit(solution)/shard_map/ppermute | solution.py:400
  28.4 10.5 %collective-permute-start.2 = (f32[336,256]{1,0:T(8,128)S(1)}, f32[336,256]{1,0:T(8,128)S(1)}, u32[]{:S(2)}, u32[]{:S(2)}) collective-permute-start(f32[336,256]{1,0:T(8,128)S(1)} %get-tuple-element.33.refs_0_), channel_id=1, source_target_pairs={{0,4},{1,5},{2,6},{3,7},{4,0},{5,1},{6,2},{7,3},{8,12},{9,13},{10,... | collective-permute-start | bytes 1032200 | tf_op jit(solution)/shard_map/ppermute | solution.py:400
  38.9 9.5 %collective-permute-start.3 = (f32[336,256]{1,0:T(8,128)S(1)}, f32[336,256]{1,0:T(8,128)S(1)}, u32[]{:S(2)}, u32[]{:S(2)}) collective-permute-start(f32[336,256]{1,0:T(8,128)S(1)} %collective-permute-done.2.refs_1_), channel_id=1, source_target_pairs={{0,2},{1,3},{2,0},{3,1},{4,6},{5,7},{6,4},{7,5},{8,10},{9,11},{10,... | collective-permute-start | bytes 1032200 | tf_op jit(solution)/shard_map/ppermute | solution.py:400
  39.5 5.0 %collective-permute-start.4 = (f32[128,256]{1,0:T(8,128)S(1)}, f32[128,256]{1,0:T(8,128)S(1)}, u32[]{:S(2)}, u32[]{:S(2)}) collective-permute-start(f32[128,256]{1,0:T(8,128)S(1)} %collective-permute-done.1.refs_3_), channel_id=1, source_target_pairs={{0,4},{1,5},{2,6},{3,7},{4,0},{5,1},{6,2},{7,3},{8,12},{9,13},{10,... | collective-permute-start | bytes 393224 | tf_op jit(solution)/shard_map/ppermute | solution.py:400
  40.9 15.1 %collective-permute-start.7 = (f32[336,256]{1,0:T(8,128)S(1)}, f32[336,256]{1,0:T(8,128)S(1)}, u32[]{:S(2)}, u32[]{:S(2)}) collective-permute-start(f32[336,256]{1,0:T(8,128)S(1)} %collective-permute-done.2.refs_1_), channel_id=1, source_target_pairs={{0,1},{1,0},{2,3},{3,2},{4,5},{5,4},{6,7},{7,6},{8,9},{9,8},{10,11... | collective-permute-start | bytes 1032200 | tf_op jit(solution)/shard_map/ppermute | solution.py:400
  48.4 7.6 %collective-permute-start.9 = (f32[336,256]{1,0:T(8,128)S(1)}, f32[336,256]{1,0:T(8,128)S(1)}, u32[]{:S(2)}, u32[]{:S(2)}) collective-permute-start(f32[336,256]{1,0:T(8,128)S(1)} %collective-permute-done.3.refs_2_), channel_id=1, source_target_pairs={{0,1},{1,0},{2,3},{3,2},{4,5},{5,4},{6,7},{7,6},{8,9},{9,8},{10,11... | collective-permute-start | bytes 1032200 | tf_op jit(solution)/shard_map/ppermute | solution.py:400
  48.4 5.9 %collective-permute-start.6 = (f32[128,256]{1,0:T(8,128)S(1)}, f32[128,256]{1,0:T(8,128)S(1)}, u32[]{:S(2)}, u32[]{:S(2)}) collective-permute-start(f32[128,256]{1,0:T(8,128)S(1)} %get-tuple-element.34.refs_1_), channel_id=1, source_target_pairs={{0,4},{1,5},{2,6},{3,7},{4,0},{5,1},{6,2},{7,3},{8,12},{9,13},{10,... | collective-permute-start | bytes 393224 | tf_op jit(solution)/shard_map/ppermute | solution.py:400
  54.3 1.6 %collective-permute-start.8 = (f32[128,256]{1,0:T(8,128)S(1)}, f32[128,256]{1,0:T(8,128)S(1)}, u32[]{:S(2)}, u32[]{:S(2)}) collective-permute-start(f32[128,256]{1,0:T(8,128)S(1)} %collective-permute-done.6.refs_2_), channel_id=1, source_target_pairs={{0,1},{1,0},{2,3},{3,2},{4,5},{5,4},{6,7},{7,6},{8,9},{9,8},{10,11... | collective-permute-start | bytes 393224 | tf_op jit(solution)/shard_map/ppermute | solution.py:400
  54.3 1.7 %collective-permute-start.10 = (f32[128,256]{1,0:T(8,128)S(1)}, f32[128,256]{1,0:T(8,128)S(1)}, u32[]{:S(2)}, u32[]{:S(2)}) collective-permute-start(f32[128,256]{1,0:T(8,128)S(1)} %collective-permute-done.4.refs_3_), channel_id=1, source_target_pairs={{0,1},{1,0},{2,3},{3,2},{4,5},{5,4},{6,7},{7,6},{8,9},{9,8},{10,11... | collective-permute-start | bytes 393224 | tf_op jit(solution)/shard_map/ppermute | solution.py:400
  57.1 1.3 %collective-permute-start.11 = (f32[10,16,128]{2,1,0:T(8,128)S(1)}, f32[10,16,128]{2,1,0:T(8,128)S(1)}, u32[]{:S(2)}, u32[]{:S(2)}) collective-permute-start(f32[10,16,128]{2,1,0:T(8,128)S(1)} %get-tuple-element.50), channel_id=1, source_target_pairs={{0,1},{1,0},{2,3},{3,2},{4,5},{5,4},{6,7},{7,6},{8,9},{9,8},{10,11... | collective-permute-start | bytes 245768 | tf_op jit(solution)/shard_map/ppermute | solution.py:400
  58.5 4.6 %collective-permute-start.12 = (f32[10,16,128]{2,1,0:T(8,128)S(1)}, f32[10,16,128]{2,1,0:T(8,128)S(1)}, u32[]{:S(2)}, u32[]{:S(2)}) collective-permute-start(f32[10,16,128]{2,1,0:T(8,128)S(1)} %add.3.own_ref), channel_id=1, source_target_pairs={{0,2},{1,3},{2,0},{3,1},{4,6},{5,7},{6,4},{7,5},{8,10},{9,11},{10,... | collective-permute-start | bytes 245768 | tf_op jit(solution)/shard_map/ppermute | solution.py:400
  59.2 4.4 %collective-permute-start.13 = (f32[10,16,128]{2,1,0:T(8,128)S(1)}, f32[10,16,128]{2,1,0:T(8,128)S(1)}, u32[]{:S(2)}, u32[]{:S(2)}) collective-permute-start(f32[10,16,128]{2,1,0:T(8,128)S(1)} %add.3.own_ref), channel_id=1, source_target_pairs={{0,4},{1,5},{2,6},{3,7},{4,0},{5,1},{6,2},{7,3},{8,12},{9,13},{10,... | collective-permute-start | bytes 245768 | tf_op jit(solution)/shard_map/ppermute | solution.py:400
  60.6 5.6 %collective-permute-start.14 = (f32[10,16,128]{2,1,0:T(8,128)S(1)}, f32[10,16,128]{2,1,0:T(8,128)S(1)}, u32[]{:S(2)}, u32[]{:S(2)}) collective-permute-start(f32[10,16,128]{2,1,0:T(8,128)S(1)} %add.3.own_ref), channel_id=1, source_target_pairs={{0,6},{1,7},{2,4},{3,5},{4,2},{5,3},{6,0},{7,1},{8,14},{9,15},{10,... | collective-permute-start | bytes 245768 | tf_op jit(solution)/shard_map/ppermute | solution.py:400
  66.2 8.4 %copy-start.2 = (f32[59392]{0:T(1024)S(1)}, f32[59392]{0:T(1024)}, u32[]{:S(2)}) copy-start(f32[59392]{0:T(1024)} %param.6) | copy-start | bytes 712708
  66.2 8.4 %copy-start.3 = (f32[59392]{0:T(1024)S(1)}, f32[59392]{0:T(1024)}, u32[]{:S(2)}) copy-start(f32[59392]{0:T(1024)} %param.7) | copy-start | bytes 712708
  66.2 8.4 %copy-start.4 = (f32[1,59392]{1,0:T(1,128)S(1)}, f32[1,59392]{1,0:T(1,128)}, u32[]{:S(2)}) copy-start(f32[1,59392]{1,0:T(1,128)} %param.8) | copy-start | bytes 712708
  69.9 18.4 %all-to-all-start.1 = ((f32[16,30,2,128]{3,2,1,0:T(2,128)}), f32[16,30,2,128]{3,2,1,0:T(2,128)S(1)}, u32[]{:S(2)}, u32[]{:S(2)}) async-start(f32[16,30,2,128]{3,2,1,0:T(2,128)} %bitcast.7), calls=%async_computation.1 | async-start | bytes 983040 | tf_op jit(solution)/shard_map/all_to_all | solution.py:394

commit v4 on v3

--- a/solution.py
+++ b/solution.py
@@ -81,14 +81,19 @@
     return lax.broadcasted_iota(jnp.int32, shape, axis)
 
 
-def pick_kernel(plan, img_ref, meta_ref, *parts):
+def prior_kernel(plan, at_ref, out_ref):
+    shape = (plan.flat, LANES)
+    index = at_ref[0] + iota(shape, 0) * LANES + iota(shape, 1)
+    out_ref[...] = precision_of(index, plan.din)
+
+
+def pick_kernel(plan, img_ref, lab_ref, idx_ref, *parts):
     pool = img_ref.shape[1]
-    picks = meta_ref[:, pool:].astype(jnp.int32)
-    hot = (iota((pool, plan.batch), 0) == picks).astype(BF16)
+    hot = (iota((pool, plan.batch), 0) == idx_ref[...]).astype(BF16)
     hi, mid, lo = split3(img_ref[...])
     rows = dot(hi, hot, NN) + dot(mid, hot, NN) + dot(lo, hot, NN)
     spare = plan.xrows - plan.din
-    marks = jnp.broadcast_to(meta_ref[:, :pool], (spare, pool)).astype(BF16)
+    marks = jnp.broadcast_to(lab_ref[...].astype(F32), (spare, pool)).astype(BF16)
     marks = dot(marks, hot, NN)
     at = iota((spare, plan.batch), 0)
     rows = jnp.concatenate([rows, jnp.where(at == 0, 1.0, jnp.where(at == 1, marks, 0.0))], axis=0)
@@ -174,10 +179,9 @@
     for s, m in enumerate(slots):
         for i in range(per):
             own, other, at = m * per + i, (m ^ 1) * per + i, (s * per + i) * LANES
-            for o in range(OUT):
-                row = lg[o : o + 1, at : at + LANES]
-                own_ref[o, own : own + 1, :] = row
-                send_ref[o, other : other + 1, :] = row
+            block = lg[:OUT, at : at + LANES]
+            own_ref[pl.ds(own, OUT, stride=plan.group * per), :] = block
+            send_ref[pl.ds(other, OUT, stride=plan.group * per), :] = block
 
 
 def ready_kernel(plan, *refs):
@@ -240,14 +244,20 @@
     diag = iota((plan.classes, LANES), 0) == iota((plan.classes, LANES), 1)
     row = (plan.n - 1) * plan.unit + (plan.tail + OUT) * plan.nb
     bias = w_ref[row : row + 1, :]
-    for m in range(plan.group):
-        value = own_ref[:, m * per : (m + 1) * per, :]
+    wide = 2 * per
+
+    def placed(ref, o, q):
+        at = [o * lines + (p ^ q) * wide for p in range(plan.group // 2)]
+        return jnp.concatenate([ref[start : start + wide, :] for start in at], axis=0)
+
+    values = []
+    for o in range(OUT):
+        value = own_ref[o * lines : (o + 1) * lines, :]
         for i, ref in enumerate(lg_refs):
-            other = m ^ (2 * (i + 1))
-            value = value + ref[:, other * per : (other + 1) * per, :]
-        lg_ref[:, m * per : (m + 1) * per, :] = value
+            value = value + placed(ref, o, i + 1)
+        values.append(value)
     labels = lab_ref[...].astype(jnp.int32)
-    logits = [lg_ref[o] + bias[:, o : o + 1] for o in range(OUT)]
+    logits = [values[o] + bias[:, o : o + 1] for o in range(OUT)]
     top = functools.reduce(jnp.maximum, logits)
     ex = [jnp.exp(v - top) for v in logits]
     norm = functools.reduce(jnp.add, ex)
@@ -258,9 +268,10 @@
     dl_ref[...] = jnp.zeros_like(dl_ref)
     for o in range(OUT):
         value = ex[o] * share - jnp.where(hits[o], 1.0, 0.0)
-        for i in range(lines):
-            at = (order.index(i // per) * per + i % per) * LANES
-            dl_ref[o : o + 1, at : at + LANES] = value[i : i + 1, :]
+        lg_ref[o * lines : (o + 1) * lines, :] = value
+    for i in range(lines):
+        at = (order.index(i // per) * per + i % per) * LANES
+        dl_ref[:OUT, at : at + LANES] = lg_ref[pl.ds(i, OUT, stride=lines), :]
     dl = dl_ref[...]
     dbias = jnp.sum(dl, axis=1, keepdims=True)
     dbias = jnp.sum(jnp.where(diag, dbias, 0.0), axis=0, keepdims=True)
@@ -283,8 +294,6 @@
             dh_ref[cols:, here] = dh_lo
         da = da + dot(h_ref[...], dl_cat[:, start : start + width], NT)
         start += width
-    da = da.T
-    da = da[:classes, :cols] + (da[classes:, :cols] + da[:classes, cols:])
     dw, start = 0.0, 0
     for x_ref in (x1_ref, x2_ref, x3_ref):
         here = slice(start, start + x_ref.shape[1])
@@ -297,6 +306,8 @@
         for b in range(plan.nb):
             piece = dw_ref[first : first + count, b * LANES : (b + 1) * LANES]
             out_ref[pl.ds(d * plan.back + b, count, stride=plan.nb), :] = piece
+    da = da.T
+    da = da[:classes, :cols] + (da[classes:, :cols] + da[:classes, cols:])
     mask, place = class_masks(plan)
     hi, mid, lo = split3(da)
     parts = []
@@ -315,16 +326,14 @@
         out_ref[at : at + 1, :] = jnp.broadcast_to(nll, (1, LANES))
 
 
-def prepare_kernel(plan, at_ref, par_ref, mom_ref, noise_ref, base_ref, keep_ref, mom, noise, sems):
+def prepare_kernel(prior_ref, par_ref, mom_ref, noise_ref, base_ref, keep_ref, mom, noise, sems):
     loads = [pltpu.make_async_copy(s, d, sems.at[i]) for i, (s, d) in enumerate(
         ((par_ref, keep_ref), (mom_ref, mom), (noise_ref, noise)))]
     for load in loads:
         load.start()
     for load in loads:
         load.wait()
-    shape = (plan.flat, LANES)
-    index = at_ref[0] + iota(shape, 0) * LANES + iota(shape, 1)
-    prior = precision_of(index, plan.din) * keep_ref[...]
+    prior = prior_ref[...] * keep_ref[...]
     base = (1.0 - step_size * friction) * mom[...] - step_size * prior
     base_ref[...] = base + math.sqrt(2.0 * friction * step_size) * noise[...]
 
@@ -366,11 +375,11 @@
     return jnp.where(index < in_end, float(din), inner)
 
 
-def call(kernel, args, outs, scratch=(), smem=0, limit=16, whole=0, cost=1):
+def call(kernel, args, outs, scratch=(), smem=0, limit=16, whole=0, cost=1, lead=0):
     vm = pl.BlockSpec(memory_space=pltpu.VMEM)
     sm = pl.BlockSpec(memory_space=pltpu.SMEM)
     anywhere = pl.BlockSpec(memory_space=pltpu.HBM)
-    specs = [sm] * smem + [anywhere] * whole
+    specs = [sm] * smem + [vm] * lead + [anywhere] * whole
     return pl.pallas_call(
         kernel,
         out_shape=[jax.ShapeDtypeStruct(s, t) for s, t in outs],
@@ -394,16 +403,23 @@
         return lax.all_to_all(x, "dp", 0, 0, tiled=True).reshape(-1, LANES)
 
     total = plan.group * plan.batch
-    dense = (OUT, total // LANES, LANES)
+    lines = total // LANES
+    dense = (OUT * lines, LANES)
 
     def hop(x, k):
         return lax.ppermute(x, "dp", [(d, d ^ k) for d in range(n)])
 
 
-    meta = jnp.concatenate([labels, indices[0]]).astype(F32).reshape(1, -1)
+    (prior,) = call(
+        functools.partial(prior_kernel, plan),
+        ((me * params.shape[0]).reshape(1),),
+        [(flat, F32)],
+        smem=1,
+        cost=3,
+    )
     a, b = call(
         functools.partial(pick_kernel, plan),
-        (images.T, meta),
+        (images.T, labels.reshape(1, pool), indices),
         [((part.stop - part.start, plan.batch), F32) for part in plan.parts],
     )
     b2 = hop(b, 2)
@@ -423,7 +439,7 @@
     join, marks = call(
         functools.partial(ready_kernel, plan),
         (a, b, a2, b2),
-        [((len(plan.early), plan.xrows, plan.batch), F32), (dense[1:], F32)],
+        [((len(plan.early), plan.xrows, plan.batch), F32), ((lines, LANES), F32)],
     )
     weights, join = lax.optimization_barrier((weights, join))
     other = hop(join, 1)
@@ -452,7 +468,7 @@
                 ((2 * plan.cols, width), BF16),
                 (dense, F32),
                 (dense, F32),
-                (dense[1:], F32),
+                ((lines, LANES), F32),
             ],
             cost=2,
         )
@@ -481,11 +497,11 @@
     count = n * plan.batch
     spot = jnp.stack([me * params.shape[0], last])
     base, old = call(
-        functools.partial(prepare_kernel, plan),
-        (spot, params.reshape(flat), momentum.reshape(flat), noise_draws.reshape(flat)),
+        prepare_kernel,
+        (prior, params.reshape(flat), momentum.reshape(flat), noise_draws.reshape(flat)),
         [(flat, F32), (flat, F32)],
         [pltpu.VMEM(flat, F32), pltpu.VMEM(flat, F32), pltpu.SemaphoreType.DMA((3,))],
-        smem=1,
+        lead=1,
         whole=3,
     )
     new_params, new_momentum, loss = call(

time: 90.2 us -> 90.1 us (level)
  local copies, waits for them, and re-layouts: 0.96 us -> 2.01 us
    unnamed x14, local copies, waits for them, and re-layouts: 0.96 us -> 2.01 us
    pallas_call x9 -> x10, Pallas kernels: 11.5 us -> 10.9 us  [call(): pl.pallas_call(kernel, out_shape=[jax.ShapeDtypeStruct(s, t) for s, t in...]
  transfers between devices with their start and end apart: 17 -> 17, of which waited for: 10 -> 10; matrix products, arithmetic and copies ran while one was open for 0% -> 0% of each run, Pallas kernels for 5% -> 4%
where the time goes in v4:
time: 90.1 us; the launch traced here: 89.7 us
  waiting for transfers between devices  52.4 us (58%)
  starting transfers between devices  23.5 us (26%)
  Pallas kernels  10.9 us (12%)
  local copies, waits for them, and re-layouts  2.01 us (2%)
    ppermute x15, waiting for transfers between devices, hop(): return lax.ppermute(x, 'dp', [(d, d ^ k) for d in range(n)])  40.9 us
    all_to_all x2, starting transfers between devices, exchange(): return lax.all_to_all(x, 'dp', 0, 0, tiled=True).reshape(-1, LANES)  12 us
    ppermute x15, starting transfers between devices, hop(): return lax.ppermute(x, 'dp', [(d, d ^ k) for d in range(n)])  11.5 us
    all_to_all x2, waiting for transfers between devices, exchange(): return lax.all_to_all(x, 'dp', 0, 0, tiled=True).reshape(-1, LANES)  11.5 us
    pallas_call x10, Pallas kernels, call(): pl.pallas_call(kernel, out_shape=[jax.ShapeDtypeStruct(s, t) for s, t in...  10.9 us
    unnamed x14, local copies, waits for them, and re-layouts  2.01 us
  transfers between devices with their start and end apart: 17, of which 10 were waited for; matrix products, arithmetic and copies ran while one was open for 0% of the time, Pallas kernels for 4%

profile of v4, /device:TPU:0, one launch (start us, length us, event | category | flops | bytes accessed | tf_op | source)
XLA Modules:
  0.0 89.7 jit_solution(17925165902998129769)
XLA Ops:
  0.6 0.9 %copy-done.1 = f32[59392]{0:T(1024)S(1)} copy-done((f32[59392]{0:T(1024)S(1)}, f32[59392]{0:T(1024)}, u32[]{:S(2)}) %copy-start.1) | copy-done | bytes 237592
  2.5 7.4 %all-to-all-start = ((f32[16,29,2,128]{3,2,1,0:T(2,128)}), f32[16,29,2,128]{3,2,1,0:T(2,128)S(1)}, u32[]{:S(2)}, u32[]{:S(2)}) async-start(f32[16,29,2,128]{3,2,1,0:T(2,128)} %bitcast.3), calls=%async_computation | async-start | bytes 950272 | tf_op jit(solution)/shard_map/all_to_all | solution.py:403
  10.5 2.0 %collective-permute-start = (f32[336,256]{1,0:T(8,128)S(1)}, f32[336,256]{1,0:T(8,128)S(1)}, u32[]{:S(2)}, u32[]{:S(2)}) collective-permute-start(f32[336,256]{1,0:T(8,128)S(1)} %get-tuple-element.33.refs_0_), channel_id=1, source_target_pairs={{0,2},{1,3},{2,0},{3,1},{4,6},{5,7},{6,4},{7,5},{8,10},{9,11},{10,... | collective-permute-start | bytes 1032200 | tf_op jit(solution)/shard_map/ppermute | solution.py:410
  12.6 15.7 %collective-permute-done.1.refs_3_ = f32[128,256]{1,0:T(8,128)S(1)} collective-permute-done((f32[128,256]{1,0:T(8,128)S(1)}, f32[128,256]{1,0:T(8,128)S(1)}, u32[]{:S(2)}, u32[]{:S(2)}) %collective-permute-start.1) | collective-permute-done | bytes 131104 | tf_op jit(solution)/shard_map/ppermute | solution.py:410
  28.4 1.5 %collective-permute-start.2 = (f32[336,256]{1,0:T(8,128)S(1)}, f32[336,256]{1,0:T(8,128)S(1)}, u32[]{:S(2)}, u32[]{:S(2)}) collective-permute-start(f32[336,256]{1,0:T(8,128)S(1)} %get-tuple-element.33.refs_0_), channel_id=1, source_target_pairs={{0,4},{1,5},{2,6},{3,7},{4,0},{5,1},{6,2},{7,3},{8,12},{9,13},{10,... | collective-permute-start | bytes 1032200 | tf_op jit(solution)/shard_map/ppermute | solution.py:410
  29.9 8.9 %collective-permute-done.2.refs_1_ = f32[336,256]{1,0:T(8,128)S(1)} collective-permute-done((f32[336,256]{1,0:T(8,128)S(1)}, f32[336,256]{1,0:T(8,128)S(1)}, u32[]{:S(2)}, u32[]{:S(2)}) %collective-permute-start.2) | collective-permute-done | bytes 344096 | tf_op jit(solution)/shard_map/ppermute | solution.py:410
  39.5 1.4 %collective-permute-start.4 = (f32[128,256]{1,0:T(8,128)S(1)}, f32[128,256]{1,0:T(8,128)S(1)}, u32[]{:S(2)}, u32[]{:S(2)}) collective-permute-start(f32[128,256]{1,0:T(8,128)S(1)} %collective-permute-done.1.refs_3_), channel_id=1, source_target_pairs={{0,4},{1,5},{2,6},{3,7},{4,0},{5,1},{6,2},{7,3},{8,12},{9,13},{10,... | collective-permute-start | bytes 393224 | tf_op jit(solution)/shard_map/ppermute | solution.py:410
  40.9 0.9 %shard_map.88 = (bf16[928,512]{1,0:T(8,128)(2,1)S(1)}, bf16[512,512]{1,0:T(8,128)(2,1)S(1)}, f32[16,256]{1,0:T(8,128)S(1)}, bf16[512,464]{1,0:T(8,128)(2,1)S(1)}...) custom-call(f32[928,128]{1,0:T(8,128)S(1)} %bitcast.16, f32[2,464,256]{2,1,0:T(8,128)S(1)} %get-tuple-element.37.join_ref), custom_call_target="tpu_custom_call" | custom-call | flops 3000000000 | bytes 1048576 | tf_op jit(solution)/shard_map/pallas_call | solution.py:383
  41.8 2.6 %collective-permute-done.4.refs_3_ = f32[128,256]{1,0:T(8,128)S(1)} collective-permute-done((f32[128,256]{1,0:T(8,128)S(1)}, f32[128,256]{1,0:T(8,128)S(1)}, u32[]{:S(2)}, u32[]{:S(2)}) %collective-permute-start.4) | collective-permute-done | bytes 131104 | tf_op jit(solution)/shard_map/ppermute | solution.py:410
  44.5 4.0 %collective-permute-done.3.refs_2_ = f32[336,256]{1,0:T(8,128)S(1)} collective-permute-done((f32[336,256]{1,0:T(8,128)S(1)}, f32[336,256]{1,0:T(8,128)S(1)}, u32[]{:S(2)}, u32[]{:S(2)}) %collective-permute-start.3) | collective-permute-done | bytes 344096 | tf_op jit(solution)/shard_map/ppermute | solution.py:410
  48.4 1.5 %collective-permute-start.6 = (f32[128,256]{1,0:T(8,128)S(1)}, f32[128,256]{1,0:T(8,128)S(1)}, u32[]{:S(2)}, u32[]{:S(2)}) collective-permute-start(f32[128,256]{1,0:T(8,128)S(1)} %get-tuple-element.34.refs_1_), channel_id=1, source_target_pairs={{0,4},{1,5},{2,6},{3,7},{4,0},{5,1},{6,2},{7,3},{8,12},{9,13},{10,... | collective-permute-start | bytes 393224 | tf_op jit(solution)/shard_map/ppermute | solution.py:410
  49.9 4.4 %collective-permute-done.6.refs_2_ = f32[128,256]{1,0:T(8,128)S(1)} collective-permute-done((f32[128,256]{1,0:T(8,128)S(1)}, f32[128,256]{1,0:T(8,128)S(1)}, u32[]{:S(2)}, u32[]{:S(2)}) %collective-permute-start.6) | collective-permute-done | bytes 131104 | tf_op jit(solution)/shard_map/ppermute | solution.py:410
  54.8 1.1 %shard_map.89 = (bf16[928,768]{1,0:T(8,128)(2,1)S(1)}, bf16[512,768]{1,0:T(8,128)(2,1)S(1)}, f32[160,128]{1,0:T(8,128)S(1)}, f32[160,128]{1,0:T(8,128)S(1)}, f32[16,128]{1,0:T(8,128)S(1)}) custom-call(bf16[512,464]{1,0:T(8,128)(2,1)S(1)} %get-tuple-element.38.cat_ref, f32[16,256]{1,0:T(8,128)S(1)} %get-tuple-element.40.a_ref, ...), custom_call_target="tpu_custom_call" | custom-call | flops 2000000000 | bytes 1048576 | tf_op jit(solution)/shard_map/pallas_call | solution.py:383
  56.0 1.1 %shard_map.90 = (bf16[928,768]{1,0:T(8,128)(2,1)S(1)}, bf16[512,768]{1,0:T(8,128)(2,1)S(1)}, f32[160,128]{1,0:T(8,128)S(1)}, f32[160,128]{1,0:T(8,128)S(1)}, f32[16,128]{1,0:T(8,128)S(1)}) custom-call(bf16[512,464]{1,0:T(8,128)(2,1)S(1)} %get-tuple-element.38.cat_ref, f32[16,256]{1,0:T(8,128)S(1)} %get-tuple-element.40.a_ref, ...), custom_call_target="tpu_custom_call" | custom-call | flops 2000000000 | bytes 1048576 | tf_op jit(solution)/shard_map/pallas_call | solution.py:383
  57.3 1.1 %collective-permute-done.11 = f32[160,128]{1,0:T(8,128)S(1)} collective-permute-done((f32[160,128]{1,0:T(8,128)S(1)}, f32[160,128]{1,0:T(8,128)S(1)}, u32[]{:S(2)}, u32[]{:S(2)}) %collective-permute-start.11) | collective-permute-done | bytes 81952 | tf_op jit(solution)/shard_map/ppermute | solution.py:410
  59.1 1.4 %collective-permute-start.13 = (f32[160,128]{1,0:T(8,128)S(1)}, f32[160,128]{1,0:T(8,128)S(1)}, u32[]{:S(2)}, u32[]{:S(2)}) collective-permute-start(f32[160,128]{1,0:T(8,128)S(1)} %add.3.own_ref), channel_id=1, source_target_pairs={{0,4},{1,5},{2,6},{3,7},{4,0},{5,1},{6,2},{7,3},{8,12},{9,13},{10,... | collective-permute-start | bytes 245768 | tf_op jit(solution)/shard_map/ppermute | solution.py:410
  60.5 1.5 %collective-permute-start.14 = (f32[160,128]{1,0:T(8,128)S(1)}, f32[160,128]{1,0:T(8,128)S(1)}, u32[]{:S(2)}, u32[]{:S(2)}) collective-permute-start(f32[160,128]{1,0:T(8,128)S(1)} %add.3.own_ref), channel_id=1, source_target_pairs={{0,6},{1,7},{2,4},{3,5},{4,2},{5,3},{6,0},{7,1},{8,14},{9,15},{10,... | collective-permute-start | bytes 245768 | tf_op jit(solution)/shard_map/ppermute | solution.py:410
  62.0 1.0 %collective-permute-done.12.refs_0_ = f32[160,128]{1,0:T(8,128)S(1)} collective-permute-done((f32[160,128]{1,0:T(8,128)S(1)}, f32[160,128]{1,0:T(8,128)S(1)}, u32[]{:S(2)}, u32[]{:S(2)}) %collective-permute-start.12) | collective-permute-done | bytes 81952 | tf_op jit(solution)/shard_map/ppermute | solution.py:410
  63.6 2.6 %collective-permute-done.14.refs_2_ = f32[160,128]{1,0:T(8,128)S(1)} collective-permute-done((f32[160,128]{1,0:T(8,128)S(1)}, f32[160,128]{1,0:T(8,128)S(1)}, u32[]{:S(2)}, u32[]{:S(2)}) %collective-permute-start.14) | collective-permute-done | bytes 81952 | tf_op jit(solution)/shard_map/ppermute | solution.py:410
  66.2 3.7 %shard_map.91 = f32[960,128]{1,0:T(8,128)} custom-call(f32[160,128]{1,0:T(8,128)S(1)} %add.3.own_ref, f32[928,128]{1,0:T(8,128)S(1)} %bitcast.17, f32[16,256]{1,0:T(8,128)S(1)} %get-tuple-element.40.a_ref, bf16[928,512]{1,0:T(8,128)(2,1)S(1)} %get-tuple-element.51.x1_ref, bf16[928,768]{1,0:T(8,128)(2,1)S(1)} %get-tuple-element.52.x2_ref, ...), custom_call_target="tpu_custom_call" | custom-call | flops 4000000000 | bytes 1048576 | tf_op jit(solution)/shard_map/pallas_call | solution.py:383
  69.8 4.7 %all-to-all-start.1 = ((f32[16,30,2,128]{3,2,1,0:T(2,128)}), f32[16,30,2,128]{3,2,1,0:T(2,128)S(1)}, u32[]{:S(2)}, u32[]{:S(2)}) async-start(f32[16,30,2,128]{3,2,1,0:T(2,128)} %bitcast.7), calls=%async_computation.1 | async-start | bytes 983040 | tf_op jit(solution)/shard_map/all_to_all | solution.py:403
  75.7 1.0 %shard_map.93 = (f32[464,128]{1,0:T(8,128)S(1)}, f32[464,128]{1,0:T(8,128)S(1)}) custom-call(f32[464,128]{1,0:T(8,128)S(1)} %shard_map.92.prior_ref, f32[464,128]{1,0:T(8,128)S(1)} %bitcast.20, f32[464,128]{1,0:T(8,128)S(1)} %bitcast.21, f32[464,128]{1,0:T(8,128)S(1)} %bitcast.22), custom_call_target="tpu_custom_call" | custom-call | flops 1000000000 | bytes 1048576 | tf_op jit(solution)/shard_map/pallas_call | solution.py:383
  76.8 11.5 %all-to-all-done.1 = f32[16,30,2,128]{3,2,1,0:T(2,128)S(1)} async-done(((f32[16,30,2,128]{3,2,1,0:T(2,128)}), f32[16,30,2,128]{3,2,1,0:T(2,128)S(1)}, u32[]{:S(2)}, u32[]{:S(2)}) %all-to-all-start.1) | async-done | bytes 491552 | tf_op jit(solution)/shard_map/all_to_all | solution.py:403
  88.2 1.5 %shard_map.94 = (f32[464,128]{1,0:T(8,128)}, f32[464,128]{1,0:T(8,128)}, f32[1,128]{1,0:T(1,128)}) custom-call(s32[2]{0:T(128)S(1)} %pad_add_fusion.at_ref, f32[960,128]{1,0:T(8,128)S(1)} %bitcast.15, f32[464,128]{1,0:T(8,128)S(1)} %get-tuple-element.58.base_ref, f32[464,128]{1,0:T(8,128)S(1)} %get-tuple-element.59.par_ref), custom_call_target="tpu_custom_call" | custom-call | flops 1000000000 | bytes 1048576 | tf_op jit(solution)/shard_map/pallas_call | solution.py:383
  (36 shorter events, 5.5 us)
Async XLA Ops:
  0.6 0.9 %copy-start.1 = (f32[59392]{0:T(1024)S(1)}, f32[59392]{0:T(1024)}, u32[]{:S(2)}) copy-start(f32[59392]{0:T(1024)} %param.6) | copy-start | bytes 712708
  1.6 8.3 %copy-start = (f32[512,448]{0,1:T(8,128)S(1)}, f32[512,448]{0,1:T(8,128)}, u32[]{:S(2)}) copy-start(f32[512,448]{0,1:T(8,128)} %param.9) | copy-start | bytes 2752516
  1.6 8.3 %copy-start.5 = (s32[512]{0:T(512)S(1)}, s32[512]{0:T(512)}, u32[]{:S(2)}) copy-start(s32[512]{0:T(512)} %param.10) | copy-start | bytes 6148
  1.6 8.3 %copy-start.6 = (s32[1,256]{1,0:T(1,128)S(1)}, s32[1,256]{1,0:T(1,128)}, u32[]{:S(2)}) copy-start(s32[1,256]{1,0:T(1,128)} %idx_ref.1) | copy-start | bytes 3076
  2.5 25.8 %all-to-all-start = ((f32[16,29,2,128]{3,2,1,0:T(2,128)}), f32[16,29,2,128]{3,2,1,0:T(2,128)S(1)}, u32[]{:S(2)}, u32[]{:S(2)}) async-start(f32[16,29,2,128]{3,2,1,0:T(2,128)} %bitcast.3), calls=%async_computation | async-start | bytes 950272 | tf_op jit(solution)/shard_map/all_to_all | solution.py:403
  10.5 17.8 %collective-permute-start = (f32[336,256]{1,0:T(8,128)S(1)}, f32[336,256]{1,0:T(8,128)S(1)}, u32[]{:S(2)}, u32[]{:S(2)}) collective-permute-start(f32[336,256]{1,0:T(8,128)S(1)} %get-tuple-element.33.refs_0_), channel_id=1, source_target_pairs={{0,2},{1,3},{2,0},{3,1},{4,6},{5,7},{6,4},{7,5},{8,10},{9,11},{10,... | collective-permute-start | bytes 1032200 | tf_op jit(solution)/shard_map/ppermute | solution.py:410
  12.5 15.8 %collective-permute-start.1 = (f32[128,256]{1,0:T(8,128)S(1)}, f32[128,256]{1,0:T(8,128)S(1)}, u32[]{:S(2)}, u32[]{:S(2)}) collective-permute-start(f32[128,256]{1,0:T(8,128)S(1)} %get-tuple-element.34.refs_1_), channel_id=1, source_target_pairs={{0,2},{1,3},{2,0},{3,1},{4,6},{5,7},{6,4},{7,5},{8,10},{9,11},{10,... | collective-permute-start | bytes 393224 | tf_op jit(solution)/shard_map/ppermute | solution.py:410
  28.3 26.5 %collective-permute-start.5 = (f32[2,464,256]{2,1,0:T(8,128)S(1)}, f32[2,464,256]{2,1,0:T(8,128)S(1)}, u32[]{:S(2)}, u32[]{:S(2)}) collective-permute-start(f32[2,464,256]{2,1,0:T(8,128)S(1)} %get-tuple-element.37.join_ref), channel_id=1, source_target_pairs={{0,1},{1,0},{2,3},{3,2},{4,5},{5,4},{6,7},{7,6},{8,9},{9,8},{10,11... | collective-permute-start | bytes 2850824 | tf_op jit(solution)/shard_map/ppermute | solution.py:410
  28.4 10.5 %collective-permute-start.2 = (f32[336,256]{1,0:T(8,128)S(1)}, f32[336,256]{1,0:T(8,128)S(1)}, u32[]{:S(2)}, u32[]{:S(2)}) collective-permute-start(f32[336,256]{1,0:T(8,128)S(1)} %get-tuple-element.33.refs_0_), channel_id=1, source_target_pairs={{0,4},{1,5},{2,6},{3,7},{4,0},{5,1},{6,2},{7,3},{8,12},{9,13},{10,... | collective-permute-start | bytes 1032200 | tf_op jit(solution)/shard_map/ppermute | solution.py:410
  38.9 9.5 %collective-permute-start.3 = (f32[336,256]{1,0:T(8,128)S(1)}, f32[336,256]{1,0:T(8,128)S(1)}, u32[]{:S(2)}, u32[]{:S(2)}) collective-permute-start(f32[336,256]{1,0:T(8,128)S(1)} %collective-permute-done.2.refs_1_), channel_id=1, source_target_pairs={{0,2},{1,3},{2,0},{3,1},{4,6},{5,7},{6,4},{7,5},{8,10},{9,11},{10,... | collective-permute-start | bytes 1032200 | tf_op jit(solution)/shard_map/ppermute | solution.py:410
  39.5 5.0 %collective-permute-start.4 = (f32[128,256]{1,0:T(8,128)S(1)}, f32[128,256]{1,0:T(8,128)S(1)}, u32[]{:S(2)}, u32[]{:S(2)}) collective-permute-start(f32[128,256]{1,0:T(8,128)S(1)} %collective-permute-done.1.refs_3_), channel_id=1, source_target_pairs={{0,4},{1,5},{2,6},{3,7},{4,0},{5,1},{6,2},{7,3},{8,12},{9,13},{10,... | collective-permute-start | bytes 393224 | tf_op jit(solution)/shard_map/ppermute | solution.py:410
  40.9 15.1 %collective-permute-start.7 = (f32[336,256]{1,0:T(8,128)S(1)}, f32[336,256]{1,0:T(8,128)S(1)}, u32[]{:S(2)}, u32[]{:S(2)}) collective-permute-start(f32[336,256]{1,0:T(8,128)S(1)} %collective-permute-done.2.refs_1_), channel_id=1, source_target_pairs={{0,1},{1,0},{2,3},{3,2},{4,5},{5,4},{6,7},{7,6},{8,9},{9,8},{10,11... | collective-permute-start | bytes 1032200 | tf_op jit(solution)/shard_map/ppermute | solution.py:410
  48.4 7.6 %collective-permute-start.9 = (f32[336,256]{1,0:T(8,128)S(1)}, f32[336,256]{1,0:T(8,128)S(1)}, u32[]{:S(2)}, u32[]{:S(2)}) collective-permute-start(f32[336,256]{1,0:T(8,128)S(1)} %collective-permute-done.3.refs_2_), channel_id=1, source_target_pairs={{0,1},{1,0},{2,3},{3,2},{4,5},{5,4},{6,7},{7,6},{8,9},{9,8},{10,11... | collective-permute-start | bytes 1032200 | tf_op jit(solution)/shard_map/ppermute | solution.py:410
  48.4 5.9 %collective-permute-start.6 = (f32[128,256]{1,0:T(8,128)S(1)}, f32[128,256]{1,0:T(8,128)S(1)}, u32[]{:S(2)}, u32[]{:S(2)}) collective-permute-start(f32[128,256]{1,0:T(8,128)S(1)} %get-tuple-element.34.refs_1_), channel_id=1, source_target_pairs={{0,4},{1,5},{2,6},{3,7},{4,0},{5,1},{6,2},{7,3},{8,12},{9,13},{10,... | collective-permute-start | bytes 393224 | tf_op jit(solution)/shard_map/ppermute | solution.py:410
  54.3 1.6 %collective-permute-start.8 = (f32[128,256]{1,0:T(8,128)S(1)}, f32[128,256]{1,0:T(8,128)S(1)}, u32[]{:S(2)}, u32[]{:S(2)}) collective-permute-start(f32[128,256]{1,0:T(8,128)S(1)} %collective-permute-done.6.refs_2_), channel_id=1, source_target_pairs={{0,1},{1,0},{2,3},{3,2},{4,5},{5,4},{6,7},{7,6},{8,9},{9,8},{10,11... | collective-permute-start | bytes 393224 | tf_op jit(solution)/shard_map/ppermute | solution.py:410
  54.3 1.6 %collective-permute-start.10 = (f32[128,256]{1,0:T(8,128)S(1)}, f32[128,256]{1,0:T(8,128)S(1)}, u32[]{:S(2)}, u32[]{:S(2)}) collective-permute-start(f32[128,256]{1,0:T(8,128)S(1)} %collective-permute-done.4.refs_3_), channel_id=1, source_target_pairs={{0,1},{1,0},{2,3},{3,2},{4,5},{5,4},{6,7},{7,6},{8,9},{9,8},{10,11... | collective-permute-start | bytes 393224 | tf_op jit(solution)/shard_map/ppermute | solution.py:410
  57.1 1.3 %collective-permute-start.11 = (f32[160,128]{1,0:T(8,128)S(1)}, f32[160,128]{1,0:T(8,128)S(1)}, u32[]{:S(2)}, u32[]{:S(2)}) collective-permute-start(f32[160,128]{1,0:T(8,128)S(1)} %get-tuple-element.50), channel_id=1, source_target_pairs={{0,1},{1,0},{2,3},{3,2},{4,5},{5,4},{6,7},{7,6},{8,9},{9,8},{10,11... | collective-permute-start | bytes 245768 | tf_op jit(solution)/shard_map/ppermute | solution.py:410
  58.4 4.6 %collective-permute-start.12 = (f32[160,128]{1,0:T(8,128)S(1)}, f32[160,128]{1,0:T(8,128)S(1)}, u32[]{:S(2)}, u32[]{:S(2)}) collective-permute-start(f32[160,128]{1,0:T(8,128)S(1)} %add.3.own_ref), channel_id=1, source_target_pairs={{0,2},{1,3},{2,0},{3,1},{4,6},{5,7},{6,4},{7,5},{8,10},{9,11},{10,... | collective-permute-start | bytes 245768 | tf_op jit(solution)/shard_map/ppermute | solution.py:410
  59.1 4.4 %collective-permute-start.13 = (f32[160,128]{1,0:T(8,128)S(1)}, f32[160,128]{1,0:T(8,128)S(1)}, u32[]{:S(2)}, u32[]{:S(2)}) collective-permute-start(f32[160,128]{1,0:T(8,128)S(1)} %add.3.own_ref), channel_id=1, source_target_pairs={{0,4},{1,5},{2,6},{3,7},{4,0},{5,1},{6,2},{7,3},{8,12},{9,13},{10,... | collective-permute-start | bytes 245768 | tf_op jit(solution)/shard_map/ppermute | solution.py:410
  60.5 5.6 %collective-permute-start.14 = (f32[160,128]{1,0:T(8,128)S(1)}, f32[160,128]{1,0:T(8,128)S(1)}, u32[]{:S(2)}, u32[]{:S(2)}) collective-permute-start(f32[160,128]{1,0:T(8,128)S(1)} %add.3.own_ref), channel_id=1, source_target_pairs={{0,6},{1,7},{2,4},{3,5},{4,2},{5,3},{6,0},{7,1},{8,14},{9,15},{10,... | collective-permute-start | bytes 245768 | tf_op jit(solution)/shard_map/ppermute | solution.py:410
  69.8 18.4 %all-to-all-start.1 = ((f32[16,30,2,128]{3,2,1,0:T(2,128)}), f32[16,30,2,128]{3,2,1,0:T(2,128)S(1)}, u32[]{:S(2)}, u32[]{:S(2)}) async-start(f32[16,30,2,128]{3,2,1,0:T(2,128)} %bitcast.7), calls=%async_computation.1 | async-start | bytes 983040 | tf_op jit(solution)/shard_map/all_to_all | solution.py:403
  74.5 0.9 %copy-start.2 = (f32[59392]{0:T(1024)S(1)}, f32[59392]{0:T(1024)}, u32[]{:S(2)}) copy-start(f32[59392]{0:T(1024)} %param.6) | copy-start | bytes 712708
  74.5 1.0 %copy-start.3 = (f32[59392]{0:T(1024)S(1)}, f32[59392]{0:T(1024)}, u32[]{:S(2)}) copy-start(f32[59392]{0:T(1024)} %param.7) | copy-start | bytes 712708
  74.5 1.2 %copy-start.4 = (f32[1,59392]{1,0:T(1,128)S(1)}, f32[1,59392]{1,0:T(1,128)}, u32[]{:S(2)}) copy-start(f32[1,59392]{1,0:T(1,128)} %param.8) | copy-start | bytes 712708
